TPU v7x, 128 devices: a whole 4x4x4 slice. The times are simulated.
128 devices in a mesh: dp: 8 (over x, z_hi), cls: 16 (over z_lo, y, core).
Axes of the slice: x: 4, y: 4, z: 4 (z_hi: 2, z_lo: 2; z = z_hi * 2 + z_lo), core: 2. Of those that a mesh axis runs over, the one named last changes fastest.
Arguments:
- sketches: bfloat16 [32768, 4096], P(('dp', 'cls')), may hold values from -6 to 6
- labels: int32 [32768], P(('dp', 'cls')), may hold values from 0 to 15, as said below
- places: int32 [32768], P(('dp', 'cls')), may hold values from 0 to 4095, as said below
- counts: int32 [16, 8, 128], P('cls'), may hold values from 0 to 4, as said below
- chosen: int32 [3, 16], P(None, 'cls'), may hold values from 0 to 4095, as said below
Outputs:
- gain_scores: float32 [3, 16, 4096], P(None, 'cls', 'dp')
- coverage: float32 [16, 4096], P('cls', 'dp')
Inputs may be any that keep to these rules, and one draw needn't show every extreme that they name: `labels`: every class has 8 or more examples. `places`: an example of device s (its index along dp and cls together) with class k has place m * 512 + s * 4 + j in class k's block: m is the member of dp that receives it, and for each k, m and s the j run over 0 to counts[k, m, s] - 1 without gaps, so no two examples share a place. In every draw one class and member receive 4 examples from every device. counts[k, m, s] is the number of examples of device s that take places of class k on member m. chosen[t, k] is a place of class k's block that holds an example; the 3 picks of a class differ.
All inputs are finite; a program needn't handle non-finite values.
Results may differ from a plain program's by a relative error of at most 0.0003.
Values may be sent and summed in bfloat16 or wider, within the bound.
No kernel may reach another device: no remote copies, remote signals or barrier semaphores. Data moves between devices by JAX's collectives and lax.ppermute only.
A program may use at most 128 MiB of HBM per device.

v0:
```python
import jax
import jax.numpy as jnp
from jax import lax
from jax.sharding import PartitionSpec as P


def in_blocks(value, dim, peers):
    dims = value.shape
    blocks = value.reshape(*dims[:dim], peers, dims[dim] // peers, *dims[dim + 1 :])
    return jnp.moveaxis(blocks, dim, 0)


def laid_out(blocks, dim):
    blocks = jnp.moveaxis(blocks, 0, dim)
    dims = blocks.shape
    return blocks.reshape(*dims[:dim], dims[dim] * dims[dim + 1], *dims[dim + 2 :])


def exchange_both(value, axis, axes, splits, concats):
    sizes = [lax.axis_size(a) for a in axes]
    blocks = in_blocks(value, splits[0], sizes[0])
    blocks = jnp.moveaxis(in_blocks(blocks, splits[1] + 1, sizes[1]), 0, 1)
    inside = blocks.shape[2:]
    blocks = blocks.reshape(-1, *inside)
    blocks = lax.all_to_all(blocks, axis, split_axis=0, concat_axis=0, tiled=True)
    blocks = laid_out(blocks.reshape(*sizes, *inside), concats[0] + 1)
    return laid_out(blocks, concats[1])


def from_everyone(value, axis):
    copies = jnp.broadcast_to(value, (lax.axis_size(axis), *value.shape))
    return lax.all_to_all(copies, axis, split_axis=0, concat_axis=0, tiled=True)


def over_copies(value, axis):
    return from_everyone(value, axis).max(axis=0)


def sum_at_owner(value, axis, dim):
    peers = lax.axis_size(axis)
    blocks = lax.all_to_all(in_blocks(value, dim, peers), axis, 0, 0, tiled=True)
    return jnp.sum(blocks, axis=0)


def squared_norms(matrix):
    wide = matrix.astype(jnp.float32)
    return jnp.sum(wide * wide, axis=1)


def distances(left, left_norms, right, right_norms, width):
    inner = lax.dot_general(
        left, right, (((1,), (1,)), ((), ())), preferred_element_type=jnp.float32
    )
    return (left_norms[:, None] + right_norms[None, :] - 2.0 * inner) / width


def coverage_chain(similar_picks):
    current = jnp.zeros((similar_picks.shape[0],), jnp.float32)
    before = []
    for turn_index in range(similar_picks.shape[1]):
        before.append(current)
        current = jnp.maximum(current, similar_picks[:, turn_index])
    return (jnp.stack(before, axis=1), current)


def column_gains(similar, row_weight, row_cover):
    return jnp.stack(
        [
            jnp.sum(
                row_weight[:, None] * jnp.maximum(similar - row_cover[:, turn_index][:, None], 0.0),
                axis=0,
            )
            for turn_index in range(row_cover.shape[1])
        ]
    )


def masked_largest(pair_block, row_weight, column_weight):
    return jnp.max(jnp.where(row_weight[:, None] * column_weight[None, :] > 0.0, pair_block, 0.0))


def body(sketches, labels, places, counts, chosen):
    row_count, width = sketches.shape
    members = lax.axis_size("dp")
    owners = lax.axis_size("cls")
    devices = members * owners
    per_source = 2 * row_count // devices
    capacity = devices * per_source
    member = lax.axis_index("dp")
    picked = chosen[:, 0]
    pick_count = picked.shape[0]
    target = (places // capacity * owners + labels) * per_source + places % per_source
    send_table = (
        lax.broadcasted_iota(jnp.int32, (2 * row_count, row_count), 0) == target[None, :]
    ).astype(jnp.bfloat16)
    outgoing = jnp.dot(send_table, sketches, preferred_element_type=jnp.float32).astype(
        jnp.bfloat16
    )
    arrived = exchange_both(
        outgoing.reshape(members, owners, per_source, width),
        ("dp", "cls"),
        ("dp", "cls"),
        (0, 1),
        (0, 1),
    )
    local_rows = arrived.reshape(capacity, width)
    class_counts = counts[0]
    valid_all = (
        (
            lax.broadcasted_iota(jnp.int32, (members, devices, per_source), 2)
            < class_counts[:, :, None]
        )
        .reshape(members, capacity)
        .astype(jnp.float32)
    )
    own_valid = lax.dynamic_index_in_dim(valid_all, member, 0, keepdims=False)
    total = jnp.sum(class_counts).astype(jnp.float32)
    local_norms = squared_norms(local_rows)
    block_rows = lax.all_gather(local_rows, "dp", axis=0, tiled=True)
    spread_all = distances(local_rows, local_norms, block_rows, squared_norms(block_rows), width)
    largest = masked_largest(spread_all, own_valid, valid_all.reshape(-1))
    bound = over_copies(largest, "dp")
    similar = bound - spread_all
    pick_columns = jnp.stack(
        [
            lax.dynamic_index_in_dim(similar, picked[turn_index], 1, keepdims=False)
            for turn_index in range(pick_count)
        ],
        axis=1,
    )
    cover_before, cover_final = coverage_chain(pick_columns)
    partial_value = column_gains(similar, own_valid, cover_before)
    summed = sum_at_owner(partial_value, "dp", 1)
    gain_scores = (summed * own_valid[None, :] / total)[:, None, :]
    coverage = (cover_final * own_valid)[None, :]
    return (gain_scores, coverage)


def solution(mesh):
    placed = (
        P(("dp", "cls"), None),
        P(("dp", "cls")),
        P(("dp", "cls")),
        P("cls", None, None),
        P(None, "cls"),
    )
    return jax.shard_map(
        body,
        mesh=mesh,
        in_specs=placed,
        out_specs=(P(None, "cls", "dp"), P("cls", "dp")),
        check_vma=False,
    )
```

profile of v0, /device:TPU:0, one launch (start us, length us, event | category | flops | bytes accessed | tf_op | source)
XLA Modules:
  0.0 505.1 jit_solution(2520177475090422252)
XLA Ops:
  7.2 0.0 copy-start
  7.2 0.0 all-gather.2.cloned.1.call-start
  7.2 0.8 fusion.3
  8.1 0.7 copy-done
  8.8 3.2 convolution_convert_fusion
  12.0 7.2 %reshape_transpose_transpose_reshape_reshape_reshape.3 = bf16[128,1,1,4,4096]{4,3,0,2,1:T(4,128)(2,1)} reshape(bf16[512,4096]{1,0:T(8,128)(2,1)} %convolution_convert_fusion) | data formatting | bytes 8388608 | tf_op jit(solution)/shard_map/reshape;transpose;transpose;reshape;reshape;reshape | solution.py:24
  19.2 64.3 %all_to_all.16 = bf16[128,1,1,4,4096]{4,3,2,1,0:T(4,128)(2,1)} all-to-all(bf16[128,1,1,4,4096]{4,3,2,1,0:T(4,128)(2,1)} %bitcast.30), channel_id=1, replica_groups=mesh['dp'=8,'cls'=16] {'dp','cls'}, dimensions={0} | all-to-all | bytes 8388608 | tf_op jit(solution)/shard_map/all_to_all | solution.py:25
  83.5 0.0 copy-start.6
  83.5 0.0 copy-start.5
  83.5 6.9 %reshape_reshape.3 = bf16[512,4096]{1,0:T(8,128)(2,1)} reshape(bf16[8,16,1,4,4096]{4,3,1,0,2:T(4,128)(2,1)} %bitcast.28) | data formatting | bytes 8388608 | tf_op jit(solution)/shard_map/reshape;reshape | solution.py:106
  90.5 0.0 all-gather.2.cloned.1.call-update
  90.5 0.0 copy-done.6
  90.5 0.6 fusion.4
  94.8 0.0 copy-done.5
  94.8 0.7 reduce_sum.72
  95.5 0.1 copy.31
  95.6 0.1 iota.25
  95.7 0.2 lt.42
  95.9 0.3 lt.46
  98.8 0.3 convert_reduce_fusion
  99.1 5.2 %multiply_reduce_fusion.4 = f32[8,16,4]{2,1,0:T(8,128)S(1)} fusion(bf16[8,16,1,4,4096]{4,3,1,0,2:T(4,128)(2,1)} %bitcast.29), kind=kLoop, calls=%fused_computation.6 | loop fusion | flops 6290944 | bytes 4196352 | tf_op jit(solution)/shard_map/reduce_sum | solution.py:47
  104.3 0.1 add.46
  104.4 322.6 %all-gather.2.cloned.1.call-done = bf16[4096,4096]{1,0:T(8,128)(2,1)} async-done(((bf16[512,4096]{1,0:T(8,128)(2,1)}), bf16[4096,4096]{1,0:T(8,128)(2,1)}) %all-gather.2.cloned.1.call-update) | async-done | bytes 33554448 | tf_op jit(solution)/shard_map/all_gather | solution.py:119
  426.9 0.0 copy-start.3
  426.9 11.5 %multiply_reduce_fusion = f32[4096]{0:T(1024)S(1)} fusion(bf16[4096,4096]{1,0:T(8,128)(2,1)} %all-gather.2.cloned.1.call-done), kind=kLoop, calls=%fused_computation | loop fusion | flops 50327552 | bytes 33570816 | tf_op jit(solution)/shard_map/reduce_sum | solution.py:47
  438.4 0.3 copy-done.3
  438.7 24.8 %select_reduce_fusion = (f32[]{:T(128)}, f32[512,4096]{1,0:T(8,128)}) fusion(f32[4096]{0:T(1024)S(1)} %compare_convert_fusion, f32[512]{0:T(512)S(1)} %get-tuple-element.17, bf16[512,4096]{1,0:T(8,128)(2,1)S(1)} %copy-done.3, bf16[4096,4096]{1,0:T(8,128)(2,1)} %all-gather.2.cloned.1.call-done, f32[4096]{0:T(1024)S(1)} %multiply_reduce_fusion, f32[512]{0:T(512)S(1)} %add.46), kind=kOutput, calls=%fused_computation.4 | convolution fusion | flops 17196646400 | bytes 46174212 | tf_op jit(solution)/shard_map/dot_general | solution.py:51
  463.5 0.6 broadcast_in_dim.5
  464.2 10.2 %all_to_all.17 = f32[8,1,1]{2,1,0:T(1,128)S(1)} all-to-all(f32[8,1,1]{2,1,0:T(1,128)S(1)} %broadcast_in_dim.5), channel_id=1, replica_groups=mesh['dp'=8,'cls'=16] {'dp'}, dimensions={0} | all-to-all | bytes 64 | tf_op jit(solution)/shard_map/all_to_all | solution.py:32
  474.4 0.6 reduce_max.19
  475.0 0.0 copy-start.2
  475.0 0.0 copy-start.1
  475.0 5.1 %broadcast_subtract_fusion = f32[512,4096]{1,0:T(8,128)S(1)} fusion(f32[512,4096]{1,0:T(8,128)} %get-tuple-element.23, f32[]{:T(128)} %reduce_max.19), kind=kLoop, calls=%fused_computation.9 | loop fusion | flops 2097152 | bytes 16777220 | tf_op jit(solution)/shard_map/sub | solution.py:123
  480.1 0.0 copy-start.4
  480.1 0.4 fusion.1
  480.5 0.3 copy-done.2
  480.8 5.1 %multiply_reduce_fusion.3 = (f32[4096]{0:T(1024)S(1)}, f32[4096]{0:T(1024)S(1)}, f32[4096]{0:T(1024)S(1)}) fusion(f32[512]{0:T(512)S(1)} %get-tuple-element.17, f32[512]{0:T(512)S(1)} %get-tuple-element.16, f32[512]{0:T(512)S(1)} %get-tuple-element.15, f32[512,4096]{1,0:T(8,128)S(1)} %copy-done.2, f32[]{:T(128)} %reduce_max.19), kind=kLoop, calls=%fused_computation.3 | loop fusion | flops 25153536 | bytes 8443908 | tf_op jit(solution)/shard_map/reduce_sum | solution.py:69
  485.9 0.0 copy-done.4
  485.9 0.7 maximum_bitcast_fusion
  486.5 3.3 all-to-all-start.2
  489.9 1.4 convert_multiply_fusion
  491.3 0.7 copy.29
  492.0 5.6 %all-to-all-done.2 = f32[8,3,512]{2,1,0:T(4,128)S(1)} async-done(((f32[8,3,512]{2,1,0:T(4,128)}), f32[8,3,512]{2,1,0:T(4,128)S(1)}, u32[]{:S(2)}, u32[]{:S(2)}) %all-to-all-start.2) | async-done | bytes 49184 | tf_op jit(solution)/shard_map/all_to_all | solution.py:41
  497.6 0.6 multiply_divide_fusion
  498.2 0.0 copy-done.1
  (6 shorter events, 0.1 us)
Async XLA Ops:
  7.2 1.6 copy-start
  7.2 419.7 %all-gather.2.cloned.1.call-start = ((), (), s32[]{:S(2)}) async-start(), calls=%async_computation.3 | async-start | bytes 37748736 | tf_op jit(solution)/shard_map/all_gather | solution.py:119
  83.5 7.0 %copy-start.6 = (s32[3,1]{0,1:T(1,128)S(1)}, s32[3,1]{0,1:T(1,128)}, u32[]{:S(2)}) copy-start(s32[3,1]{0,1:T(1,128)} %param.9) | copy-start | bytes 40
  83.5 11.3 %copy-start.5 = (s32[1,8,128]{2,1,0:T(8,128)S(1)}, s32[1,8,128]{2,1,0:T(8,128)}, u32[]{:S(2)}) copy-start(s32[1,8,128]{2,1,0:T(8,128)} %param.8) | copy-start | bytes 12292
  426.9 11.8 %copy-start.3 = (bf16[512,4096]{1,0:T(8,128)(2,1)S(1)}, bf16[512,4096]{1,0:T(8,128)(2,1)}, u32[]{:S(2)}) copy-start(bf16[512,4096]{1,0:T(8,128)(2,1)} %reshape_reshape.3) | copy-start | bytes 12582916
  475.0 5.8 %copy-start.2 = (f32[512,4096]{1,0:T(8,128)S(1)}, f32[512,4096]{1,0:T(8,128)}, u32[]{:S(2)}) copy-start(f32[512,4096]{1,0:T(8,128)} %get-tuple-element.23) | copy-start | bytes 25165828
  475.0 23.2 %copy-start.1 = (bf16[256,4096]{1,0:T(8,128)(2,1)S(1)}, bf16[256,4096]{1,0:T(8,128)(2,1)}, u32[]{:S(2)}) copy-start(bf16[256,4096]{1,0:T(8,128)(2,1)} %param.5) | copy-start | bytes 6291460
  480.1 5.7 %copy-start.4 = (f32[512,4096]{1,0:T(8,128)}, f32[512,4096]{1,0:T(8,128)S(1)}, u32[]{:S(2)}) copy-start(f32[512,4096]{1,0:T(8,128)S(1)} %broadcast_subtract_fusion) | copy-start | bytes 25165828
  486.5 11.0 %all-to-all-start.2 = ((f32[8,3,512]{2,1,0:T(4,128)}), f32[8,3,512]{2,1,0:T(4,128)S(1)}, u32[]{:S(2)}, u32[]{:S(2)}) async-start(f32[8,3,512]{2,1,0:T(4,128)} %maximum_bitcast_fusion), calls=%async_computation.2 | async-start | bytes 131072 | tf_op jit(solution)/shard_map/all_to_all | solution.py:41
Sparse Core Ops, SparseCore 0:
  90.6 336.2 all-gather.1
where the time goes:
time: 506 us; the launch traced here: 505 us
  waiting for transfers between devices  328 us (65%)
  blocking collectives  74.5 us (15%)
  other arithmetic  32.3 us (6%)
  matrix products  28 us (6%)
  between operations  20.4 us (4%)
  local copies, waits for them, and re-layouts  18.2 us (4%)
    all_gather x1, waiting for transfers between devices, body(): block_rows = lax.all_gather(local_rows, 'dp', axis=0, tiled=True)  323 us
    all_to_all x1, blocking collectives, exchange_both(): lax.all_to_all(blocks, axis, split_axis=0, concat_axis=0, tiled=True)  64.3 us
    dot_general x1, matrix products, distances(): lax.dot_general(left, right, (((1,), (1,)), ((), ())), preferred_element_...  24.8 us
    reduce_sum x2, other arithmetic, squared_norms(): return jnp.sum(wide * wide, axis=1)  16.6 us
    all_to_all x1, blocking collectives, from_everyone(): return lax.all_to_all(copies, axis, split_axis=0, concat_axis=0, tiled=True)  10.2 us
  transfers between devices with their start and end apart: 2, of which 2 were waited for; matrix products, arithmetic and copies ran while one was open for 2% of the time, Pallas kernels for 0%

commit v1 on v0

v1 whole, which is shorter than its diff:
```python
import jax
import jax.numpy as jnp
from jax import lax
from jax.sharding import PartitionSpec as P

AX = ("dp", "cls")
F32 = jnp.float32
BF16 = jnp.bfloat16
BIG = 1e30
CHUNKS = (5, 5, 4, 2)


def dix(x, y, z, c):
    return x * 32 + (z // 2) * 16 + (z % 2) * 8 + y * 2 + c


def xyz(d):
    return d // 32, (d // 2) % 4, ((d // 16) % 2) * 2 + (d // 8) % 2, d % 2


DEV = range(128)
MATE = ((1, 0, 3, 2), (3, 2, 1, 0))
PAIRS = (((0, 1), (2, 3)), ((2, 1), (0, 3)))


def mate(d):
    x, y, z, c = xyz(d)
    return dix(x, MATE[c][y], z, c)


def along(d, k):
    x, y, z, c = xyz(d)
    return dix((x + k) % 4, y, z, c) if c == 0 else dix(x, y, (z + k) % 4, c)


def side(d):
    return xyz(d)[1] % 2


SWAP = [(d, d ^ 1) for d in DEV]
UP = [(d, along(d, 1)) for d in DEV]
DOWN = [(d, along(d, -1)) for d in DEV]
ACROSS = [(d, mate(d)) for d in DEV]
FOURTH = [(d, mate(d) if side(d) == 1 else mate(along(d, 1))) for d in DEV]


def regroup_groups():
    groups = []
    for x in range(4):
        for ys in ((0, 3), (1, 2)):
            groups.append([dix(x, y, z, 0) for y in ys for z in range(4)])
    for z in range(4):
        for ys in ((1, 0), (2, 3)):
            groups.append([dix(x, y, z, 1) for y in ys for x in range(4)])
    return groups


def class_groups():
    groups = []
    for c in (0, 1):
        for pair in PAIRS[c]:
            for u in range(4):
                group = [dix(t, y, u, 0) if c == 0 else dix(u, y, t, 1) for t in range(4) for y in pair]
                groups.append(group)
    return groups


def final_groups():
    groups = []
    for c in (0, 1):
        for pair in PAIRS[c]:
            groups.append([dix(x, y, z, c) for x in range(4) for z in range(4) for y in pair])
    return groups


def info_pairs():
    out = []
    for d in DEV:
        x, y, z, c = xyz(d)
        zh, zl = z // 2, z % 2
        if c == 0:
            src = dix(x, (y // 2) * 2 + zh, (y % 2) * 2 + zl, 0)
        else:
            yk = y if y % 2 == x % 2 else MATE[1][y]
            src = dix(zh * 2 + zl, yk, (y % 2) * 2 + x // 2, 1)
        out.append((src, d))
    return out


INFO = info_pairs()


def send(value, pairs):
    return lax.ppermute(value, AX, pairs)


def iota(shape, dim):
    return lax.broadcasted_iota(jnp.int32, shape, dim)


def inner(left, right):
    return lax.dot_general(left, right, (((1,), (1,)), ((), ())), preferred_element_type=F32)


def exact(left, right):
    return jnp.dot(left, right, precision=lax.Precision.HIGHEST, preferred_element_type=F32)


def reach(pair, rows, columns):
    out = [jnp.sum(pair, axis=0)]
    for t in (2, 3):
        out.append(jnp.sum(jnp.maximum(pair + rows[t][:, None] - columns[0][None, :], 0.0), axis=0))
    return jnp.stack(out)


def furthest(pair, rows, columns):
    return jnp.max(rows[1][:, None] + columns[1][None, :] - pair)


def source_of(place_in_line, x, z, y, core, row):
    group, sub, member, slot = row // 64, row // 32 % 2, row // 4 % 8, row % 4
    i, w = group // 4, group % 4
    outer = (y == 0) | (y == 3)
    low = y < 2
    y0 = jnp.where(outer, 3 * i, 1 + i)
    y1 = jnp.where(low, 1 - i, 2 + i)
    sx = jnp.where(core == 0, x, w)
    sz = jnp.where(core == 0, w, z)
    sy = jnp.where(core == 0, y0, y1)
    return dix(sx, sy, sz, jnp.where(sub == 0, 0, 1)), member, slot


def body(sketches, labels, places, counts, chosen):
    rows_dev, width = sketches.shape
    dp, cls = lax.axis_index("dp"), lax.axis_index("cls")
    x, zh, zl, y, core = dp // 2, dp % 2, cls // 8, cls // 2 % 4, cls % 2
    z = zh * 2 + zl
    edge = y % 2
    first = core == 0

    packed = jnp.concatenate([counts[0], jnp.broadcast_to(chosen, (3, 128))], axis=0)
    packed = send(packed, INFO)
    host_counts = packed[:8].astype(F32)
    picks = packed[8:11, 0]

    k_core, k_y, k_zl = labels % 2, labels // 2 % 4, labels // 8
    group = jnp.where(
        k_core == 0,
        (k_y // 2) * 4 + (k_y % 2) * 2 + k_zl,
        ((k_y + 3) % 4 // 2) * 4 + k_zl * 2 + k_y % 2,
    )
    spot = group * 64 + core * 32 + places // 512 * 4 + places % 4
    mine = jnp.where(k_core == core, spot, -1)
    theirs = jnp.where(k_core == core, -1, spot)
    from_twin = send(sketches, SWAP)
    twin_spot = send(theirs, SWAP)
    slots = iota((2 * rows_dev, rows_dev), 0)
    table_own = (slots == mine[None, :]).astype(BF16)
    table_twin = (slots == twin_spot[None, :]).astype(BF16)
    outgoing = (
        jnp.dot(table_own, sketches, preferred_element_type=F32)
        + jnp.dot(table_twin, from_twin, preferred_element_type=F32)
    ).astype(BF16)
    own = lax.all_to_all(
        outgoing.reshape(8, 64, width), AX, 0, 0, axis_index_groups=regroup_groups(), tiled=True
    ).reshape(512, width)

    edges = [0]
    for size in CHUNKS:
        edges.append(edges[-1] + width // sum(CHUNKS) * size)
    o, l, r, f = [], [], [], []
    for lo, hi in zip(edges, edges[1:]):
        part = own[:, lo:hi]
        o.append(part)
        l.append(send(part, UP))
        r.append(send(part, DOWN))
        f.append(send(jnp.where(edge == 0, l[-1], part), ACROSS))

    src, member, slot = source_of(None, x, z, y, core, iota((1, 512), 1))
    place = member * 512 + src * 4 + slot
    seen = jnp.sum(
        jnp.where(iota((128, 512), 0) == src, exact(host_counts.T, (iota((8, 512), 0) == member).astype(F32)), 0.0),
        axis=0,
    )
    valid = slot[0].astype(F32) < seen
    n_valid = jnp.sum(host_counts)
    hit = (place == jnp.concatenate([picks, -jnp.ones((5,), jnp.int32)])[:, None]).astype(BF16)
    found = jnp.dot(hit, own, preferred_element_type=F32).astype(BF16)
    found = lax.all_gather(found, AX, axis_index_groups=class_groups())
    found = jnp.sum(found.astype(F32), axis=0).astype(BF16)
    to_picks = inner(found, own)
    pick_half = 0.5 * jnp.sum(jnp.square(found.astype(F32)), axis=1)
    half = 0.5 * jnp.sum(jnp.square(own.astype(F32)), axis=1)
    near = pick_half[:3, None] - to_picks[:3]
    near1 = near[0]
    near2 = jnp.minimum(near[0], near[1])
    near3 = jnp.minimum(near2, near[2])
    info = jnp.stack(
        [half, jnp.where(valid, half, -BIG), jnp.where(valid, near1, -BIG), jnp.where(valid, near2, -BIG)]
    )
    info_l = send(info, UP)
    info_r = send(info, DOWN)
    info_f = send(info, FOURTH)

    def product(a, b):
        total = inner(a[0], b[0])
        for u, v in zip(a[1:], b[1:]):
            total = total + inner(u, v)
        return total

    oo, ol, lr, fr, fo = product(o, o), product(o, l), product(l, r), product(f, r), product(f, o)
    to_o = reach(oo, info, info) + reach(ol.T, info_l, info) + reach(fo, info_f, info)
    to_l = reach(ol, info, info_l)
    to_r = reach(lr, info_l, info_r) + reach(fr, info_f, info_r)
    to_f = reach(fr.T, info_r, info_f) + reach(fo.T, info, info_f)
    bound = jnp.maximum(
        jnp.max(
            jnp.stack(
                [
                    furthest(oo, info, info),
                    furthest(ol, info, info_l),
                    furthest(lr, info_l, info_r),
                    furthest(fr, info_f, info_r),
                    furthest(fo, info_f, info),
                ]
            )
        ),
        0.0,
    )
    to_o = to_o.at[0].add(-n_valid * half)
    extra = jnp.stack(
        [half + near3, jnp.broadcast_to(bound, (512,)), jnp.broadcast_to(jnp.sum(half), (512,)), jnp.zeros((512,), F32)]
    )
    given = jnp.concatenate([jnp.stack([to_o, to_l, to_r, to_f]), extra[:, None, :]], axis=1)

    lane = iota((512, 512), 0)
    to_lane = (lane // 4 % 8) * 64 + (lane // 32) * 4 + lane % 4
    by_member = (to_lane == iota((512, 512), 1)).astype(F32)
    given = exact(given.reshape(16, 512), by_member)
    given = given.reshape(16, 8, 64).transpose(1, 0, 2)
    zl_p, edge_p = iota((4, 1, 1), 0) // 2, iota((4, 1, 1), 0) % 2
    wanted = jnp.where(first, edge_p * 2 + zl_p == z, zl_p * 2 + edge_p == x)
    outbox = jnp.where(wanted[None], given[:, None], 0.0).reshape(32, 16, 64)
    inbox = lax.all_to_all(outbox, AX, 0, 0, axis_index_groups=final_groups(), tiled=True)
    inbox = inbox.reshape(4, 4, 2, 4, 4, 64)
    inbox = jnp.where(first, jnp.sum(inbox, axis=1), jnp.sum(inbox, axis=0))
    o_part, l_part, r_part, f_part = (inbox[:, :, b] for b in range(4))
    total3 = o_part[:, :, :3] + jnp.roll(l_part[:, :, :3], -1, axis=0) + jnp.roll(r_part[:, :, :3], 1, axis=0)
    f_home = jnp.stack([jnp.roll(f_part[:, 1, :3], -1, axis=0), f_part[:, 0, :3]], axis=1)
    total3 = total3 + f_home
    merged = jnp.concatenate([total3, o_part[:, :, 3:4]], axis=2)
    far = 2.0 * jnp.max(l_part[:, :, 3])
    half_sum = jnp.sum(r_part[:, :, 3, 0])
    flat = merged.transpose(2, 0, 1, 3).reshape(4, 512)

    lane1 = iota((512, 1), 0)
    line, sd, rest = lane1 // 128, lane1 // 64 % 2, lane1 % 64
    pair_y0 = y // 2 * 2 + sd
    pair_low = (y == 1) | (y == 2)
    pair_y1 = jnp.where(pair_low, 2 - sd, 3 * sd)
    pair_y = jnp.where(first, pair_y0, pair_y1)
    src2, _, slot2 = source_of(None, line, line, pair_y, core, (rest // 4) * 32 + rest % 4)
    order = (src2 * 4 + slot2 == iota((512, 512), 1)).astype(F32)
    final = exact(flat, order)

    class_counts = counts[0]
    own_counts = lax.dynamic_index_in_dim(class_counts, dp, 0, keepdims=False)
    keep = (iota((128, 4), 1) < own_counts[:, None]).reshape(512).astype(F32)
    total = jnp.sum(class_counts).astype(F32)
    gain0 = (2.0 * final[0] + total * far - 2.0 * half_sum) / width
    gains = jnp.stack([gain0, 2.0 * final[1] / width, 2.0 * final[2] / width])
    gain_scores = (gains * keep[None, :] / total)[:, None, :]
    coverage = (keep * (far - 2.0 * final[3]) / width)[None, :]
    return (gain_scores, coverage)


def solution(mesh):
    placed = (
        P(("dp", "cls"), None),
        P(("dp", "cls")),
        P(("dp", "cls")),
        P("cls", None, None),
        P(None, "cls"),
    )
    return jax.shard_map(
        body,
        mesh=mesh,
        in_specs=placed,
        out_specs=(P(None, "cls", "dp"), P("cls", "dp")),
        check_vma=False,
    )
```

time: 506 us -> 214 us (0.42)
  waiting for transfers between devices: 328 us -> 53.1 us
  blocking collectives: 74.5 us -> 28.8 us
  starting transfers between devices: 3.39 us -> 46.1 us
  matrix products: 28 us -> 52.4 us
  other arithmetic: 32.3 us -> 16.3 us
  between operations: 20.4 us -> 7.11 us
  local copies, waits for them, and re-layouts: 18.2 us -> 8.75 us
    all_gather x1 -> x0, waiting for transfers between devices: 323 us -> none  [body(): block_rows = lax.all_gather(local_rows, 'dp', axis=0, tiled=True)]
    all_to_all x2 -> x0, blocking collectives: 74.5 us -> none  [the longest x1 64.3 us: exchange_both(): lax.all_to_all(blocks, axis, split_axis=0, concat_axis=0, tiled=True)]
    ppermute x0 -> x18, starting transfers between devices: none -> 32 us  [send(): return lax.ppermute(value, AX, pairs)]
    all_gather x0 -> x1, blocking collectives: none -> 28.8 us  [body(): found = lax.all_gather(found, AX, axis_index_groups=class_groups())]
    all_to_all x1 -> x2, waiting for transfers between devices: 5.59 us -> 31.6 us  [the longest x1 24.8 us: body(): lax.all_to_all(outgoing.reshape(8, 64, width), AX, 0, 0, axis_index_group...]
    dot_general x2 -> x27, matrix products: 28 us -> 52.4 us  [the longest x21 41.7 us: inner(): lax.dot_general(left, right, (((1,), (1,)), ((), ())), preferred_element_...]
    ppermute x0 -> x18, waiting for transfers between devices: none -> 21.6 us  [send(): return lax.ppermute(value, AX, pairs)]
    reduce_sum x5 -> x7, other arithmetic: 22.4 us -> 5.23 us  [the longest x1 3.08 us: body(): half = 0.5 * jnp.sum(jnp.square(own.astype(F32)), axis=1)]
  transfers between devices with their start and end apart: 2 -> 20, of which waited for: 2 -> 9; matrix products, arithmetic and copies ran while one was open for 2% -> 27% of each run, Pallas kernels for 0% -> 0%
where the time goes in v1:
time: 214 us; the launch traced here: 213 us
  waiting for transfers between devices  53.1 us (25%)
  matrix products  52.4 us (24%)
  starting transfers between devices  46.1 us (22%)
  blocking collectives  28.8 us (13%)
  other arithmetic  16.3 us (8%)
  local copies, waits for them, and re-layouts  8.75 us (4%)
  between operations  7.11 us (3%)
    dot_general x21, matrix products, inner(): lax.dot_general(left, right, (((1,), (1,)), ((), ())), preferred_element_...  41.7 us
    ppermute x18, starting transfers between devices, send(): return lax.ppermute(value, AX, pairs)  32 us
    all_gather x1, blocking collectives, body(): found = lax.all_gather(found, AX, axis_index_groups=class_groups())  28.8 us
    all_to_all x1, waiting for transfers between devices, body(): lax.all_to_all(outgoing.reshape(8, 64, width), AX, 0, 0, axis_index_group...  24.8 us
    ppermute x18, waiting for transfers between devices, send(): return lax.ppermute(value, AX, pairs)  21.6 us
    all_to_all x1, starting transfers between devices, body(): lax.all_to_all(outgoing.reshape(8, 64, width), AX, 0, 0, axis_index_group...  8.01 us
    all_to_all x1, waiting for transfers between devices, body(): lax.all_to_all(outbox, AX, 0, 0, axis_index_groups=final_groups(), tiled=...  6.79 us
    select_n x4, other arithmetic, body(): f.append(send(jnp.where(edge == 0, l[-1], part), ACROSS))  6.3 us
  transfers between devices with their start and end apart: 20, of which 9 were waited for; matrix products, arithmetic and copies ran while one was open for 27% of the time, Pallas kernels for 0%

profile of v1, /device:TPU:0, one launch (start us, length us, event | category | flops | bytes accessed | tf_op | source)
XLA Modules:
  0.0 212.6 jit_solution(14835696430719475510)
XLA Ops:
  0.7 0.7 broadcast_select_fusion.11
  2.0 2.8 %fusion.29 = f32[512,4096]{1,0:T(8,128)S(1)} fusion(bf16[256,4096]{1,0:T(8,128)(2,1)} %param.7, s32[256]{0:T(256)S(1)} %broadcast_select_fusion.10), kind=kOutput, calls=%fused_computation.74 | convolution fusion | flops 1073872896 | bytes 10486784 | tf_op jit(solution)/shard_map/dot_general | solution.py:161
  5.1 3.4 %add_convert_fusion = bf16[512,4096]{1,0:T(8,128)(2,1)} fusion(f32[512,4096]{1,0:T(8,128)S(1)} %fusion.29, bf16[256,4096]{1,0:T(8,128)(2,1)S(1)} %collective-permute-done.1, s32[256]{0:T(256)S(1)} %collective-permute-done), kind=kOutput, calls=%fused_computation.1 | convolution fusion | flops 1078067200 | bytes 14681088 | tf_op jit(solution)/shard_map/dot_general | solution.py:162
  8.4 8.0 %all-to-all-start = ((bf16[8,64,4096]{2,1,0:T(8,128)(2,1)}), bf16[8,64,4096]{2,1,0:T(8,128)(2,1)}, u32[]{:S(2)}, u32[]{:S(2)}) async-start(bf16[8,64,4096]{2,1,0:T(8,128)(2,1)} %bitcast.133), calls=%async_computation | async-start | bytes 8388608 | tf_op jit(solution)/shard_map/all_to_all | solution.py:164
  16.6 0.7 collective-permute-start.2
  17.7 0.6 fusion.48
  19.3 24.8 %all-to-all-done = bf16[8,64,4096]{2,1,0:T(8,128)(2,1)} async-done(((bf16[8,64,4096]{2,1,0:T(8,128)(2,1)}), bf16[8,64,4096]{2,1,0:T(8,128)(2,1)}, u32[]{:S(2)}, u32[]{:S(2)}) %all-to-all-start) | async-done | bytes 4194336 | tf_op jit(solution)/shard_map/all_to_all | solution.py:164
  44.1 1.4 slice.226
  45.5 2.3 %slice.228 = bf16[512,1024]{1,0:T(8,128)(2,1)} slice(bf16[512,4096]{1,0:T(8,128)(2,1)} %bitcast.1), slice={[0:512], [2560:3584]} | slice | bytes 2097152 | tf_op jit(solution)/shard_map/slice | solution.py:173
  47.8 1.9 slice.229
  49.6 1.8 collective-permute-start.5
  51.4 1.4 collective-permute-start.15
  53.4 2.7 %collective-permute-start.16 = (bf16[512,512]{1,0:T(8,128)(2,1)}, bf16[512,512]{1,0:T(8,128)(2,1)S(1)}, u32[]{:S(2)}, u32[]{:S(2)}) collective-permute-start(bf16[512,512]{1,0:T(8,128)(2,1)} %slice.229), channel_id=1, source_target_pairs={{0,96},{1,25},{2,98},{3,27},{4,100},{5,29},{6,102},{7,31},{8,104},... | collective-permute-start | bytes 1572872 | tf_op jit(solution)/shard_map/ppermute | solution.py:94
  56.1 3.1 %multiply_reduce_fusion = f32[8,64]{1,0:T(8,128)S(1)} fusion(bf16[8,64,4096]{2,1,0:T(8,128)(2,1)} %all-to-all-done), kind=kLoop, calls=%fused_computation | loop fusion | flops 6290944 | bytes 4196352 | tf_op jit(solution)/shard_map/reduce_sum | solution.py:193
  59.9 2.8 %fusion.148 = f32[512,512]{1,0:T(8,128)S(1)} fusion(bf16[512,4096]{1,0:T(8,128)(2,1)} %bitcast.1), kind=kOutput, calls=%fused_computation.349 | convolution fusion | flops 671088640 | bytes 2359296 | tf_op jit(solution)/shard_map/dot_general | solution.py:102
  62.7 2.9 %convolution_convert_fusion = bf16[8,4096]{1,0:T(8,128)(2,1)S(1)} fusion(bf16[512,4096]{1,0:T(8,128)(2,1)} %bitcast.1, s32[512]{0:T(512)S(1)} %get-tuple-element.65, s32[8]{0:T(128)S(1)} %concatenate.83), kind=kOutput, calls=%fused_computation.2 | convolution fusion | flops 33591296 | bytes 4261920 | tf_op jit(solution)/shard_map/dot_general | solution.py:188
  65.6 28.8 %all-gather = bf16[64,4096]{1,0:T(8,128)(2,1)S(1)} all-gather(bf16[8,4096]{1,0:T(8,128)(2,1)S(1)} %convolution_convert_fusion), channel_id=2, replica_groups={{0,2,32,34,64,66,96,98},{8,10,40,42,72,74,104,106},{16,18,48,50,80,82,1..., dimensions={0}, use_global_device_ids=true | all-gather | bytes 589824 | tf_op jit(solution)/shard_map/all_gather | solution.py:189
  94.6 3.4 %convolution_subtract_fusion = f32[3,512]{1,0:T(4,128)S(1)} fusion(bf16[512,4096]{1,0:T(8,128)(2,1)} %bitcast.1, bf16[8,4096]{1,0:T(8,128)(2,1)S(1)} %bitcast_reduce_fusion, f32[3]{0:T(128)S(1)} %bitcast.190), kind=kOutput, calls=%fused_computation.28 | convolution fusion | flops 12584448 | bytes 4233728 | tf_op jit(solution)/shard_map/dot_general | solution.py:102
  98.2 2.8 %convolution_add_fusion.6 = f32[512,512]{1,0:T(8,128)S(1)} fusion(f32[512,512]{1,0:T(8,128)S(1)} %fusion.148, bf16[512,4096]{1,0:T(8,128)(2,1)} %bitcast.1), kind=kOutput, calls=%fused_computation.18 | convolution fusion | flops 671350784 | bytes 3407872 | tf_op jit(solution)/shard_map/dot_general | solution.py:102
  101.0 2.3 %convolution_add_fusion.1 = f32[512,512]{1,0:T(8,128)S(1)} fusion(f32[512,512]{1,0:T(8,128)S(1)} %convolution_add_fusion.6, bf16[512,4096]{1,0:T(8,128)(2,1)} %bitcast.1), kind=kOutput, calls=%fused_computation.9 | convolution fusion | flops 537133056 | bytes 3145728 | tf_op jit(solution)/shard_map/dot_general | solution.py:102
  103.3 1.8 convolution_add_fusion
  105.2 0.7 pad.23.clone
  105.9 3.2 %collective-permute-start.17 = (f32[4,512]{1,0:T(4,128)S(1)}, f32[4,512]{1,0:T(4,128)S(1)}, u32[]{:S(2)}, u32[]{:S(2)}) collective-permute-start(f32[4,512]{1,0:T(4,128)S(1)} %pad_maximum_fusion.1), channel_id=1, source_target_pairs={{0,96},{1,25},{2,98},{3,27},{4,100},{5,29},{6,102},{7,31},{8,104},... | collective-permute-start | bytes 24584 | tf_op jit(solution)/shard_map/ppermute | solution.py:94
  109.2 1.4 collective-permute-done.17
  110.5 2.4 %collective-permute-start.12 = (f32[4,512]{1,0:T(4,128)S(1)}, f32[4,512]{1,0:T(4,128)S(1)}, u32[]{:S(2)}, u32[]{:S(2)}) collective-permute-start(f32[4,512]{1,0:T(4,128)S(1)} %pad_maximum_fusion.1), channel_id=1, source_target_pairs={{0,34},{1,15},{2,0},{3,5},{4,38},{5,11},{6,4},{7,1},{8,42},{9,23},... | collective-permute-start | bytes 24584 | tf_op jit(solution)/shard_map/ppermute | solution.py:94
  113.0 1.4 collective-permute-done.12
  114.3 2.0 collective-permute-start.3
  116.4 1.4 collective-permute-start.13
  117.8 1.1 broadcast_select_fusion.3
  118.9 1.5 fusion.133
  120.4 3.8 %collective-permute-start.11 = (bf16[512,512]{1,0:T(8,128)(2,1)S(1)}, bf16[512,512]{1,0:T(8,128)(2,1)S(1)}, u32[]{:S(2)}, u32[]{:S(2)}) collective-permute-start(bf16[512,512]{1,0:T(8,128)(2,1)S(1)} %broadcast_select_fusion.3), channel_id=1, source_target_pairs={{0,2},{1,7},{2,0},{3,5},{4,6},{5,3},{6,4},{7,1},{8,10},{9,15},{10,... | collective-permute-start | bytes 1572872 | tf_op jit(solution)/shard_map/ppermute | solution.py:94
  124.7 1.7 broadcast_select_fusion.2
  126.4 4.9 %collective-permute-done.11 = bf16[512,512]{1,0:T(8,128)(2,1)S(1)} collective-permute-done((bf16[512,512]{1,0:T(8,128)(2,1)S(1)}, bf16[512,512]{1,0:T(8,128)(2,1)S(1)}, u32[]{:S(2)}, u32[]{:S(2)}) %collective-permute-start.11) | collective-permute-done | bytes 524320 | tf_op jit(solution)/shard_map/ppermute | solution.py:94
  131.8 1.4 collective-permute-done.3
  133.3 2.1 broadcast_select_fusion.1
  135.3 0.8 collective-permute-start.4
  136.1 1.5 fusion.131
  137.6 2.3 %fusion.138 = f32[512,512]{1,0:T(8,128)S(1)} fusion(bf16[512,1024]{1,0:T(8,128)(2,1)} %collective-permute-done.5, bf16[512,4096]{1,0:T(8,128)(2,1)} %bitcast.1), kind=kOutput, calls=%fused_computation.339 | convolution fusion | flops 536870912 | bytes 3145728 | tf_op jit(solution)/shard_map/dot_general | solution.py:102
  139.9 2.3 %fusion.163 = f32[512,512]{1,0:T(8,128)S(1)} fusion(bf16[512,1024]{1,0:T(8,128)(2,1)} %collective-permute-done.5, bf16[512,1024]{1,0:T(8,128)(2,1)} %collective-permute-done.15), kind=kOutput, calls=%fused_computation.361 | convolution fusion | flops 536870912 | bytes 3145728 | tf_op jit(solution)/shard_map/dot_general | solution.py:102
  142.2 2.6 %collective-permute-start.14 = (bf16[512,1280]{1,0:T(8,128)(2,1)S(1)}, bf16[512,1280]{1,0:T(8,128)(2,1)S(1)}, u32[]{:S(2)}, u32[]{:S(2)}) collective-permute-start(bf16[512,1280]{1,0:T(8,128)(2,1)S(1)} %get-tuple-element.71), channel_id=1, source_target_pairs={{0,96},{1,25},{2,98},{3,27},{4,100},{5,29},{6,102},{7,31},{8,104},... | collective-permute-start | bytes 3932168 | tf_op jit(solution)/shard_map/ppermute | solution.py:94
  144.8 3.7 %collective-permute-start.8 = (bf16[512,1280]{1,0:T(8,128)(2,1)S(1)}, bf16[512,1280]{1,0:T(8,128)(2,1)S(1)}, u32[]{:S(2)}, u32[]{:S(2)}) collective-permute-start(bf16[512,1280]{1,0:T(8,128)(2,1)S(1)} %get-tuple-element.70), channel_id=1, source_target_pairs={{0,2},{1,7},{2,0},{3,5},{4,6},{5,3},{6,4},{7,1},{8,10},{9,15},{10,... | collective-permute-start | bytes 3932168 | tf_op jit(solution)/shard_map/ppermute | solution.py:94
  148.5 2.0 fusion.166
  150.6 2.0 fusion.136
  152.6 1.6 collective-permute-done.4
  154.2 1.5 broadcast_select_fusion
  155.7 4.0 %collective-permute-start.9 = (bf16[512,1280]{1,0:T(8,128)(2,1)S(1)}, bf16[512,1280]{1,0:T(8,128)(2,1)S(1)}, u32[]{:S(2)}, u32[]{:S(2)}) collective-permute-start(bf16[512,1280]{1,0:T(8,128)(2,1)S(1)} %broadcast_select_fusion), channel_id=1, source_target_pairs={{0,2},{1,7},{2,0},{3,5},{4,6},{5,3},{6,4},{7,1},{8,10},{9,15},{10,... | collective-permute-start | bytes 3932168 | tf_op jit(solution)/shard_map/ppermute | solution.py:94
  159.7 2.2 %fusion.143 = f32[512,512]{1,0:T(8,128)S(1)} fusion(bf16[512,1280]{1,0:T(8,128)(2,1)S(1)} %collective-permute-done.4, bf16[512,4096]{1,0:T(8,128)(2,1)} %bitcast.1), kind=kOutput, calls=%fused_computation.344 | convolution fusion | flops 671088640 | bytes 3670016 | tf_op jit(solution)/shard_map/dot_general | solution.py:102
  161.9 0.9 fusion.162
  162.8 2.3 %fusion.4 = f32[512,512]{1,0:T(8,128)S(1)} fusion(f32[512,512]{1,0:T(8,128)S(1)} %fusion.133, f32[512,512]{1,0:T(8,128)S(1)} %fusion.138, f32[512,512]{1,0:T(8,128)S(1)} %fusion.143, bf16[512,1280]{1,0:T(8,128)(2,1)S(1)} %collective-permute-done.3, bf16[512,4096]{1,0:T(8,128)(2,1)} %bitcast.1), kind=kOutput, calls=%fused_computation.21 | convolution fusion | flops 671875072 | bytes 6815744 | tf_op jit(solution)/shard_map/dot_general | solution.py:102
  165.1 2.4 %fusion.154 = (f32[512]{0:T(512)S(1)}, f32[]{:T(128)}, f32[512]{0:T(512)S(1)}, f32[512]{0:T(512)S(1)}, f32[512]{0:T(512)S(1)}, /*index=5*/f32[512]{0:T(512)S(1)}...) fusion(f32[512]{0:T(512)S(1)} %bitcast.177, f32[512]{0:T(512)S(1)} %bitcast.187, ...), kind=kOutput, calls=%fused_computation.355 | convolution fusion | flops 680521216 | bytes 6854664 | tf_op jit(solution)/shard_map/dot_general | solution.py:102
  167.5 10.6 %collective-permute-done.9 = bf16[512,1280]{1,0:T(8,128)(2,1)S(1)} collective-permute-done((bf16[512,1280]{1,0:T(8,128)(2,1)S(1)}, bf16[512,1280]{1,0:T(8,128)(2,1)S(1)}, u32[]{:S(2)}, u32[]{:S(2)}) %collective-permute-start.9) | collective-permute-done | bytes 1310752 | tf_op jit(solution)/shard_map/ppermute | solution.py:94
  178.2 2.2 %fusion.141 = f32[512,512]{1,0:T(8,128)S(1)} fusion(bf16[512,1280]{1,0:T(8,128)(2,1)S(1)} %collective-permute-done.9, bf16[512,4096]{1,0:T(8,128)(2,1)} %bitcast.1), kind=kOutput, calls=%fused_computation.342 | convolution fusion | flops 671088640 | bytes 3670016 | tf_op jit(solution)/shard_map/dot_general | solution.py:102
  180.4 0.9 fusion.165
  181.2 0.9 fusion.7
  182.1 4.5 %fusion.150 = (f32[512]{0:T(512)S(1)}, f32[]{:T(128)}, f32[512]{0:T(512)S(1)}, f32[512]{0:T(512)S(1)}, f32[512]{0:T(512)S(1)}, /*index=5*/f32[512]{0:T(512)S(1)}...) fusion(f32[512]{0:T(512)S(1)} %get-tuple-element.121, ...), kind=kOutput, calls=%fused_computation.351 | convolution fusion | flops 686023168 | bytes 7925772 | tf_op jit(solution)/shard_map/dot_general | solution.py:102
  190.2 0.8 convolution_bitcast_fusion
  191.1 0.8 reshape.1433
  191.9 6.1 %all-to-all-start.1 = ((f32[32,1,1024]{2,1,0:T(1,128)}), f32[32,1,1024]{2,1,0:T(1,128)S(1)}, u32[]{:S(2)}, u32[]{:S(2)}) async-start(f32[32,1,1024]{2,1,0:T(1,128)} %reshape.1433), calls=%async_computation.1 | async-start | bytes 262144 | tf_op jit(solution)/shard_map/all_to_all | solution.py:244
  198.1 0.6 reduce_sum.344
  199.7 6.8 %all-to-all-done.1 = f32[32,1,1024]{2,1,0:T(1,128)S(1)} async-done(((f32[32,1,1024]{2,1,0:T(1,128)}), f32[32,1,1024]{2,1,0:T(1,128)S(1)}, u32[]{:S(2)}, u32[]{:S(2)}) %all-to-all-start.1) | async-done | bytes 131104 | tf_op jit(solution)/shard_map/all_to_all | solution.py:244
  207.0 0.9 reduce.24
  208.2 0.6 slice_reduce_fusion.1
  208.8 0.6 slice_reduce_fusion
  212.0 0.6 fusion.43
  (92 shorter events, 7.3 us)
Async XLA Ops:
  0.6 4.5 %collective-permute-start.1 = (bf16[256,4096]{1,0:T(8,128)(2,1)}, bf16[256,4096]{1,0:T(8,128)(2,1)S(1)}, u32[]{:S(2)}, u32[]{:S(2)}) collective-permute-start(bf16[256,4096]{1,0:T(8,128)(2,1)} %param.7), channel_id=1, source_target_pairs={{0,1},{1,0},{2,3},{3,2},{4,5},{5,4},{6,7},{7,6},{8,9},{9,8},{10,11... | collective-permute-start | bytes 6291464 | tf_op jit(solution)/shard_map/ppermute | solution.py:94
  1.5 3.6 %collective-permute-start = (s32[256]{0:T(256)S(1)}, s32[256]{0:T(256)S(1)}, u32[]{:S(2)}, u32[]{:S(2)}) collective-permute-start(s32[256]{0:T(256)S(1)} %get-tuple-element.67), channel_id=1, source_target_pairs={{0,1},{1,0},{2,3},{3,2},{4,5},{5,4},{6,7},{7,6},{8,9},{9,8},{10,11... | collective-permute-start | bytes 3080 | tf_op jit(solution)/shard_map/ppermute | solution.py:94
  8.4 8.0 %copy-start.1 = (s32[3,1]{0,1:T(1,128)S(1)}, s32[3,1]{0,1:T(1,128)}, u32[]{:S(2)}) copy-start(s32[3,1]{0,1:T(1,128)} %param.11) | copy-start | bytes 40
  8.4 8.1 %copy-start = (s32[1,8,128]{2,1,0:T(8,128)S(1)}, s32[1,8,128]{2,1,0:T(8,128)}, u32[]{:S(2)}) copy-start(s32[1,8,128]{2,1,0:T(8,128)} %param.10) | copy-start | bytes 12292
  8.4 35.6 %all-to-all-start = ((bf16[8,64,4096]{2,1,0:T(8,128)(2,1)}), bf16[8,64,4096]{2,1,0:T(8,128)(2,1)}, u32[]{:S(2)}, u32[]{:S(2)}) async-start(bf16[8,64,4096]{2,1,0:T(8,128)(2,1)} %bitcast.133), calls=%async_computation | async-start | bytes 8388608 | tf_op jit(solution)/shard_map/all_to_all | solution.py:164
  16.6 1.0 collective-permute-start.2
  49.6 75.1 %collective-permute-start.5 = (bf16[512,1024]{1,0:T(8,128)(2,1)}, bf16[512,1024]{1,0:T(8,128)(2,1)}, u32[]{:S(2)}, u32[]{:S(2)}) collective-permute-start(bf16[512,1024]{1,0:T(8,128)(2,1)} %slice.228), channel_id=1, source_target_pairs={{0,32},{1,9},{2,34},{3,11},{4,36},{5,13},{6,38},{7,15},{8,40},{9,1... | collective-permute-start | bytes 3145736 | tf_op jit(solution)/shard_map/ppermute | solution.py:94
  51.4 88.5 %collective-permute-start.15 = (bf16[512,1024]{1,0:T(8,128)(2,1)}, bf16[512,1024]{1,0:T(8,128)(2,1)}, u32[]{:S(2)}, u32[]{:S(2)}) collective-permute-start(bf16[512,1024]{1,0:T(8,128)(2,1)} %slice.228), channel_id=1, source_target_pairs={{0,96},{1,25},{2,98},{3,27},{4,100},{5,29},{6,102},{7,31},{8,104},... | collective-permute-start | bytes 3145736 | tf_op jit(solution)/shard_map/ppermute | solution.py:94
  52.9 63.5 %collective-permute-start.6 = (bf16[512,512]{1,0:T(8,128)(2,1)}, bf16[512,512]{1,0:T(8,128)(2,1)S(1)}, u32[]{:S(2)}, u32[]{:S(2)}) collective-permute-start(bf16[512,512]{1,0:T(8,128)(2,1)} %slice.229), channel_id=1, source_target_pairs={{0,32},{1,9},{2,34},{3,11},{4,36},{5,13},{6,38},{7,15},{8,40},{9,1... | collective-permute-start | bytes 1572872 | tf_op jit(solution)/shard_map/ppermute | solution.py:94
  53.4 66.9 %collective-permute-start.16 = (bf16[512,512]{1,0:T(8,128)(2,1)}, bf16[512,512]{1,0:T(8,128)(2,1)S(1)}, u32[]{:S(2)}, u32[]{:S(2)}) collective-permute-start(bf16[512,512]{1,0:T(8,128)(2,1)} %slice.229), channel_id=1, source_target_pairs={{0,96},{1,25},{2,98},{3,27},{4,100},{5,29},{6,102},{7,31},{8,104},... | collective-permute-start | bytes 1572872 | tf_op jit(solution)/shard_map/ppermute | solution.py:94
  98.1 7.9 %collective-permute-start.7 = (f32[4,512]{1,0:T(4,128)S(1)}, f32[4,512]{1,0:T(4,128)S(1)}, u32[]{:S(2)}, u32[]{:S(2)}) collective-permute-start(f32[4,512]{1,0:T(4,128)S(1)} %pad_maximum_fusion.1), channel_id=1, source_target_pairs={{0,32},{1,9},{2,34},{3,11},{4,36},{5,13},{6,38},{7,15},{8,40},{9,1... | collective-permute-start | bytes 24584 | tf_op jit(solution)/shard_map/ppermute | solution.py:94
  105.9 4.6 %collective-permute-start.17 = (f32[4,512]{1,0:T(4,128)S(1)}, f32[4,512]{1,0:T(4,128)S(1)}, u32[]{:S(2)}, u32[]{:S(2)}) collective-permute-start(f32[4,512]{1,0:T(4,128)S(1)} %pad_maximum_fusion.1), channel_id=1, source_target_pairs={{0,96},{1,25},{2,98},{3,27},{4,100},{5,29},{6,102},{7,31},{8,104},... | collective-permute-start | bytes 24584 | tf_op jit(solution)/shard_map/ppermute | solution.py:94
  110.5 3.8 %collective-permute-start.12 = (f32[4,512]{1,0:T(4,128)S(1)}, f32[4,512]{1,0:T(4,128)S(1)}, u32[]{:S(2)}, u32[]{:S(2)}) collective-permute-start(f32[4,512]{1,0:T(4,128)S(1)} %pad_maximum_fusion.1), channel_id=1, source_target_pairs={{0,34},{1,15},{2,0},{3,5},{4,38},{5,11},{6,4},{7,1},{8,42},{9,23},... | collective-permute-start | bytes 24584 | tf_op jit(solution)/shard_map/ppermute | solution.py:94
  114.3 18.9 %collective-permute-start.3 = (bf16[512,1280]{1,0:T(8,128)(2,1)S(1)}, bf16[512,1280]{1,0:T(8,128)(2,1)S(1)}, u32[]{:S(2)}, u32[]{:S(2)}) collective-permute-start(bf16[512,1280]{1,0:T(8,128)(2,1)S(1)} %slice.226), channel_id=1, source_target_pairs={{0,32},{1,9},{2,34},{3,11},{4,36},{5,13},{6,38},{7,15},{8,40},{9,1... | collective-permute-start | bytes 3932168 | tf_op jit(solution)/shard_map/ppermute | solution.py:94
  116.4 48.7 %collective-permute-start.13 = (bf16[512,1280]{1,0:T(8,128)(2,1)S(1)}, bf16[512,1280]{1,0:T(8,128)(2,1)S(1)}, u32[]{:S(2)}, u32[]{:S(2)}) collective-permute-start(bf16[512,1280]{1,0:T(8,128)(2,1)S(1)} %slice.226), channel_id=1, source_target_pairs={{0,96},{1,25},{2,98},{3,27},{4,100},{5,29},{6,102},{7,31},{8,104},... | collective-permute-start | bytes 3932168 | tf_op jit(solution)/shard_map/ppermute | solution.py:94
  120.4 11.0 %collective-permute-start.11 = (bf16[512,512]{1,0:T(8,128)(2,1)S(1)}, bf16[512,512]{1,0:T(8,128)(2,1)S(1)}, u32[]{:S(2)}, u32[]{:S(2)}) collective-permute-start(bf16[512,512]{1,0:T(8,128)(2,1)S(1)} %broadcast_select_fusion.3), channel_id=1, source_target_pairs={{0,2},{1,7},{2,0},{3,5},{4,6},{5,3},{6,4},{7,1},{8,10},{9,15},{10,... | collective-permute-start | bytes 1572872 | tf_op jit(solution)/shard_map/ppermute | solution.py:94
  126.3 22.2 %collective-permute-start.10 = (bf16[512,1024]{1,0:T(8,128)(2,1)S(1)}, bf16[512,1024]{1,0:T(8,128)(2,1)S(1)}, u32[]{:S(2)}, u32[]{:S(2)}) collective-permute-start(bf16[512,1024]{1,0:T(8,128)(2,1)S(1)} %broadcast_select_fusion.2), channel_id=1, source_target_pairs={{0,2},{1,7},{2,0},{3,5},{4,6},{5,3},{6,4},{7,1},{8,10},{9,15},{10,... | collective-permute-start | bytes 3145736 | tf_op jit(solution)/shard_map/ppermute | solution.py:94
  135.3 18.9 %collective-permute-start.4 = (bf16[512,1280]{1,0:T(8,128)(2,1)S(1)}, bf16[512,1280]{1,0:T(8,128)(2,1)S(1)}, u32[]{:S(2)}, u32[]{:S(2)}) collective-permute-start(bf16[512,1280]{1,0:T(8,128)(2,1)S(1)} %get-tuple-element.71), channel_id=1, source_target_pairs={{0,32},{1,9},{2,34},{3,11},{4,36},{5,13},{6,38},{7,15},{8,40},{9,1... | collective-permute-start | bytes 3932168 | tf_op jit(solution)/shard_map/ppermute | solution.py:94
  142.2 19.7 %collective-permute-start.14 = (bf16[512,1280]{1,0:T(8,128)(2,1)S(1)}, bf16[512,1280]{1,0:T(8,128)(2,1)S(1)}, u32[]{:S(2)}, u32[]{:S(2)}) collective-permute-start(bf16[512,1280]{1,0:T(8,128)(2,1)S(1)} %get-tuple-element.71), channel_id=1, source_target_pairs={{0,96},{1,25},{2,98},{3,27},{4,100},{5,29},{6,102},{7,31},{8,104},... | collective-permute-start | bytes 3932168 | tf_op jit(solution)/shard_map/ppermute | solution.py:94
  144.8 36.4 %collective-permute-start.8 = (bf16[512,1280]{1,0:T(8,128)(2,1)S(1)}, bf16[512,1280]{1,0:T(8,128)(2,1)S(1)}, u32[]{:S(2)}, u32[]{:S(2)}) collective-permute-start(bf16[512,1280]{1,0:T(8,128)(2,1)S(1)} %get-tuple-element.70), channel_id=1, source_target_pairs={{0,2},{1,7},{2,0},{3,5},{4,6},{5,3},{6,4},{7,1},{8,10},{9,15},{10,... | collective-permute-start | bytes 3932168 | tf_op jit(solution)/shard_map/ppermute | solution.py:94
  155.7 22.5 %collective-permute-start.9 = (bf16[512,1280]{1,0:T(8,128)(2,1)S(1)}, bf16[512,1280]{1,0:T(8,128)(2,1)S(1)}, u32[]{:S(2)}, u32[]{:S(2)}) collective-permute-start(bf16[512,1280]{1,0:T(8,128)(2,1)S(1)} %broadcast_select_fusion), channel_id=1, source_target_pairs={{0,2},{1,7},{2,0},{3,5},{4,6},{5,3},{6,4},{7,1},{8,10},{9,15},{10,... | collective-permute-start | bytes 3932168 | tf_op jit(solution)/shard_map/ppermute | solution.py:94
  191.9 14.5 %all-to-all-start.1 = ((f32[32,1,1024]{2,1,0:T(1,128)}), f32[32,1,1024]{2,1,0:T(1,128)S(1)}, u32[]{:S(2)}, u32[]{:S(2)}) async-start(f32[32,1,1024]{2,1,0:T(1,128)} %reshape.1433), calls=%async_computation.1 | async-start | bytes 262144 | tf_op jit(solution)/shard_map/all_to_all | solution.py:244

commit v2 on v1

v2 whole, which is shorter than its diff:
```python
import functools

import jax
import jax.numpy as jnp
from jax import lax
from jax.experimental import pallas as pl
from jax.experimental.pallas import tpu as pltpu
from jax.sharding import PartitionSpec as P


AX = ("dp", "cls")
F32 = jnp.float32
BF16 = jnp.bfloat16
BIG = 1e30
CHUNKS = (128, 128, 256)
STEP = 64
PARTS = 1


def dix(x, y, z, c):
    return x * 32 + (z // 2) * 16 + (z % 2) * 8 + y * 2 + c


def xyz(d):
    return d // 32, (d // 2) % 4, ((d // 16) % 2) * 2 + (d // 8) % 2, d % 2


DEV = range(128)
MATE = ((1, 0, 3, 2), (3, 2, 1, 0))
PAIRS = (((0, 1), (2, 3)), ((2, 1), (0, 3)))


def mate(d):
    x, y, z, c = xyz(d)
    return dix(x, MATE[c][y], z, c)


def along(d, k):
    x, y, z, c = xyz(d)
    return dix((x + k) % 4, y, z, c) if c == 0 else dix(x, y, (z + k) % 4, c)


def side(d):
    return xyz(d)[1] % 2


SWAP = [(d, d ^ 1) for d in DEV]
UP = [(d, along(d, 1)) for d in DEV]
DOWN = [(d, along(d, -1)) for d in DEV]
ACROSS = [(d, mate(d)) for d in DEV]
FOURTH = [(d, mate(d) if side(d) == 1 else mate(along(d, 1))) for d in DEV]


def regroup_groups():
    groups = []
    for x in range(4):
        for ys in ((0, 3), (1, 2)):
            groups.append([dix(x, y, z, 0) for y in ys for z in range(4)])
    for z in range(4):
        for ys in ((1, 0), (2, 3)):
            groups.append([dix(x, y, z, 1) for y in ys for x in range(4)])
    return groups


def class_groups():
    groups = []
    for c in (0, 1):
        for pair in PAIRS[c]:
            for u in range(4):
                group = [dix(t, y, u, 0) if c == 0 else dix(u, y, t, 1) for t in range(4) for y in pair]
                groups.append(group)
    return groups


def final_groups():
    groups = []
    for c in (0, 1):
        for pair in PAIRS[c]:
            groups.append([dix(x, y, z, c) for x in range(4) for z in range(4) for y in pair])
    return groups


def info_pairs():
    out = []
    for d in DEV:
        x, y, z, c = xyz(d)
        zh, zl = z // 2, z % 2
        if c == 0:
            src = dix(x, (y // 2) * 2 + zh, (y % 2) * 2 + zl, 0)
        else:
            yk = y if y % 2 == x % 2 else MATE[1][y]
            src = dix(zh * 2 + zl, yk, (y % 2) * 2 + x // 2, 1)
        out.append((src, d))
    return out


INFO = info_pairs()


def send(value, pairs):
    return lax.ppermute(value, AX, pairs)


def iota(shape, dim):
    return lax.broadcasted_iota(jnp.int32, shape, dim)


def inner(left, right):
    return lax.dot_general(left, right, (((1,), (1,)), ((), ())), preferred_element_type=F32)


def exact(left, right):
    return jnp.dot(left, right, precision=lax.Precision.HIGHEST, preferred_element_type=F32)


def exact_dot(left, right, dims=(((1,), (0,)), ((), ()))):
    return lax.dot_general(left, right, dims, precision=lax.Precision.HIGHEST, preferred_element_type=F32)


def split3(value):
    high = value.astype(BF16)
    rest = value - high.astype(F32)
    middle = rest.astype(BF16)
    return high, middle, (rest - middle.astype(F32)).astype(BF16)


def pair_work(tasks, q_parts, groups, hbm, note_refs, col_refs, q_buf, u_bufs, x_ref, side_ref, sems):
    copies = {}
    count = 0
    width = q_buf.shape[1]
    cuts = [slice(h * width // PARTS, (h + 1) * width // PARTS) for h in range(PARTS)]
    for kind, parts, bufs in (("q", q_parts, [q_buf] * len(q_parts)), ("u", groups, u_bufs)):
        for i, members in enumerate(parts):
            if members is None:
                continue
            at = i * 512 if kind == "q" else 0
            for name in members:
                k = hbm[name].shape[0]
                for h, cut in enumerate(cuts):
                    copy = pltpu.make_async_copy(hbm[name].at[:, cut], bufs[i].at[at : at + k, cut], sems.at[count])
                    copies.setdefault((kind, i, h), []).append(copy)
                    count += 1
                at += k
    begun = []
    for g, rows in tasks:
        for h in range(PARTS):
            for key in [("u", g, h)] + [("q", q, h) for q, _, _ in rows]:
                if key in copies and key not in begun:
                    begun.append(key)
                    for copy in copies[key]:
                        copy.start()
    for q in range(len(q_parts)):
        parts = jnp.concatenate([p.astype(F32) for p in split3(note_refs[q][...])], axis=0).astype(BF16)
        along = (iota((24, 512), 0) % 8 == iota((24, 512), 1) // 128).astype(BF16)
        wide = lax.dot_general(parts, along, (((0,), (0,)), ((), ())), preferred_element_type=F32)
        for j in range(4):
            side_ref[q, j] = wide[:, j * 128 : j * 128 + 128]
    ready = set()
    fresh = set(col_refs)
    far = jnp.zeros((8, 128), F32)
    lanes = {}
    for g, given in tasks:
        data = q_buf if groups[g] is None else u_bufs[g]
        m = 512 if groups[g] is None else data.shape[0]
        lo, hi = 512 * given[0][0], 512 * given[-1][0] + 512
        tiles = m // 128
        u_half, u_mark, u_one, u_two = [
            [
                jnp.broadcast_to(note_refs[len(q_parts) + g][i : i + 1, t * 128 : t * 128 + 128], (8, 128))
                for t in range(tiles)
            ]
            for i in range(4)
        ]
        for h, cut in enumerate(cuts):
            for key in [("u", g, h)] + [("q", q, h) for q, _, _ in given]:
                if key in copies and key not in ready:
                    ready.add(key)
                    for copy in copies[key]:
                        copy.wait()
            part = lax.dot_general(
                q_buf[lo:hi, cut], data[:m, cut], (((1,), (1,)), ((), ())), preferred_element_type=F32
            )
            if h == 0:
                x_ref[lo:hi, :m] = part
            else:
                x_ref[lo:hi, :m] += part
        for q, to_u, to_q in given:
            first_use = to_q and q in fresh
            if to_q:
                fresh.discard(q)

            def step(i, carry, q=q, to_u=to_u, to_q=to_q, first_use=first_use, tiles=tiles, u=(u_half, u_mark, u_one, u_two)):
                carry = [list(c) for c in carry]
                u_half, u_mark, u_one, u_two = u
                start = pl.multiple_of(i * STEP, STEP)
                for k in range(STEP // 8):
                    rows = pl.ds(start + k * 8, 8)
                    q_half, q_mark, q_one, q_two = (side_ref[q, j, rows, :] for j in range(4))
                    sums = [None, None, None]
                    for t in range(tiles):
                        x = x_ref[pl.ds(start + (q * 512 + k * 8), 8), t * 128 : t * 128 + 128]
                        carry[0][t] = jnp.maximum(carry[0][t], (q_mark - x) + u_mark[t])
                        if to_u:
                            carry[1][t] = carry[1][t] + x
                            carry[2][t] = carry[2][t] + jnp.maximum((x + q_one) - u_half[t], 0.0)
                            carry[3][t] = carry[3][t] + jnp.maximum((x + q_two) - u_half[t], 0.0)
                        if to_q:
                            off = x - q_half
                            values = (x, jnp.maximum(off + u_one[t], 0.0), jnp.maximum(off + u_two[t], 0.0))
                            sums = [v if s is None else s + v for s, v in zip(sums, values)]
                    if to_q:
                        for j in range(3):
                            if first_use:
                                col_refs[q][j, rows, :] = sums[j]
                            else:
                                col_refs[q][j, rows, :] += sums[j]
                return carry

            zero = [jnp.zeros((8, 128), F32)] * tiles
            done = lax.fori_loop(0, 512 // STEP, step, [zero] * (4 if to_u else 1))
            for t in range(tiles):
                far = jnp.maximum(far, done[0][t])
            if to_u:
                done = done[1:]
                lanes[g] = [[a + b for a, b in zip(v, w)] for v, w in zip(lanes[g], done)] if g in lanes else done
    rows = {
        g: [
            jnp.concatenate([jnp.sum(v, axis=0, keepdims=True) for v in kind], axis=1) for kind in value
        ]
        for g, value in lanes.items()
    }
    return rows, far


def scratch_for(q_parts, groups, sizes, width):
    q_bufs = [pltpu.VMEM((512 * len(q_parts), width), BF16)]
    u_sizes = [sum(sizes[i] for i in p) if p else 0 for p in groups]
    u_bufs = [pltpu.VMEM((n or 16, width), BF16) for n in u_sizes]
    n_copies = sum(len(p) for p in q_parts) + sum(len(p) for p in groups if p)
    most = max([n or 512 for n in u_sizes])
    return q_bufs + u_bufs + [
        pltpu.VMEM((512 * len(q_parts), most), F32),
        pltpu.VMEM((len(q_parts), 4, 512, 128), F32),
        pltpu.SemaphoreType.DMA((n_copies * PARTS,)),
    ]


def cost_of(tasks, q_parts, groups, sizes, width):
    def rows(p):
        return sum(sizes[i] for i in (p or q_parts[0]))

    flops = sum(2 * 512 * len(t[1]) * rows(groups[t[0]]) * width for t in tasks)
    moved = 2 * width * sum(sizes)
    return pl.CostEstimate(flops=flops, transcendentals=0, bytes_accessed=moved)


VMEM_SPEC = pl.BlockSpec(memory_space=pltpu.VMEM)
ANY_SPEC = pl.BlockSpec(memory_space=pl.ANY)
LIMIT = pltpu.CompilerParams(vmem_limit_bytes=36 * 2**20)


def early_kernel(tasks, q_parts, groups, n_hbm, lane_outs, col_outs, *refs):
    hbm, refs = refs[:n_hbm], refs[n_hbm:]
    n_notes = len(q_parts) + len(groups)
    notes, refs = refs[:n_notes], refs[n_notes:]
    lane_refs, refs = refs[: len(lane_outs)], refs[len(lane_outs) :]
    cols, refs = dict(zip(col_outs, refs)), refs[len(col_outs) :]
    far_ref, refs = refs[0], refs[1:]
    q_buf, refs = refs[0], refs[1:]
    u_bufs, (x_ref, side_ref, sems) = refs[: len(groups)], refs[len(groups) :]
    rows, far = pair_work(tasks, q_parts, groups, hbm, notes, cols, q_buf, u_bufs, x_ref, side_ref, sems)
    for g, ref in zip(lane_outs, lane_refs):
        ref[...] = jnp.zeros_like(ref)
        for j in range(3):
            ref[j : j + 1, :] = rows[g][j]
    far_ref[...] = far


def early_pairs(hbm, q_parts, groups, notes, tasks):
    sizes, width = [h.shape[0] for h in hbm], hbm[0].shape[1]
    lane_outs = [t[0] for t in tasks if any(v[1] for v in t[1])]
    col_outs = [q for q in range(len(q_parts)) if any(v[0] == q and v[2] for t in tasks for v in t[1])]
    shapes = [jax.ShapeDtypeStruct((8, notes[len(q_parts) + g].shape[1]), F32) for g in lane_outs]
    shapes += [jax.ShapeDtypeStruct((3, 512, 128), F32) for _ in col_outs]
    shapes += [jax.ShapeDtypeStruct((8, 128), F32)]
    out = pl.pallas_call(
        functools.partial(early_kernel, tasks, q_parts, groups, len(hbm), lane_outs, col_outs),
        out_shape=shapes,
        in_specs=[ANY_SPEC] * len(hbm) + [VMEM_SPEC] * len(notes),
        out_specs=[VMEM_SPEC] * len(shapes),
        scratch_shapes=scratch_for(q_parts, groups, sizes, width),
        cost_estimate=cost_of(tasks, q_parts, groups, sizes, width),
        compiler_params=LIMIT,
    )(*hbm, *notes)
    n = len(lane_outs)
    return dict(zip(lane_outs, out)), dict(zip(col_outs, out[n:])), out[-1]


def last_kernel(tasks, q_parts, groups, n_hbm, lane_rows, n_cols, n_far, own_rows, *refs):
    hbm, refs = refs[:n_hbm], refs[n_hbm:]
    n_notes = len(q_parts) + len(groups)
    notes, refs = refs[:n_notes], refs[n_notes:]
    lane_refs, refs = refs[: len(lane_rows)], refs[len(lane_rows) :]
    col_refs, refs = refs[: sum(n_cols)], refs[sum(n_cols) :]
    far_refs, refs = refs[:n_far], refs[n_far:]
    extra_ref, out_ref, refs = refs[0], refs[1], refs[2:]
    q_buf, refs = refs[0], refs[1:]
    u_bufs, refs = refs[: len(groups)], refs[len(groups) :]
    x_ref, side_ref, sems, col0_ref, col1_ref, g_ref = refs
    cols = {0: col0_ref, 1: col1_ref}
    rows, far = pair_work(tasks, q_parts, groups, hbm, notes, cols, q_buf, u_bufs, x_ref, side_ref, sems)
    g_ref[...] = extra_ref[...]
    for ref, (row, at) in zip(lane_refs, lane_rows):
        m = ref.shape[1]
        g_ref[row : row + 3, at : at + m] += ref[0:3, :]
    for g, (row, at) in own_rows.items():
        for j in range(3):
            value = rows[g][j]
            g_ref[row + j : row + j + 1, at : at + value.shape[1]] += value
    start = 0
    for q, (n, row) in enumerate(zip(n_cols, (0, 8))):
        for j in range(3):
            total = cols[q][j]
            for ref in col_refs[start : start + n]:
                total = total + ref[j]
            across = jnp.sum(jnp.transpose(total), axis=0, keepdims=True)
            g_ref[row + j : row + j + 1, :] += across
        start += n
    for ref in far_refs:
        far = jnp.maximum(far, ref[...])
    far = jnp.max(jnp.max(far, axis=0, keepdims=True), axis=1, keepdims=True)
    g_ref[7:8, :] = jnp.broadcast_to(far, (1, 512))
    lane = iota((512, 512), 0)
    to_lane = (lane // 4 % 8) * 64 + (lane // 32) * 4 + lane % 4
    by_member = (to_lane == iota((512, 512), 1)).astype(BF16)
    parts = jnp.concatenate([p.astype(F32) for p in split3(g_ref[...])], axis=0).astype(BF16)
    given = jnp.dot(parts, by_member, preferred_element_type=F32)
    given = given[0:16] + given[16:32] + given[32:48]
    for m in range(8):
        piece = given[:, m * 64 : m * 64 + 64]
        page = jnp.concatenate([piece[0:8], piece[8:16]], axis=1)
        for copy in range(4):
            out_ref[m * 4 + copy] = page


def last_pairs(hbm, q_parts, groups, notes, tasks, lanes, lane_rows, cols, fars, own_rows, extra):
    sizes, width = [h.shape[0] for h in hbm], hbm[0].shape[1]
    n_cols = tuple(len(c) for c in cols)
    small = lanes + [c for each in cols for c in each] + fars + [extra]
    return pl.pallas_call(
        functools.partial(
            last_kernel, tasks, q_parts, groups, len(hbm), lane_rows, n_cols, len(fars), own_rows
        ),
        out_shape=jax.ShapeDtypeStruct((32, 8, 128), F32),
        in_specs=[ANY_SPEC] * len(hbm) + [VMEM_SPEC] * (len(notes) + len(small)),
        out_specs=VMEM_SPEC,
        scratch_shapes=scratch_for(q_parts, groups, sizes, width)
        + [pltpu.VMEM((3, 512, 128), F32), pltpu.VMEM((3, 512, 128), F32), pltpu.VMEM((16, 512), F32)],
        cost_estimate=cost_of(tasks, q_parts, groups, sizes, width),
        compiler_params=LIMIT,
    )(*hbm, *notes, *small)


def prep_kernel(own_ref, hit_ref, found_ref, half_ref, buf, part, sems):
    slab = 128
    n = buf.shape[0] // slab
    copies = [
        pltpu.make_async_copy(own_ref.at[i * slab : i * slab + slab, :], buf.at[i * slab : i * slab + slab, :], sems.at[i])
        for i in range(n)
    ]
    for copy in copies:
        copy.start()
    for i, copy in enumerate(copies):
        copy.wait()

        def step(k, _, i=i):
            rows = pl.ds(pl.multiple_of(i * slab + k * 16, 16), 16)
            total = None
            for t in range(buf.shape[1] // 128):
                v = buf[rows, t * 128 : t * 128 + 128].astype(F32)
                total = v * v if total is None else total + v * v
            part[rows, :] = total
            return 0

        lax.fori_loop(0, slab // 16, step, 0)
    half_ref[...] = 0.5 * jnp.sum(jnp.transpose(part[...]), axis=0, keepdims=True)
    found = jnp.dot(hit_ref[...], buf[...], preferred_element_type=F32).astype(BF16)
    for i in range(8):
        found_ref[i] = found


def prepare(own, hit):
    width = own.shape[1]
    return pl.pallas_call(
        prep_kernel,
        out_shape=[jax.ShapeDtypeStruct((8, 8, width), BF16), jax.ShapeDtypeStruct((1, 512), F32)],
        in_specs=[ANY_SPEC, VMEM_SPEC],
        out_specs=[VMEM_SPEC, VMEM_SPEC],
        scratch_shapes=[pltpu.VMEM((512, width), BF16), pltpu.VMEM((512, 128), F32), pltpu.SemaphoreType.DMA((4,))],
        cost_estimate=pl.CostEstimate(flops=2 * 512 * 512 * width, transcendentals=0, bytes_accessed=own.size * 2),
        compiler_params=LIMIT,
    )(own, hit)


def close_kernel(width, where_ref, in_ref, order_ref, keep_ref, total_ref, gain_ref, cover_ref):
    lane = iota((4, 128), 1)
    row = iota((4, 128), 0)

    def page(line, sd):
        return in_ref[where_ref[0] + where_ref[1] * (line % 4) + sd]

    final = jnp.zeros((8, 512), F32)
    far = jnp.zeros((1, 64), F32)
    half_sum = jnp.zeros((1, 64), F32)
    for line in range(4):
        for sd in range(2):
            here = page(line, sd)
            far = jnp.maximum(far, here[7:8, 0:64])
            half_sum = half_sum + here[3:4, 64:128]
            low = here[0:4] + jnp.where(row < 3, page(line + 1, sd)[4:8], 0.0)
            fourth = page(line, 0) if sd == 1 else page(line + 1, 1)
            high = jnp.where(row < 3, page(line + 3, sd)[0:4] + fourth[4:8], 0.0)
            both = jnp.where(lane < 64, low, high)
            both = both[:, 0:64] + both[:, 64:128]
            both = jnp.concatenate([both, jnp.zeros((4, 64), F32)], axis=0)
            at = (line * 2 + sd) * 64
            final = final + exact_dot(both, order_ref[at : at + 64, :])
    far = 2.0 * far[:, 0:1]
    half_sum = half_sum[:, 0:1]
    keep = keep_ref[...]
    total = total_ref[:, 0:1]
    scale = 1.0 / width
    gain_ref[0:1, :] = (2.0 * final[0:1] + total * far - 2.0 * half_sum) * scale * keep / total
    gain_ref[1:3, :] = 2.0 * final[1:3] * scale * keep / total
    cover_ref[...] = keep * (far - 2.0 * final[3:4]) * scale


def source_of(x, z, y, core, row):
    group, sub, member, slot = row // 64, row // 32 % 2, row // 4 % 8, row % 4
    i, w = group // 4, group % 4
    outer = (y == 0) | (y == 3)
    low = y < 2
    y0 = jnp.where(outer, 3 * i, 1 + i)
    y1 = jnp.where(low, 1 - i, 2 + i)
    sx = jnp.where(core == 0, x, w)
    sz = jnp.where(core == 0, w, z)
    sy = jnp.where(core == 0, y0, y1)
    return dix(sx, sy, sz, jnp.where(sub == 0, 0, 1)), member, slot


def body(sketches, labels, places, counts, chosen):
    rows_dev, width = sketches.shape
    dp, cls = lax.axis_index("dp"), lax.axis_index("cls")
    x, zh, zl, y, core = dp // 2, dp % 2, cls // 8, cls // 2 % 4, cls % 2
    z = zh * 2 + zl
    edge = y % 2
    first = core == 0

    packed = jnp.concatenate([counts[0], jnp.broadcast_to(chosen, (3, 128))], axis=0)
    packed = send(packed, INFO)
    host_counts = packed[:8].astype(F32)
    picks = packed[8:11, 0]

    k_core, k_y, k_zl = labels % 2, labels // 2 % 4, labels // 8
    group = jnp.where(
        k_core == 0,
        (k_y // 2) * 4 + (k_y % 2) * 2 + k_zl,
        ((k_y + 3) % 4 // 2) * 4 + k_zl * 2 + k_y % 2,
    )
    spot = group * 64 + core * 32 + places // 512 * 4 + places % 4
    mine = jnp.where(k_core == core, spot, -1)
    theirs = jnp.where(k_core == core, -1, spot)
    from_twin = send(sketches, SWAP)
    twin_spot = send(theirs, SWAP)
    slots = iota((2 * rows_dev, rows_dev), 0)
    table_own = (slots == mine[None, :]).astype(BF16)
    table_twin = (slots == twin_spot[None, :]).astype(BF16)
    outgoing = (
        jnp.dot(table_own, sketches, preferred_element_type=F32)
        + jnp.dot(table_twin, from_twin, preferred_element_type=F32)
    ).astype(BF16)
    own = lax.all_to_all(
        outgoing.reshape(8, 64, width), AX, 0, 0, axis_index_groups=regroup_groups(), tiled=True
    ).reshape(512, width)

    src, member, slot = source_of(x, z, y, core, iota((1, 512), 1))
    place = member * 512 + src * 4 + slot
    seen = jnp.sum(
        jnp.where(iota((128, 512), 0) == src, exact(host_counts.T, (iota((8, 512), 0) == member).astype(F32)), 0.0),
        axis=0,
    )
    valid = slot[0].astype(F32) < seen
    n_valid = jnp.sum(host_counts)
    hit = (place == jnp.concatenate([picks, -jnp.ones((5,), jnp.int32)])[:, None]).astype(BF16)
    found, half = prepare(own, hit)
    half = half[0]
    edges = [0]
    for size in CHUNKS:
        edges.append(edges[-1] + size)
    spans = list(zip(edges, edges[1:]))
    l, f = [], []
    late, found = lax.optimization_barrier((own, found))
    cuts = [(late if lo else own)[lo:hi] for lo, hi in spans]
    for cut in cuts:
        l.append(send(cut, UP))
    for i, cut in enumerate(cuts):
        f.append(send(jnp.where(edge == 0, l[i], cut), ACROSS))
    r = []
    for cut in cuts:
        r.append(send(cut, DOWN))

    found = lax.all_to_all(found, AX, 0, 0, axis_index_groups=class_groups(), tiled=True)
    found = jnp.sum(found.astype(F32), axis=0).astype(BF16)
    to_picks = inner(found, own)
    pick_half = 0.5 * jnp.sum(jnp.square(found.astype(F32)), axis=1)
    near = pick_half[:3, None] - to_picks[:3]
    near1 = near[0]
    near2 = jnp.minimum(near[0], near[1])
    near3 = jnp.minimum(near2, near[2])
    info = jnp.stack(
        [half, jnp.where(valid, half, -BIG), jnp.where(valid, near1, -BIG), jnp.where(valid, near2, -BIG)]
        + [jnp.zeros((512,), F32)] * 4
    )
    info_l = send(info, UP)
    info_r = send(info, DOWN)
    info_f = send(info, FOURTH)

    mid = edges[2]
    l_low, l_high = info_l[:, :mid], info_l[:, mid:]
    f_low, f_high = info_f[:, :mid], info_f[:, mid:]
    lanes_a, cols_a, far_a = early_pairs(
        [own, l[0], l[1]],
        [[0]],
        [None, [1, 2]],
        [info, info, l_low],
        [(0, [(0, True, False)]), (1, [(0, True, True)])],
    )
    lanes_b, cols_b, far_b = early_pairs(
        [own, *r, *l, f[0], f[1]],
        [[0], [1, 2, 3]],
        [[7, 8], [6], [4, 5]],
        [info, info_r, f_low, l_high, l_low],
        [(0, [(0, True, True), (1, True, True)]), (1, [(0, True, True), (1, False, True)]), (2, [(1, False, True)])],
    )
    none = jnp.zeros((512,), F32)
    extra = [none] * 16
    extra[0] = -n_valid * half
    extra[3] = half + near3
    extra[11] = jnp.broadcast_to(jnp.sum(half), (512,))
    extra = jnp.stack(extra)
    lane_list = [
        (lanes_a[0], (0, 0)),
        (lanes_a[1], (4, 0)),
        (lanes_b[0], (12, 0)),
        (lanes_b[1], (4, mid)),
    ]
    outbox = last_pairs(
        [own, *r, f[2]],
        [[0], [1, 2, 3]],
        [[4]],
        [info, info_r, f_high],
        [(0, [(0, True, True), (1, True, True)])],
        [v for v, _ in lane_list],
        [at for _, at in lane_list],
        [[cols_a[0], cols_b[0]], [cols_b[1]]],
        [far_a, far_b],
        {0: (12, mid)},
        extra,
    )
    inbox = lax.all_to_all(outbox, AX, 0, 0, axis_index_groups=final_groups(), tiled=True)

    lane1 = iota((512, 1), 0)
    line, sd, rest = lane1 // 128, lane1 // 64 % 2, lane1 % 64
    pair_y0 = y // 2 * 2 + sd
    pair_low = (y == 1) | (y == 2)
    pair_y1 = jnp.where(pair_low, 2 - sd, 3 * sd)
    pair_y = jnp.where(first, pair_y0, pair_y1)
    src2, _, slot2 = source_of(line, line, pair_y, core, (rest // 4) * 32 + rest % 4)
    in_order = (src2 * 4 + slot2 == iota((512, 512), 1)).astype(F32)

    class_counts = counts[0]
    own_counts = lax.dynamic_index_in_dim(class_counts, dp, 0, keepdims=False)
    keep = (iota((128, 4), 1) < own_counts[:, None]).reshape(1, 512).astype(F32)
    total = jnp.broadcast_to(jnp.sum(class_counts).astype(F32), (1, 128))
    host = jnp.where(first, (edge * 2 + zl) * 2, (zl * 2 + edge) * 8)
    where = jnp.stack([host, jnp.where(first, 8, 2)])
    gains, cover = pl.pallas_call(
        functools.partial(close_kernel, width),
        out_shape=[jax.ShapeDtypeStruct((3, 512), F32), jax.ShapeDtypeStruct((1, 512), F32)],
        in_specs=[pl.BlockSpec(memory_space=pltpu.SMEM)] + [VMEM_SPEC] * 4,
        out_specs=[VMEM_SPEC, VMEM_SPEC],
    )(where, inbox, in_order, keep, total)
    return (gains[:, None, :], cover)


def solution(mesh):
    placed = (
        P(("dp", "cls"), None),
        P(("dp", "cls")),
        P(("dp", "cls")),
        P("cls", None, None),
        P(None, "cls"),
    )
    return jax.shard_map(
        body,
        mesh=mesh,
        in_specs=placed,
        out_specs=(P(None, "cls", "dp"), P("cls", "dp")),
        check_vma=False,
    )
```

time: 214 us -> 212 us (level)
  the two profiles are of different devices: /device:TPU:0 before, /device:TPU:1 now
where the time goes in v2:
time: 212 us
  waiting for transfers between devices  93.5 us (44%)
  starting transfers between devices  40.3 us (19%)
  Pallas kernels  40.2 us (19%)
  other arithmetic  14.1 us (7%)
  local copies, waits for them, and re-layouts  11.4 us (5%)
  matrix products  9.9 us (5%)
    ppermute x15, waiting for transfers between devices, send(): return lax.ppermute(value, AX, pairs)  62.3 us
    all_to_all x1, waiting for transfers between devices, body(): lax.all_to_all(outgoing.reshape(8, 64, width), AX, 0, 0, axis_index_group...  25.3 us
    pallas_call x2, Pallas kernels, early_pairs(): pl.pallas_call(functools.partial(early_kernel, tasks, q_parts, groups, le...  24.9 us
    ppermute x15, starting transfers between devices, send(): return lax.ppermute(value, AX, pairs)  14.1 us
    all_to_all x1, starting transfers between devices, body(): lax.all_to_all(found, AX, 0, 0, axis_index_groups=class_groups(), tiled=T...  11.8 us
    pallas_call x1, Pallas kernels, last_pairs(): pl.pallas_call(functools.partial(last_kernel, tasks, q_parts, groups, len...  8.83 us
    all_to_all x1, starting transfers between devices, body(): lax.all_to_all(outbox, AX, 0, 0, axis_index_groups=final_groups(), tiled=...  8.44 us
    select_n x3, other arithmetic, body(): f.append(send(jnp.where(edge == 0, l[i], cut), ACROSS))  8.21 us
  transfers between devices with their start and end apart: 18, of which 8 were waited for; matrix products, arithmetic and copies ran while one was open for 14% of the time, Pallas kernels for 12%

profile of v2, /device:TPU:1, one launch (start us, length us, event | category | flops | bytes accessed | tf_op | source)
XLA Modules:
  0.0 211.5 jit_solution(17355620744251057268)
XLA Ops:
  0.6 1.5 collective-permute-start.1
  2.1 0.7 broadcast_select_fusion.6
  2.8 0.1 collective-permute-start
  2.9 2.8 %fusion.2 = f32[512,4096]{1,0:T(8,128)S(1)} fusion(bf16[256,4096]{1,0:T(8,128)(2,1)} %param.5, s32[256]{0:T(256)S(1)} %broadcast_select_fusion.5), kind=kOutput, calls=%fused_computation.11 | convolution fusion | flops 1073872896 | bytes 10486784 | tf_op jit(solution)/shard_map/dot_general | solution.py:479
  5.8 0.3 collective-permute-done
  6.1 0.0 collective-permute-done.1
  6.1 3.4 %add_convert_fusion = bf16[512,4096]{1,0:T(8,128)(2,1)} fusion(f32[512,4096]{1,0:T(8,128)S(1)} %fusion.2, bf16[256,4096]{1,0:T(8,128)(2,1)S(1)} %collective-permute-done.1, s32[256]{0:T(256)S(1)} %collective-permute-done), kind=kOutput, calls=%fused_computation | convolution fusion | flops 1078067200 | bytes 14681088 | tf_op jit(solution)/shard_map/dot_general | solution.py:480
  9.4 6.0 %all-to-all-start = ((bf16[8,64,4096]{2,1,0:T(8,128)(2,1)}), bf16[8,64,4096]{2,1,0:T(8,128)(2,1)}, u32[]{:S(2)}, u32[]{:S(2)}) async-start(bf16[8,64,4096]{2,1,0:T(8,128)(2,1)} %bitcast.16), calls=%async_computation | async-start | bytes 8388608 | tf_op jit(solution)/shard_map/all_to_all | solution.py:482
  15.4 0.1 pad.2.clone
  15.5 0.1 pad_add_fusion
  15.6 0.7 collective-permute-start.3
  16.3 0.0 collective-permute-done.3
  16.4 0.1 slice_reduce_fusion
  16.5 0.1 compare_convert_fusion.hit_ref
  16.6 25.3 %all-to-all-done = bf16[8,64,4096]{2,1,0:T(8,128)(2,1)} async-done(((bf16[8,64,4096]{2,1,0:T(8,128)(2,1)}), bf16[8,64,4096]{2,1,0:T(8,128)(2,1)}, u32[]{:S(2)}, u32[]{:S(2)}) %all-to-all-start) | async-done | bytes 4194336 | tf_op jit(solution)/shard_map/all_to_all | solution.py:482
  41.8 4.0 %shard_map.68 = (bf16[8,8,4096]{2,1,0:T(8,128)(2,1)}, f32[1,512]{1,0:T(1,128)S(1)}) custom-call(bf16[512,4096]{1,0:T(8,128)(2,1)} %bitcast.3.own_ref.refs_0_, bf16[8,512]{1,0:T(8,128)(2,1)S(1)} %compare_convert_fusion.hit_ref), custom_call_target="tpu_custom_call" | custom-call | flops 2147483648 | bytes 4194304 | tf_op jit(solution)/shard_map/pallas_call | solution.py:394
  45.9 11.8 %all-to-all-start.1 = ((bf16[8,8,4096]{2,1,0:T(8,128)(2,1)}), bf16[8,8,4096]{2,1,0:T(8,128)(2,1)}, u32[]{:S(2)}, u32[]{:S(2)}) async-start(bf16[8,8,4096]{2,1,0:T(8,128)(2,1)} %get-tuple-element.20), calls=%async_computation.1 | async-start | bytes 1048576 | tf_op jit(solution)/shard_map/all_to_all | solution.py:512
  57.7 0.6 fusion.12
  59.0 0.3 fusion
  59.3 2.3 %slice.49 = bf16[128,4096]{1,0:T(8,128)(2,1)} slice(bf16[512,4096]{1,0:T(8,128)(2,1)} %bitcast.3.own_ref.refs_0_), slice={[128:256], [0:4096]} | slice | bytes 2097152 | tf_op jit(solution)/shard_map/slice | solution.py:503
  61.6 3.2 %slice.50 = bf16[256,4096]{1,0:T(8,128)(2,1)} slice(bf16[512,4096]{1,0:T(8,128)(2,1)} %bitcast.3.own_ref.refs_0_), slice={[256:512], [0:4096]} | slice | bytes 4194304 | tf_op jit(solution)/shard_map/slice | solution.py:503
  64.8 2.7 %collective-permute-start.5 = (bf16[256,4096]{1,0:T(8,128)(2,1)}, bf16[256,4096]{1,0:T(8,128)(2,1)}, u32[]{:S(2)}, u32[]{:S(2)}) collective-permute-start(bf16[256,4096]{1,0:T(8,128)(2,1)} %slice.50), channel_id=1, source_target_pairs={{0,96},{1,25},{2,98},{3,27},{4,100},{5,29},{6,102},{7,31},{8,104},... | collective-permute-start | bytes 6291464 | tf_op jit(solution)/shard_map/ppermute | solution.py:101
  67.4 0.0 collective-permute-start.6
  67.4 0.3 collective-permute-start.11
  67.7 2.4 %collective-permute-start.4 = (bf16[128,4096]{1,0:T(8,128)(2,1)}, bf16[128,4096]{1,0:T(8,128)(2,1)}, u32[]{:S(2)}, u32[]{:S(2)}) collective-permute-start(bf16[128,4096]{1,0:T(8,128)(2,1)} %slice.49), channel_id=1, source_target_pairs={{0,96},{1,25},{2,98},{3,27},{4,100},{5,29},{6,102},{7,31},{8,104},... | collective-permute-start | bytes 3145736 | tf_op jit(solution)/shard_map/ppermute | solution.py:101
  70.1 2.3 %slice.63 = bf16[2,64,4096]{2,1,0:T(8,128)(2,1)} slice(bf16[8,64,4096]{2,1,0:T(8,128)(2,1)} %all-to-all-done), slice={[0:2], [0:64], [0:4096]} | slice | bytes 2097152 | tf_op jit(solution)/shard_map/slice | solution.py:503
  72.4 0.0 collective-permute-start.10
  72.4 0.0 all-to-all-done.1
  72.4 1.1 reduce_sum.61
  73.5 0.1 multiply_reduce_fusion
  73.7 3.4 %convolution_subtract_fusion = f32[3,512]{1,0:T(4,128)S(1)} fusion(bf16[512,4096]{1,0:T(8,128)(2,1)} %bitcast.3.own_ref.refs_0_, bf16[8,4096]{1,0:T(8,128)(2,1)S(1)} %reduce_sum.61, f32[3]{0:T(128)S(1)} %bitcast.20), kind=kOutput, calls=%fused_computation.4 | convolution fusion | flops 12584448 | bytes 4233728 | tf_op jit(solution)/shard_map/dot_general | solution.py:109
  77.1 0.6 fusion.79
  77.7 27.6 %collective-permute-done.11.refs_2_.refs_5_ = bf16[128,4096]{1,0:T(8,128)(2,1)S(1)} collective-permute-done((bf16[128,4096]{1,0:T(8,128)(2,1)}, bf16[128,4096]{1,0:T(8,128)(2,1)S(1)}, u32[]{:S(2)}, u32[]{:S(2)}) %collective-permute-start.11) | collective-permute-done | bytes 1048608 | tf_op jit(solution)/shard_map/ppermute | solution.py:101
  105.4 0.0 collective-permute-start.12
  105.4 2.4 %broadcast_select_fusion.1 = bf16[128,4096]{1,0:T(8,128)(2,1)} fusion(bf16[128,4096]{1,0:T(8,128)(2,1)S(1)} %collective-permute-done.11.refs_2_.refs_5_, pred[]{:T(512)S(6)} %eq.167, bf16[512,4096]{1,0:T(8,128)(2,1)} %bitcast.3.own_ref.refs_0_), kind=kLoop, calls=%fused_computation.7 | loop fusion | flops 524288 | bytes 3145729 | tf_op jit(solution)/shard_map/jit(_where)/select_n | solution.py:507
  107.7 1.2 collective-permute-start.9
  108.9 3.2 %broadcast_select_fusion = bf16[256,4096]{1,0:T(8,128)(2,1)} fusion(bf16[256,4096]{1,0:T(8,128)(2,1)S(1)} %collective-permute-done.6.refs_6_, pred[]{:T(512)S(6)} %eq.167, bf16[512,4096]{1,0:T(8,128)(2,1)} %bitcast.3.own_ref.refs_0_), kind=kLoop, calls=%fused_computation.1 | loop fusion | flops 1048576 | bytes 6291457 | tf_op jit(solution)/shard_map/jit(_where)/select_n | solution.py:507
  112.1 4.3 %collective-permute-done.12 = f32[8,512]{1,0:T(8,128)S(1)} collective-permute-done((f32[8,512]{1,0:T(8,128)S(1)}, f32[8,512]{1,0:T(8,128)S(1)}, u32[]{:S(2)}, u32[]{:S(2)}) %collective-permute-start.12) | collective-permute-done | bytes 16416 | tf_op jit(solution)/shard_map/ppermute | solution.py:101
  116.4 0.0 collective-permute-start.8
  116.4 0.0 collective-permute-done.10.refs_1_.refs_4_
  116.4 2.6 %collective-permute-start.7 = (bf16[256,4096]{1,0:T(8,128)(2,1)}, bf16[256,4096]{1,0:T(8,128)(2,1)}, u32[]{:S(2)}, u32[]{:S(2)}) collective-permute-start(bf16[256,4096]{1,0:T(8,128)(2,1)} %broadcast_select_fusion), channel_id=1, source_target_pairs={{0,2},{1,7},{2,0},{3,5},{4,6},{5,3},{6,4},{7,1},{8,10},{9,15},{10,... | collective-permute-start | bytes 6291464 | tf_op jit(solution)/shard_map/ppermute | solution.py:101
  119.0 2.6 %broadcast_select_fusion.2 = bf16[128,4096]{1,0:T(8,128)(2,1)} fusion(bf16[128,4096]{1,0:T(8,128)(2,1)} %collective-permute-done.10.refs_1_.refs_4_, pred[]{:T(512)S(6)} %eq.167, bf16[2,64,4096]{2,1,0:T(8,128)(2,1)} %slice.63), kind=kLoop, calls=%fused_computation.8 | loop fusion | flops 524288 | bytes 3145729 | tf_op jit(solution)/shard_map/jit(_where)/select_n | solution.py:507
  121.6 0.6 collective-permute-start.14
  122.2 2.2 %collective-permute-start.13 = (bf16[128,4096]{1,0:T(8,128)(2,1)}, bf16[128,4096]{1,0:T(8,128)(2,1)}, u32[]{:S(2)}, u32[]{:S(2)}) collective-permute-start(bf16[128,4096]{1,0:T(8,128)(2,1)} %broadcast_select_fusion.2), channel_id=1, source_target_pairs={{0,2},{1,7},{2,0},{3,5},{4,6},{5,3},{6,4},{7,1},{8,10},{9,15},{10,... | collective-permute-start | bytes 3145736 | tf_op jit(solution)/shard_map/ppermute | solution.py:101
  124.4 1.1 fusion.1.order_ref
  125.5 0.6 stack_broadcast_in_dim.7
  126.2 0.2 stack.24.refs_17_
  126.3 8.9 %shard_map.69 = (f32[8,512]{1,0:T(8,128)S(1)}, f32[8,256]{1,0:T(8,128)S(1)}, f32[3,512,128]{2,1,0:T(8,128)S(1)}, f32[8,128]{1,0:T(8,128)S(1)}) custom-call(bf16[512,4096]{1,0:T(8,128)(2,1)} %bitcast.3.own_ref.refs_0_, bf16[128,4096]{1,0:T(8,128)(2,1)} %collective-permute-done.10.refs_1_.refs_4_, ...), custom_call_target="tpu_custom_call" | custom-call | flops 3221225472 | bytes 6291456 | tf_op jit(solution)/shard_map/pallas_call | solution.py:286
  135.2 0.7 collective-permute-done.2.refs_1_
  135.9 18.2 %collective-permute-done.14.refs_8_ = bf16[128,4096]{1,0:T(8,128)(2,1)} collective-permute-done((bf16[128,4096]{1,0:T(8,128)(2,1)}, bf16[128,4096]{1,0:T(8,128)(2,1)}, u32[]{:S(2)}, u32[]{:S(2)}) %collective-permute-start.14) | collective-permute-done | bytes 1048608 | tf_op jit(solution)/shard_map/ppermute | solution.py:101
  154.0 11.2 %collective-permute-done.13.refs_7_ = bf16[128,4096]{1,0:T(8,128)(2,1)} collective-permute-done((bf16[128,4096]{1,0:T(8,128)(2,1)}, bf16[128,4096]{1,0:T(8,128)(2,1)}, u32[]{:S(2)}, u32[]{:S(2)}) %collective-permute-start.13) | collective-permute-done | bytes 1048608 | tf_op jit(solution)/shard_map/ppermute | solution.py:101
  165.3 0.0 collective-permute-done.5.refs_3_
  165.3 16.1 %shard_map.70 = (f32[8,256]{1,0:T(8,128)S(1)}, f32[8,256]{1,0:T(8,128)S(1)}, f32[3,512,128]{2,1,0:T(8,128)S(1)}, f32[3,512,128]{2,1,0:T(8,128)S(1)}, f32[8,128]{1,0:T(8,128)S(1)}) custom-call(bf16[512,4096]{1,0:T(8,128)(2,1)} %bitcast.3.own_ref.refs_0_, bf16[128,4096]{1,0:T(8,128)(2,1)} %collective-permute-done.2.refs_1_, ...), custom_call_target="tpu_custom_call" | custom-call | flops 5368709120 | bytes 14680064 | tf_op jit(solution)/shard_map/pallas_call | solution.py:286
  181.3 8.8 %shard_map.71 = f32[32,8,128]{2,1,0:T(8,128)} custom-call(bf16[512,4096]{1,0:T(8,128)(2,1)} %bitcast.3.own_ref.refs_0_, bf16[128,4096]{1,0:T(8,128)(2,1)} %collective-permute-done.2.refs_1_, bf16[128,4096]{1,0:T(8,128)(2,1)} %collective-permute-done.4.refs_2_, bf16[256,4096]{1,0:T(8,128)(2,1)} %collective-permute-done.5.refs_3_, ...), custom_call_target="tpu_custom_call" | custom-call | flops 2147483648 | bytes 10485760 | tf_op jit(solution)/shard_map/pallas_call | solution.py:350
  190.2 8.4 %all-to-all-start.2 = ((f32[32,8,128]{2,1,0:T(8,128)}), f32[32,8,128]{2,1,0:T(8,128)S(1)}, u32[]{:S(2)}, u32[]{:S(2)}) async-start(f32[32,8,128]{2,1,0:T(8,128)} %shard_map.71), calls=%async_computation.2 | async-start | bytes 262144 | tf_op jit(solution)/shard_map/all_to_all | solution.py:570
  198.6 0.1 fusion.5
  198.7 0.6 reduce_sum.65
  199.4 0.7 reshape.778.keep_ref
  200.6 0.6 pad_add_fusion.1.where_ref
  201.2 5.9 %all-to-all-done.2.in_ref = f32[32,8,128]{2,1,0:T(8,128)S(1)} async-done(((f32[32,8,128]{2,1,0:T(8,128)}), f32[32,8,128]{2,1,0:T(8,128)S(1)}, u32[]{:S(2)}, u32[]{:S(2)}) %all-to-all-start.2) | async-done | bytes 131104 | tf_op jit(solution)/shard_map/all_to_all | solution.py:570
  207.1 0.6 broadcast_in_dim.54.total_ref
  207.8 0.0 copy-done
  207.8 2.4 %shard_map.72 = (f32[3,512]{1,0:T(4,128)}, f32[1,512]{1,0:T(1,128)}) custom-call(s32[2]{0:T(128)} %pad_add_fusion.1.where_ref, f32[32,8,128]{2,1,0:T(8,128)} %copy-done, f32[512,512]{1,0:T(8,128)} %fusion.1.order_ref, f32[1,512]{1,0:T(1,128)} %reshape.778.keep_ref, f32[1,128]{1,0:T(1,128)} %broadcast_in_dim.54.total_ref), custom_call_target="tpu_custom_call" | custom-call | tf_op jit(solution)/shard_map/pallas_call | solution.py:587
  210.2 1.3 copy.9
  (24 shorter events, 0.2 us)
Async XLA Ops:
  0.6 5.5 %collective-permute-start.1 = (bf16[256,4096]{1,0:T(8,128)(2,1)}, bf16[256,4096]{1,0:T(8,128)(2,1)S(1)}, u32[]{:S(2)}, u32[]{:S(2)}) collective-permute-start(bf16[256,4096]{1,0:T(8,128)(2,1)} %param.5), channel_id=1, source_target_pairs={{0,1},{1,0},{2,3},{3,2},{4,5},{5,4},{6,7},{7,6},{8,9},{9,8},{10,11... | collective-permute-start | bytes 6291464 | tf_op jit(solution)/shard_map/ppermute | solution.py:101
  2.8 3.3 %collective-permute-start = (s32[256]{0:T(256)S(1)}, s32[256]{0:T(256)S(1)}, u32[]{:S(2)}, u32[]{:S(2)}) collective-permute-start(s32[256]{0:T(256)S(1)} %get-tuple-element.42), channel_id=1, source_target_pairs={{0,1},{1,0},{2,3},{3,2},{4,5},{5,4},{6,7},{7,6},{8,9},{9,8},{10,11... | collective-permute-start | bytes 3080 | tf_op jit(solution)/shard_map/ppermute | solution.py:101
  9.4 6.0 %copy-start.2 = (s32[3,1]{0,1:T(1,128)S(1)}, s32[3,1]{0,1:T(1,128)}, u32[]{:S(2)}) copy-start(s32[3,1]{0,1:T(1,128)} %param.9) | copy-start | bytes 40
  9.4 6.1 %copy-start.1 = (s32[1,8,128]{2,1,0:T(8,128)S(1)}, s32[1,8,128]{2,1,0:T(8,128)}, u32[]{:S(2)}) copy-start(s32[1,8,128]{2,1,0:T(8,128)} %param.8) | copy-start | bytes 12292
  9.4 32.4 %all-to-all-start = ((bf16[8,64,4096]{2,1,0:T(8,128)(2,1)}), bf16[8,64,4096]{2,1,0:T(8,128)(2,1)}, u32[]{:S(2)}, u32[]{:S(2)}) async-start(bf16[8,64,4096]{2,1,0:T(8,128)(2,1)} %bitcast.16), calls=%async_computation | async-start | bytes 8388608 | tf_op jit(solution)/shard_map/all_to_all | solution.py:482
  15.6 0.8 collective-permute-start.3
  45.9 26.5 %all-to-all-start.1 = ((bf16[8,8,4096]{2,1,0:T(8,128)(2,1)}), bf16[8,8,4096]{2,1,0:T(8,128)(2,1)}, u32[]{:S(2)}, u32[]{:S(2)}) async-start(bf16[8,8,4096]{2,1,0:T(8,128)(2,1)} %get-tuple-element.20), calls=%async_computation.1 | async-start | bytes 1048576 | tf_op jit(solution)/shard_map/all_to_all | solution.py:512
  64.8 100.5 %collective-permute-start.5 = (bf16[256,4096]{1,0:T(8,128)(2,1)}, bf16[256,4096]{1,0:T(8,128)(2,1)}, u32[]{:S(2)}, u32[]{:S(2)}) collective-permute-start(bf16[256,4096]{1,0:T(8,128)(2,1)} %slice.50), channel_id=1, source_target_pairs={{0,96},{1,25},{2,98},{3,27},{4,100},{5,29},{6,102},{7,31},{8,104},... | collective-permute-start | bytes 6291464 | tf_op jit(solution)/shard_map/ppermute | solution.py:101
  67.4 40.3 %collective-permute-start.6 = (bf16[256,4096]{1,0:T(8,128)(2,1)}, bf16[256,4096]{1,0:T(8,128)(2,1)S(1)}, u32[]{:S(2)}, u32[]{:S(2)}) collective-permute-start(bf16[256,4096]{1,0:T(8,128)(2,1)} %slice.50), channel_id=1, source_target_pairs={{0,32},{1,9},{2,34},{3,11},{4,36},{5,13},{6,38},{7,15},{8,40},{9,1... | collective-permute-start | bytes 6291464 | tf_op jit(solution)/shard_map/ppermute | solution.py:101
  67.4 37.9 %collective-permute-start.11 = (bf16[128,4096]{1,0:T(8,128)(2,1)}, bf16[128,4096]{1,0:T(8,128)(2,1)S(1)}, u32[]{:S(2)}, u32[]{:S(2)}) collective-permute-start(bf16[128,4096]{1,0:T(8,128)(2,1)} %slice.49), channel_id=1, source_target_pairs={{0,32},{1,9},{2,34},{3,11},{4,36},{5,13},{6,38},{7,15},{8,40},{9,1... | collective-permute-start | bytes 3145736 | tf_op jit(solution)/shard_map/ppermute | solution.py:101
  67.7 54.5 %collective-permute-start.4 = (bf16[128,4096]{1,0:T(8,128)(2,1)}, bf16[128,4096]{1,0:T(8,128)(2,1)}, u32[]{:S(2)}, u32[]{:S(2)}) collective-permute-start(bf16[128,4096]{1,0:T(8,128)(2,1)} %slice.49), channel_id=1, source_target_pairs={{0,96},{1,25},{2,98},{3,27},{4,100},{5,29},{6,102},{7,31},{8,104},... | collective-permute-start | bytes 3145736 | tf_op jit(solution)/shard_map/ppermute | solution.py:101
  72.4 44.0 %collective-permute-start.10 = (bf16[128,4096]{1,0:T(8,128)(2,1)}, bf16[128,4096]{1,0:T(8,128)(2,1)}, u32[]{:S(2)}, u32[]{:S(2)}) collective-permute-start(bf16[128,4096]{1,0:T(8,128)(2,1)} %bitcast.4), channel_id=1, source_target_pairs={{0,32},{1,9},{2,34},{3,11},{4,36},{5,13},{6,38},{7,15},{8,40},{9,1... | collective-permute-start | bytes 3145736 | tf_op jit(solution)/shard_map/ppermute | solution.py:101
  105.4 11.0 %collective-permute-start.12 = (f32[8,512]{1,0:T(8,128)S(1)}, f32[8,512]{1,0:T(8,128)S(1)}, u32[]{:S(2)}, u32[]{:S(2)}) collective-permute-start(f32[8,512]{1,0:T(8,128)S(1)} %stack.23.refs_3_.refs_4_.refs_9_.refs_5_), channel_id=1, source_target_pairs={{0,32},{1,9},{2,34},{3,11},{4,36},{5,13},{6,38},{7,15},{8,40},{9,1... | collective-permute-start | bytes 49160 | tf_op jit(solution)/shard_map/ppermute | solution.py:101
  107.7 13.9 %collective-permute-start.9 = (f32[8,512]{1,0:T(8,128)S(1)}, f32[8,512]{1,0:T(8,128)S(1)}, u32[]{:S(2)}, u32[]{:S(2)}) collective-permute-start(f32[8,512]{1,0:T(8,128)S(1)} %stack.23.refs_3_.refs_4_.refs_9_.refs_5_), channel_id=1, source_target_pairs={{0,34},{1,15},{2,0},{3,5},{4,38},{5,11},{6,4},{7,1},{8,42},{9,23},... | collective-permute-start | bytes 49160 | tf_op jit(solution)/shard_map/ppermute | solution.py:101
  116.4 5.2 %collective-permute-start.8 = (f32[8,512]{1,0:T(8,128)S(1)}, f32[8,512]{1,0:T(8,128)S(1)}, u32[]{:S(2)}, u32[]{:S(2)}) collective-permute-start(f32[8,512]{1,0:T(8,128)S(1)} %stack.23.refs_3_.refs_4_.refs_9_.refs_5_), channel_id=1, source_target_pairs={{0,96},{1,25},{2,98},{3,27},{4,100},{5,29},{6,102},{7,31},{8,104},... | collective-permute-start | bytes 49160 | tf_op jit(solution)/shard_map/ppermute | solution.py:101
  116.4 64.9 %collective-permute-start.7 = (bf16[256,4096]{1,0:T(8,128)(2,1)}, bf16[256,4096]{1,0:T(8,128)(2,1)}, u32[]{:S(2)}, u32[]{:S(2)}) collective-permute-start(bf16[256,4096]{1,0:T(8,128)(2,1)} %broadcast_select_fusion), channel_id=1, source_target_pairs={{0,2},{1,7},{2,0},{3,5},{4,6},{5,3},{6,4},{7,1},{8,10},{9,15},{10,... | collective-permute-start | bytes 6291464 | tf_op jit(solution)/shard_map/ppermute | solution.py:101
  121.6 14.3 %collective-permute-start.2 = (bf16[128,4096]{1,0:T(8,128)(2,1)}, bf16[128,4096]{1,0:T(8,128)(2,1)}, u32[]{:S(2)}, u32[]{:S(2)}) collective-permute-start(bf16[128,4096]{1,0:T(8,128)(2,1)} %bitcast.4), channel_id=1, source_target_pairs={{0,96},{1,25},{2,98},{3,27},{4,100},{5,29},{6,102},{7,31},{8,104},... | collective-permute-start | bytes 3145736 | tf_op jit(solution)/shard_map/ppermute | solution.py:101
  121.6 32.4 %collective-permute-start.14 = (bf16[128,4096]{1,0:T(8,128)(2,1)}, bf16[128,4096]{1,0:T(8,128)(2,1)}, u32[]{:S(2)}, u32[]{:S(2)}) collective-permute-start(bf16[128,4096]{1,0:T(8,128)(2,1)} %broadcast_select_fusion.1), channel_id=1, source_target_pairs={{0,2},{1,7},{2,0},{3,5},{4,6},{5,3},{6,4},{7,1},{8,10},{9,15},{10,... | collective-permute-start | bytes 3145736 | tf_op jit(solution)/shard_map/ppermute | solution.py:101
  122.2 43.1 %collective-permute-start.13 = (bf16[128,4096]{1,0:T(8,128)(2,1)}, bf16[128,4096]{1,0:T(8,128)(2,1)}, u32[]{:S(2)}, u32[]{:S(2)}) collective-permute-start(bf16[128,4096]{1,0:T(8,128)(2,1)} %broadcast_select_fusion.2), channel_id=1, source_target_pairs={{0,2},{1,7},{2,0},{3,5},{4,6},{5,3},{6,4},{7,1},{8,10},{9,15},{10,... | collective-permute-start | bytes 3145736 | tf_op jit(solution)/shard_map/ppermute | solution.py:101
  190.2 17.0 %all-to-all-start.2 = ((f32[32,8,128]{2,1,0:T(8,128)}), f32[32,8,128]{2,1,0:T(8,128)S(1)}, u32[]{:S(2)}, u32[]{:S(2)}) async-start(f32[32,8,128]{2,1,0:T(8,128)} %shard_map.71), calls=%async_computation.2 | async-start | bytes 262144 | tf_op jit(solution)/shard_map/all_to_all | solution.py:570
  207.1 0.7 copy-start

commit v3 on v2

--- a/solution.py
+++ b/solution.py
@@ -12,9 +12,7 @@
 F32 = jnp.float32
 BF16 = jnp.bfloat16
 BIG = 1e30
-CHUNKS = (128, 128, 256)
 STEP = 64
-PARTS = 1
 
 
 def dix(x, y, z, c):
@@ -124,31 +122,37 @@
     return high, middle, (rest - middle.astype(F32)).astype(BF16)
 
 
-def pair_work(tasks, q_parts, groups, hbm, note_refs, col_refs, q_buf, u_bufs, x_ref, side_ref, sems):
+def pair_work(side, tasks, q_parts, groups, hbm, note_refs, col_refs, q_buf, u_bufs, x_ref, side_ref, sems):
     copies = {}
     count = 0
-    width = q_buf.shape[1]
-    cuts = [slice(h * width // PARTS, (h + 1) * width // PARTS) for h in range(PARTS)]
     for kind, parts, bufs in (("q", q_parts, [q_buf] * len(q_parts)), ("u", groups, u_bufs)):
         for i, members in enumerate(parts):
             if members is None:
                 continue
             at = i * 512 if kind == "q" else 0
-            for name in members:
-                k = hbm[name].shape[0]
-                for h, cut in enumerate(cuts):
-                    copy = pltpu.make_async_copy(hbm[name].at[:, cut], bufs[i].at[at : at + k, cut], sems.at[count])
-                    copies.setdefault((kind, i, h), []).append(copy)
-                    count += 1
+            for member in members:
+                either = isinstance(member, tuple)
+                k = hbm[member[2] if either else member].shape[0]
+                target = bufs[i].at[at : at + k, :]
+                if either:
+                    one = pltpu.make_async_copy(hbm[member[0]].at[member[1] : member[1] + k, :], target, sems.at[count])
+                    two = pltpu.make_async_copy(hbm[member[2]], target, sems.at[count])
+                    copies.setdefault((kind, i), []).append((one, two))
+                else:
+                    copies.setdefault((kind, i), []).append((pltpu.make_async_copy(hbm[member], target, sems.at[count]),))
+                count += 1
                 at += k
     begun = []
     for g, rows in tasks:
-        for h in range(PARTS):
-            for key in [("u", g, h)] + [("q", q, h) for q, _, _ in rows]:
-                if key in copies and key not in begun:
-                    begun.append(key)
-                    for copy in copies[key]:
-                        copy.start()
+        for key in [("u", g)] + [("q", q) for q, _, _ in rows]:
+            if key in copies and key not in begun:
+                begun.append(key)
+                for copy in copies[key]:
+                    if len(copy) == 1:
+                        copy[0].start()
+                    else:
+                        for choice in (0, 1):
+                            pl.when(side == choice)(copy[choice].start)
     for q in range(len(q_parts)):
         parts = jnp.concatenate([p.astype(F32) for p in split3(note_refs[q][...])], axis=0).astype(BF16)
         along = (iota((24, 512), 0) % 8 == iota((24, 512), 1) // 128).astype(BF16)
@@ -171,19 +175,14 @@
             ]
             for i in range(4)
         ]
-        for h, cut in enumerate(cuts):
-            for key in [("u", g, h)] + [("q", q, h) for q, _, _ in given]:
-                if key in copies and key not in ready:
-                    ready.add(key)
-                    for copy in copies[key]:
-                        copy.wait()
-            part = lax.dot_general(
-                q_buf[lo:hi, cut], data[:m, cut], (((1,), (1,)), ((), ())), preferred_element_type=F32
-            )
-            if h == 0:
-                x_ref[lo:hi, :m] = part
-            else:
-                x_ref[lo:hi, :m] += part
+        for key in [("u", g)] + [("q", q) for q, _, _ in given]:
+            if key in copies and key not in ready:
+                ready.add(key)
+                for copy in copies[key]:
+                    copy[0].wait()
+        x_ref[lo:hi, :m] = lax.dot_general(
+            q_buf[lo:hi], data[:m], (((1,), (1,)), ((), ())), preferred_element_type=F32
+        )
         for q, to_u, to_q in given:
             first_use = to_q and q in fresh
             if to_q:
@@ -232,22 +231,26 @@
     return rows, far
 
 
+def rows_of(part, sizes):
+    return sum(sizes[i[2] if isinstance(i, tuple) else i] for i in part)
+
+
 def scratch_for(q_parts, groups, sizes, width):
     q_bufs = [pltpu.VMEM((512 * len(q_parts), width), BF16)]
-    u_sizes = [sum(sizes[i] for i in p) if p else 0 for p in groups]
+    u_sizes = [rows_of(p, sizes) if p else 0 for p in groups]
     u_bufs = [pltpu.VMEM((n or 16, width), BF16) for n in u_sizes]
     n_copies = sum(len(p) for p in q_parts) + sum(len(p) for p in groups if p)
     most = max([n or 512 for n in u_sizes])
     return q_bufs + u_bufs + [
         pltpu.VMEM((512 * len(q_parts), most), F32),
         pltpu.VMEM((len(q_parts), 4, 512, 128), F32),
-        pltpu.SemaphoreType.DMA((n_copies * PARTS,)),
+        pltpu.SemaphoreType.DMA((n_copies,)),
     ]
 
 
 def cost_of(tasks, q_parts, groups, sizes, width):
     def rows(p):
-        return sum(sizes[i] for i in (p or q_parts[0]))
+        return rows_of(p or q_parts[0], sizes)
 
     flops = sum(2 * 512 * len(t[1]) * rows(groups[t[0]]) * width for t in tasks)
     moved = 2 * width * sum(sizes)
@@ -255,11 +258,12 @@
 
 
 VMEM_SPEC = pl.BlockSpec(memory_space=pltpu.VMEM)
-ANY_SPEC = pl.BlockSpec(memory_space=pl.ANY)
+SMEM_SPEC = pl.BlockSpec(memory_space=pltpu.SMEM)
+ANY_SPEC = pl.BlockSpec(memory_space=pltpu.HBM)
 LIMIT = pltpu.CompilerParams(vmem_limit_bytes=36 * 2**20)
 
 
-def early_kernel(tasks, q_parts, groups, n_hbm, lane_outs, col_outs, *refs):
+def early_kernel(tasks, q_parts, groups, n_hbm, lane_outs, col_outs, side_ref_in, *refs):
     hbm, refs = refs[:n_hbm], refs[n_hbm:]
     n_notes = len(q_parts) + len(groups)
     notes, refs = refs[:n_notes], refs[n_notes:]
@@ -268,7 +272,7 @@
     far_ref, refs = refs[0], refs[1:]
     q_buf, refs = refs[0], refs[1:]
     u_bufs, (x_ref, side_ref, sems) = refs[: len(groups)], refs[len(groups) :]
-    rows, far = pair_work(tasks, q_parts, groups, hbm, notes, cols, q_buf, u_bufs, x_ref, side_ref, sems)
+    rows, far = pair_work(side_ref_in[0], tasks, q_parts, groups, hbm, notes, cols, q_buf, u_bufs, x_ref, side_ref, sems)
     for g, ref in zip(lane_outs, lane_refs):
         ref[...] = jnp.zeros_like(ref)
         for j in range(3):
@@ -276,7 +280,7 @@
     far_ref[...] = far
 
 
-def early_pairs(hbm, q_parts, groups, notes, tasks):
+def early_pairs(edge, hbm, q_parts, groups, notes, tasks):
     sizes, width = [h.shape[0] for h in hbm], hbm[0].shape[1]
     lane_outs = [t[0] for t in tasks if any(v[1] for v in t[1])]
     col_outs = [q for q in range(len(q_parts)) if any(v[0] == q and v[2] for t in tasks for v in t[1])]
@@ -286,17 +290,17 @@
     out = pl.pallas_call(
         functools.partial(early_kernel, tasks, q_parts, groups, len(hbm), lane_outs, col_outs),
         out_shape=shapes,
-        in_specs=[ANY_SPEC] * len(hbm) + [VMEM_SPEC] * len(notes),
+        in_specs=[SMEM_SPEC] + [ANY_SPEC] * len(hbm) + [VMEM_SPEC] * len(notes),
         out_specs=[VMEM_SPEC] * len(shapes),
         scratch_shapes=scratch_for(q_parts, groups, sizes, width),
         cost_estimate=cost_of(tasks, q_parts, groups, sizes, width),
         compiler_params=LIMIT,
-    )(*hbm, *notes)
+    )(edge.reshape(1), *hbm, *notes)
     n = len(lane_outs)
     return dict(zip(lane_outs, out)), dict(zip(col_outs, out[n:])), out[-1]
 
 
-def last_kernel(tasks, q_parts, groups, n_hbm, lane_rows, n_cols, n_far, own_rows, *refs):
+def last_kernel(tasks, q_parts, groups, n_hbm, lane_rows, n_cols, n_far, own_rows, side_ref_in, *refs):
     hbm, refs = refs[:n_hbm], refs[n_hbm:]
     n_notes = len(q_parts) + len(groups)
     notes, refs = refs[:n_notes], refs[n_notes:]
@@ -308,7 +312,7 @@
     u_bufs, refs = refs[: len(groups)], refs[len(groups) :]
     x_ref, side_ref, sems, col0_ref, col1_ref, g_ref = refs
     cols = {0: col0_ref, 1: col1_ref}
-    rows, far = pair_work(tasks, q_parts, groups, hbm, notes, cols, q_buf, u_bufs, x_ref, side_ref, sems)
+    rows, far = pair_work(side_ref_in[0], tasks, q_parts, groups, hbm, notes, cols, q_buf, u_bufs, x_ref, side_ref, sems)
     g_ref[...] = extra_ref[...]
     for ref, (row, at) in zip(lane_refs, lane_rows):
         m = ref.shape[1]
@@ -343,7 +347,7 @@
             out_ref[m * 4 + copy] = page
 
 
-def last_pairs(hbm, q_parts, groups, notes, tasks, lanes, lane_rows, cols, fars, own_rows, extra):
+def last_pairs(edge, hbm, q_parts, groups, notes, tasks, lanes, lane_rows, cols, fars, own_rows, extra):
     sizes, width = [h.shape[0] for h in hbm], hbm[0].shape[1]
     n_cols = tuple(len(c) for c in cols)
     small = lanes + [c for each in cols for c in each] + fars + [extra]
@@ -352,16 +356,17 @@
             last_kernel, tasks, q_parts, groups, len(hbm), lane_rows, n_cols, len(fars), own_rows
         ),
         out_shape=jax.ShapeDtypeStruct((32, 8, 128), F32),
-        in_specs=[ANY_SPEC] * len(hbm) + [VMEM_SPEC] * (len(notes) + len(small)),
+        in_specs=[SMEM_SPEC] + [ANY_SPEC] * len(hbm) + [VMEM_SPEC] * (len(notes) + len(small)),
         out_specs=VMEM_SPEC,
         scratch_shapes=scratch_for(q_parts, groups, sizes, width)
         + [pltpu.VMEM((3, 512, 128), F32), pltpu.VMEM((3, 512, 128), F32), pltpu.VMEM((16, 512), F32)],
         cost_estimate=cost_of(tasks, q_parts, groups, sizes, width),
         compiler_params=LIMIT,
-    )(*hbm, *notes, *small)
-
-
-def prep_kernel(own_ref, hit_ref, found_ref, half_ref, buf, part, sems):
+    )(edge.reshape(1), *hbm, *notes, *small)
+
+
+def prep_kernel(pieces, own_ref, hit_ref, found_ref, half_ref, *refs):
+    piece_refs, (buf, part, sems) = refs[: len(pieces)], refs[len(pieces) :]
     slab = 128
     n = buf.shape[0] // slab
     copies = [
@@ -370,8 +375,15 @@
     ]
     for copy in copies:
         copy.start()
+    out = [
+        pltpu.make_async_copy(buf.at[lo:hi, :], ref, sems.at[n + i])
+        for i, ((lo, hi), ref) in enumerate(zip(pieces, piece_refs))
+    ]
     for i, copy in enumerate(copies):
         copy.wait()
+        for each, (lo, hi) in zip(out, pieces):
+            if hi == i * slab + slab:
+                each.start()
 
         def step(k, _, i=i):
             rows = pl.ds(pl.multiple_of(i * slab + k * 16, 16), 16)
@@ -387,16 +399,23 @@
     found = jnp.dot(hit_ref[...], buf[...], preferred_element_type=F32).astype(BF16)
     for i in range(8):
         found_ref[i] = found
-
-
-def prepare(own, hit):
+    for each in out:
+        each.wait()
+
+
+def prepare(own, hit, pieces):
     width = own.shape[1]
     return pl.pallas_call(
-        prep_kernel,
-        out_shape=[jax.ShapeDtypeStruct((8, 8, width), BF16), jax.ShapeDtypeStruct((1, 512), F32)],
+        functools.partial(prep_kernel, pieces),
+        out_shape=[jax.ShapeDtypeStruct((8, 8, width), BF16), jax.ShapeDtypeStruct((1, 512), F32)]
+        + [jax.ShapeDtypeStruct((hi - lo, width), BF16) for lo, hi in pieces],
         in_specs=[ANY_SPEC, VMEM_SPEC],
-        out_specs=[VMEM_SPEC, VMEM_SPEC],
-        scratch_shapes=[pltpu.VMEM((512, width), BF16), pltpu.VMEM((512, 128), F32), pltpu.SemaphoreType.DMA((4,))],
+        out_specs=[VMEM_SPEC, VMEM_SPEC] + [ANY_SPEC] * len(pieces),
+        scratch_shapes=[
+            pltpu.VMEM((512, width), BF16),
+            pltpu.VMEM((512, 128), F32),
+            pltpu.SemaphoreType.DMA((4 + len(pieces),)),
+        ],
         cost_estimate=pl.CostEstimate(flops=2 * 512 * 512 * width, transcendentals=0, bytes_accessed=own.size * 2),
         compiler_params=LIMIT,
     )(own, hit)
@@ -430,8 +449,9 @@
     keep = keep_ref[...]
     total = total_ref[:, 0:1]
     scale = 1.0 / width
-    gain_ref[0:1, :] = (2.0 * final[0:1] + total * far - 2.0 * half_sum) * scale * keep / total
-    gain_ref[1:3, :] = 2.0 * final[1:3] * scale * keep / total
+    gain_ref[0] = (2.0 * final[0:1] + total * far - 2.0 * half_sum) * scale * keep / total
+    gain_ref[1] = 2.0 * final[1:2] * scale * keep / total
+    gain_ref[2] = 2.0 * final[2:3] * scale * keep / total
     cover_ref[...] = keep * (far - 2.0 * final[3:4]) * scale
 
 
@@ -492,24 +512,16 @@
     valid = slot[0].astype(F32) < seen
     n_valid = jnp.sum(host_counts)
     hit = (place == jnp.concatenate([picks, -jnp.ones((5,), jnp.int32)])[:, None]).astype(BF16)
-    found, half = prepare(own, hit)
+    found, half, *cuts = prepare(own, hit, tuple((i, i + 128) for i in range(0, 512, 128)))
     half = half[0]
-    edges = [0]
-    for size in CHUNKS:
-        edges.append(edges[-1] + size)
-    spans = list(zip(edges, edges[1:]))
-    l, f = [], []
-    late, found = lax.optimization_barrier((own, found))
-    cuts = [(late if lo else own)[lo:hi] for lo, hi in spans]
-    for cut in cuts:
-        l.append(send(cut, UP))
-    for i, cut in enumerate(cuts):
-        f.append(send(jnp.where(edge == 0, l[i], cut), ACROSS))
-    r = []
-    for cut in cuts:
-        r.append(send(cut, DOWN))
+
+    l = [send(v, UP) for v in cuts]
+    relays = [jnp.where(edge == 0, v, cut) for v, cut in zip(l, cuts)]
+    f = [send(v, ACROSS) for v in relays]
+    r = send(own, DOWN)
 
     found = lax.all_to_all(found, AX, 0, 0, axis_index_groups=class_groups(), tiled=True)
+    found, _ = lax.optimization_barrier((found, relays[0]))
     found = jnp.sum(found.astype(F32), axis=0).astype(BF16)
     to_picks = inner(found, own)
     pick_half = 0.5 * jnp.sum(jnp.square(found.astype(F32)), axis=1)
@@ -525,22 +537,29 @@
     info_r = send(info, DOWN)
     info_f = send(info, FOURTH)
 
-    mid = edges[2]
+    mid = 256
     l_low, l_high = info_l[:, :mid], info_l[:, mid:]
     f_low, f_high = info_f[:, :mid], info_f[:, mid:]
-    lanes_a, cols_a, far_a = early_pairs(
-        [own, l[0], l[1]],
+    lanes_1, _, far_1 = early_pairs(edge, [own], [[0]], [None], [info, info], [(0, [(0, True, False)])])
+    lanes_2, cols_2, far_2 = early_pairs(
+        edge,
+        [own, l[0], l[1], f[0], f[1]],
         [[0]],
-        [None, [1, 2]],
-        [info, info, l_low],
-        [(0, [(0, True, False)]), (1, [(0, True, True)])],
-    )
-    lanes_b, cols_b, far_b = early_pairs(
-        [own, *r, *l, f[0], f[1]],
-        [[0], [1, 2, 3]],
-        [[7, 8], [6], [4, 5]],
+        [[1, 2], [3, 4]],
+        [info, l_low, f_low],
+        [(0, [(0, True, True)]), (1, [(0, True, True)])],
+    )
+    lanes_3, cols_3, far_3 = early_pairs(
+        edge,
+        [own, r, *l, f[0], f[1]],
+        [[0], [1]],
+        [[6, 7], [4, 5], [2, 3]],
         [info, info_r, f_low, l_high, l_low],
-        [(0, [(0, True, True), (1, True, True)]), (1, [(0, True, True), (1, False, True)]), (2, [(1, False, True)])],
+        [
+            (2, [(1, False, True)]),
+            (0, [(1, True, True)]),
+            (1, [(0, True, True), (1, False, True)]),
+        ],
     )
     none = jnp.zeros((512,), F32)
     extra = [none] * 16
@@ -549,21 +568,23 @@
     extra[11] = jnp.broadcast_to(jnp.sum(half), (512,))
     extra = jnp.stack(extra)
     lane_list = [
-        (lanes_a[0], (0, 0)),
-        (lanes_a[1], (4, 0)),
-        (lanes_b[0], (12, 0)),
-        (lanes_b[1], (4, mid)),
+        (lanes_1[0], (0, 0)),
+        (lanes_2[0], (4, 0)),
+        (lanes_2[1], (12, 0)),
+        (lanes_3[0], (12, 0)),
+        (lanes_3[1], (4, mid)),
     ]
     outbox = last_pairs(
-        [own, *r, f[2]],
-        [[0], [1, 2, 3]],
-        [[4]],
+        edge,
+        [own, r, f[2], f[3]],
+        [[0], [1]],
+        [[2, 3]],
         [info, info_r, f_high],
         [(0, [(0, True, True), (1, True, True)])],
         [v for v, _ in lane_list],
         [at for _, at in lane_list],
-        [[cols_a[0], cols_b[0]], [cols_b[1]]],
-        [far_a, far_b],
+        [[cols_2[0], cols_3[0]], [cols_3[1]]],
+        [far_1, far_2, far_3],
         {0: (12, mid)},
         extra,
     )
@@ -586,11 +607,11 @@
     where = jnp.stack([host, jnp.where(first, 8, 2)])
     gains, cover = pl.pallas_call(
         functools.partial(close_kernel, width),
-        out_shape=[jax.ShapeDtypeStruct((3, 512), F32), jax.ShapeDtypeStruct((1, 512), F32)],
+        out_shape=[jax.ShapeDtypeStruct((3, 1, 512), F32), jax.ShapeDtypeStruct((1, 512), F32)],
         in_specs=[pl.BlockSpec(memory_space=pltpu.SMEM)] + [VMEM_SPEC] * 4,
         out_specs=[VMEM_SPEC, VMEM_SPEC],
     )(where, inbox, in_order, keep, total)
-    return (gains[:, None, :], cover)
+    return (gains, cover)
 
 
 def solution(mesh):

time: 212 us -> 187 us (0.88)
  waiting for transfers between devices: 93.5 us -> 70.6 us
  starting transfers between devices: 40.3 us -> 49.4 us
  local copies, waits for them, and re-layouts: 11.4 us -> 2.37 us
    ppermute x15, waiting for transfers between devices: 62.3 us -> 5.17 us  [send(): return lax.ppermute(value, AX, pairs)]
    all_to_all x1, waiting for transfers between devices: 0.01 us -> 34.2 us  [body(): lax.all_to_all(found, AX, 0, 0, axis_index_groups=class_groups(), tiled=T...]
    ppermute x15, starting transfers between devices: 14.1 us -> 28.2 us  [send(): return lax.ppermute(value, AX, pairs)]
    slice x3 -> x0, local copies, waits for them, and re-layouts: 7.75 us -> none  [body(): cuts = [(late if lo else own)[lo:hi] for lo, hi in spans]]
    all_to_all x1, starting transfers between devices: 11.8 us -> 7.04 us  [body(): lax.all_to_all(found, AX, 0, 0, axis_index_groups=class_groups(), tiled=T...]
    pallas_call x2 -> x3, Pallas kernels: 24.9 us -> 23.5 us  [early_pairs(): pl.pallas_call(functools.partial(early_kernel, tasks, q_parts, groups, le...]
    select_n x3 -> x4, other arithmetic: 8.21 us -> 6.92 us  [body(): relays = [jnp.where(edge == 0, v, cut) for v, cut in zip(l, cuts)]]
  transfers between devices with their start and end apart: 18 -> 18, of which waited for: 8 -> 6; matrix products, arithmetic and copies ran while one was open for 14% -> 11% of each run, Pallas kernels for 12% -> 13%
where the time goes in v3:
time: 187 us; the launch traced here: 186 us
  waiting for transfers between devices  70.6 us (38%)
  starting transfers between devices  49.4 us (26%)
  Pallas kernels  38.6 us (21%)
  other arithmetic  12.9 us (7%)
  matrix products  9.9 us (5%)
  local copies, waits for them, and re-layouts  2.37 us (1%)
  between operations  2.12 us (1%)
    all_to_all x1, waiting for transfers between devices, body(): lax.all_to_all(found, AX, 0, 0, axis_index_groups=class_groups(), tiled=T...  34.2 us
    ppermute x15, starting transfers between devices, send(): return lax.ppermute(value, AX, pairs)  28.2 us
    all_to_all x1, waiting for transfers between devices, body(): lax.all_to_all(outgoing.reshape(8, 64, width), AX, 0, 0, axis_index_group...  25.3 us
    pallas_call x3, Pallas kernels, early_pairs(): pl.pallas_call(functools.partial(early_kernel, tasks, q_parts, groups, le...  23.5 us
    pallas_call x1, Pallas kernels, last_pairs(): pl.pallas_call(functools.partial(last_kernel, tasks, q_parts, groups, len...  8.37 us
    all_to_all x1, starting transfers between devices, body(): lax.all_to_all(outbox, AX, 0, 0, axis_index_groups=final_groups(), tiled=...  8.21 us
    all_to_all x1, starting transfers between devices, body(): lax.all_to_all(found, AX, 0, 0, axis_index_groups=class_groups(), tiled=T...  7.04 us
    select_n x4, other arithmetic, body(): relays = [jnp.where(edge == 0, v, cut) for v, cut in zip(l, cuts)]  6.92 us
  transfers between devices with their start and end apart: 18, of which 6 were waited for; matrix products, arithmetic and copies ran while one was open for 11% of the time, Pallas kernels for 13%

profile of v3, /device:TPU:1, one launch (start us, length us, event | category | flops | bytes accessed | tf_op | source)
XLA Modules:
  0.0 185.9 jit_solution(8944397799797181089)
XLA Ops:
  0.6 1.5 collective-permute-start.1
  2.1 0.7 broadcast_select_fusion.7
  2.8 0.1 collective-permute-start
  2.9 2.8 %fusion.2 = f32[512,4096]{1,0:T(8,128)S(1)} fusion(bf16[256,4096]{1,0:T(8,128)(2,1)} %param.5, s32[256]{0:T(256)S(1)} %broadcast_select_fusion.6), kind=kOutput, calls=%fused_computation.12 | convolution fusion | flops 1073872896 | bytes 10486784 | tf_op jit(solution)/shard_map/dot_general | solution.py:499
  5.8 0.3 collective-permute-done
  6.1 0.0 collective-permute-done.1
  6.1 3.4 %add_convert_fusion = bf16[512,4096]{1,0:T(8,128)(2,1)} fusion(f32[512,4096]{1,0:T(8,128)S(1)} %fusion.2, bf16[256,4096]{1,0:T(8,128)(2,1)S(1)} %collective-permute-done.1, s32[256]{0:T(256)S(1)} %collective-permute-done), kind=kOutput, calls=%fused_computation | convolution fusion | flops 1078067200 | bytes 14681088 | tf_op jit(solution)/shard_map/dot_general | solution.py:500
  9.4 6.0 %all-to-all-start = ((bf16[8,64,4096]{2,1,0:T(8,128)(2,1)}), bf16[8,64,4096]{2,1,0:T(8,128)(2,1)}, u32[]{:S(2)}, u32[]{:S(2)}) async-start(bf16[8,64,4096]{2,1,0:T(8,128)(2,1)} %bitcast.14), calls=%async_computation | async-start | bytes 8388608 | tf_op jit(solution)/shard_map/all_to_all | solution.py:502
  15.4 0.1 pad.2.clone
  15.5 0.1 pad_add_fusion
  15.6 0.7 collective-permute-start.3
  16.3 0.0 collective-permute-done.3
  16.4 0.1 slice_reduce_fusion
  16.5 0.1 compare_convert_fusion.hit_ref
  16.6 25.3 %all-to-all-done = bf16[8,64,4096]{2,1,0:T(8,128)(2,1)} async-done(((bf16[8,64,4096]{2,1,0:T(8,128)(2,1)}), bf16[8,64,4096]{2,1,0:T(8,128)(2,1)}, u32[]{:S(2)}, u32[]{:S(2)}) %all-to-all-start) | async-done | bytes 4194336 | tf_op jit(solution)/shard_map/all_to_all | solution.py:502
  41.8 4.2 %shard_map.68 = (bf16[8,8,4096]{2,1,0:T(8,128)(2,1)}, f32[1,512]{1,0:T(1,128)S(1)}, bf16[128,4096]{1,0:T(8,128)(2,1)S(1)}, bf16[128,4096]{1,0:T(8,128)(2,1)}, bf...) custom-call(bf16[512,4096]{1,0:T(8,128)(2,1)} %bitcast.4.own_ref.refs_0_, bf16[8,512]{1,0:T(8,128)(2,1)S(1)} %compare_convert_fusion.hit_ref), custom_call_target="tpu_custom_call" | custom-call | flops 2147483648 | bytes 4194304 | tf_op jit(solution)/shard_map/pallas_call | solution.py:408
  46.1 6.6 %collective-permute-start.8 = (bf16[128,4096]{1,0:T(8,128)(2,1)S(1)}, bf16[128,4096]{1,0:T(8,128)(2,1)S(1)}, u32[]{:S(2)}, u32[]{:S(2)}) collective-permute-start(bf16[128,4096]{1,0:T(8,128)(2,1)S(1)} %get-tuple-element.24), channel_id=1, source_target_pairs={{0,32},{1,9},{2,34},{3,11},{4,36},{5,13},{6,38},{7,15},{8,40},{9,1... | collective-permute-start | bytes 3145736 | tf_op jit(solution)/shard_map/ppermute | solution.py:99
  52.8 1.2 fusion.1.order_ref
  54.0 0.6 fusion.12
  55.2 0.3 fusion
  55.6 0.1 collective-permute-start.2
  55.7 7.0 %all-to-all-start.1 = ((bf16[8,8,4096]{2,1,0:T(8,128)(2,1)}), bf16[8,8,4096]{2,1,0:T(8,128)(2,1)}, u32[]{:S(2)}, u32[]{:S(2)}) async-start(bf16[8,8,4096]{2,1,0:T(8,128)(2,1)} %get-tuple-element.23), calls=%async_computation.1 | async-start | bytes 1048576 | tf_op jit(solution)/shard_map/all_to_all | solution.py:523
  62.7 1.5 collective-permute-start.11
  64.2 1.2 collective-permute-start.4
  65.3 0.9 collective-permute-start.6
  66.2 0.0 collective-permute-done.8.refs_1_.refs_2_
  66.2 1.1 broadcast_select_fusion.1
  67.4 3.8 %collective-permute-start.12 = (bf16[128,4096]{1,0:T(8,128)(2,1)}, bf16[128,4096]{1,0:T(8,128)(2,1)S(1)}, u32[]{:S(2)}, u32[]{:S(2)}) collective-permute-start(bf16[128,4096]{1,0:T(8,128)(2,1)} %broadcast_select_fusion.1), channel_id=1, source_target_pairs={{0,2},{1,7},{2,0},{3,5},{4,6},{5,3},{6,4},{7,1},{8,10},{9,15},{10,... | collective-permute-start | bytes 3145736 | tf_op jit(solution)/shard_map/ppermute | solution.py:99
  71.2 34.2 %all-to-all-done.1 = bf16[8,8,4096]{2,1,0:T(8,128)(2,1)} async-done(((bf16[8,8,4096]{2,1,0:T(8,128)(2,1)}), bf16[8,8,4096]{2,1,0:T(8,128)(2,1)}, u32[]{:S(2)}, u32[]{:S(2)}) %all-to-all-start.1) | async-done | bytes 524320 | tf_op jit(solution)/shard_map/all_to_all | solution.py:523
  105.4 1.1 reduce_sum.61
  106.5 0.1 multiply_reduce_fusion
  106.7 3.4 %convolution_subtract_fusion = f32[3,512]{1,0:T(4,128)S(1)} fusion(bf16[512,4096]{1,0:T(8,128)(2,1)} %bitcast.4.own_ref.refs_0_, bf16[8,4096]{1,0:T(8,128)(2,1)S(1)} %reduce_sum.61, f32[3]{0:T(128)S(1)} %bitcast.17), kind=kOutput, calls=%fused_computation.3 | convolution fusion | flops 12584448 | bytes 4233728 | tf_op jit(solution)/shard_map/dot_general | solution.py:107
  110.1 0.6 fusion.79
  110.7 0.0 collective-permute-done.11.refs_2_.refs_3_
  110.7 0.8 collective-permute-start.14
  111.6 1.1 broadcast_select_fusion
  112.7 0.0 collective-permute-done.6.refs_5_
  112.7 5.2 %collective-permute-start.10 = (f32[8,512]{1,0:T(8,128)S(1)}, f32[8,512]{1,0:T(8,128)S(1)}, u32[]{:S(2)}, u32[]{:S(2)}) collective-permute-start(f32[8,512]{1,0:T(8,128)S(1)} %stack.23.refs_1_.refs_2_.refs_5_.refs_8_.refs_4_), channel_id=1, source_target_pairs={{0,34},{1,15},{2,0},{3,5},{4,38},{5,11},{6,4},{7,1},{8,42},{9,23},... | collective-permute-start | bytes 49160 | tf_op jit(solution)/shard_map/ppermute | solution.py:99
  117.8 2.3 %broadcast_select_fusion.2 = bf16[128,4096]{1,0:T(8,128)(2,1)} fusion(bf16[128,4096]{1,0:T(8,128)(2,1)} %collective-permute-done.6.refs_5_, bf16[128,4096]{1,0:T(8,128)(2,1)} %get-tuple-element.21, pred[]{:T(512)S(6)} %eq.162), kind=kLoop, calls=%fused_computation.8 | loop fusion | flops 524288 | bytes 3145729 | tf_op jit(solution)/shard_map/jit(_where)/select_n | solution.py:519
  120.2 0.3 collective-permute-start.13
  120.4 2.4 %broadcast_select_fusion.3 = bf16[128,4096]{1,0:T(8,128)(2,1)} fusion(bf16[128,4096]{1,0:T(8,128)(2,1)} %collective-permute-done.4.refs_4_, bf16[128,4096]{1,0:T(8,128)(2,1)} %get-tuple-element.20, pred[]{:T(512)S(6)} %eq.162), kind=kLoop, calls=%fused_computation.9 | loop fusion | flops 524288 | bytes 3145729 | tf_op jit(solution)/shard_map/jit(_where)/select_n | solution.py:519
  122.8 5.0 %shard_map.69 = (f32[8,512]{1,0:T(8,128)S(1)}, f32[8,128]{1,0:T(8,128)S(1)}) custom-call(s32[1]{0:T(128)} %bitcast.2.side_ref_in, bf16[512,4096]{1,0:T(8,128)(2,1)} %bitcast.4.own_ref.refs_0_, f32[8,512]{1,0:T(8,128)S(1)} %stack.23.refs_1_.refs_2_.refs_5_.refs_8_.refs_4_, f32[8,512]{1,0:T(8,128)S(1)} %stack.23.refs_1_.refs_2_.refs_5_.refs_8_.refs_4_), custom_call_target="tpu_custom_call" | custom-call | flops 2147483648 | bytes 4194304 | tf_op jit(solution)/shard_map/pallas_call | solution.py:290
  127.9 0.6 stack_broadcast_in_dim.7
  128.6 0.1 stack.24.refs_18_
  128.7 2.7 %collective-permute-start.7 = (bf16[128,4096]{1,0:T(8,128)(2,1)}, bf16[128,4096]{1,0:T(8,128)(2,1)S(1)}, u32[]{:S(2)}, u32[]{:S(2)}) collective-permute-start(bf16[128,4096]{1,0:T(8,128)(2,1)} %broadcast_select_fusion.2), channel_id=1, source_target_pairs={{0,2},{1,7},{2,0},{3,5},{4,6},{5,3},{6,4},{7,1},{8,10},{9,15},{10,... | collective-permute-start | bytes 3145736 | tf_op jit(solution)/shard_map/ppermute | solution.py:99
  131.4 0.3 collective-permute-start.5
  131.7 3.7 %collective-permute-done.13.refs_4_.refs_7_ = bf16[128,4096]{1,0:T(8,128)(2,1)} collective-permute-done((bf16[128,4096]{1,0:T(8,128)(2,1)}, bf16[128,4096]{1,0:T(8,128)(2,1)}, u32[]{:S(2)}, u32[]{:S(2)}) %collective-permute-start.13) | collective-permute-done | bytes 1048608 | tf_op jit(solution)/shard_map/ppermute | solution.py:99
  135.3 2.7 %collective-permute-start.9 = (f32[8,512]{1,0:T(8,128)S(1)}, f32[8,512]{1,0:T(8,128)S(1)}, u32[]{:S(2)}, u32[]{:S(2)}) collective-permute-start(f32[8,512]{1,0:T(8,128)S(1)} %stack.23.refs_1_.refs_2_.refs_5_.refs_8_.refs_4_), channel_id=1, source_target_pairs={{0,96},{1,25},{2,98},{3,27},{4,100},{5,29},{6,102},{7,31},{8,104},... | collective-permute-start | bytes 49160 | tf_op jit(solution)/shard_map/ppermute | solution.py:99
  138.0 0.0 collective-permute-done.12.refs_3_.refs_6_
  138.0 7.8 %shard_map.70 = (f32[8,256]{1,0:T(8,128)S(1)}, f32[8,256]{1,0:T(8,128)S(1)}, f32[3,512,128]{2,1,0:T(8,128)S(1)}, f32[8,128]{1,0:T(8,128)S(1)}) custom-call(s32[1]{0:T(128)} %bitcast.2.side_ref_in, bf16[512,4096]{1,0:T(8,128)(2,1)} %bitcast.4.own_ref.refs_0_, bf16[128,4096]{1,0:T(8,128)(2,1)S(1)} %collective-permute-done.8.refs_1_.refs_2_, ...), custom_call_target="tpu_custom_call" | custom-call | flops 2147483648 | bytes 8388608 | tf_op jit(solution)/shard_map/pallas_call | solution.py:290
  145.8 0.0 collective-permute-done.9.refs_9_.refs_5_
  145.8 0.0 collective-permute-done.2.refs_1_
  145.9 10.7 %shard_map.71 = (f32[8,256]{1,0:T(8,128)S(1)}, f32[8,256]{1,0:T(8,128)S(1)}, f32[3,512,128]{2,1,0:T(8,128)S(1)}, f32[3,512,128]{2,1,0:T(8,128)S(1)}, f32[8,128]{1,0:T(8,128)S(1)}) custom-call(s32[1]{0:T(128)} %bitcast.2.side_ref_in, bf16[512,4096]{1,0:T(8,128)(2,1)} %bitcast.4.own_ref.refs_0_, bf16[512,4096]{1,0:T(8,128)(2,1)} %collective-permute-done.2.refs_1_, ...), custom_call_target="tpu_custom_call" | custom-call | flops 4294967296 | bytes 14680064 | tf_op jit(solution)/shard_map/pallas_call | solution.py:290
  156.5 1.2 collective-permute-done.5.refs_2_
  157.7 8.4 %shard_map.72 = f32[32,8,128]{2,1,0:T(8,128)} custom-call(s32[1]{0:T(128)} %bitcast.2.side_ref_in, bf16[512,4096]{1,0:T(8,128)(2,1)} %bitcast.4.own_ref.refs_0_, bf16[512,4096]{1,0:T(8,128)(2,1)} %collective-permute-done.2.refs_1_, bf16[128,4096]{1,0:T(8,128)(2,1)S(1)} %collective-permute-done.5.refs_2_, ...), custom_call_target="tpu_custom_call" | custom-call | flops 2147483648 | bytes 10485760 | tf_op jit(solution)/shard_map/pallas_call | solution.py:354
  166.1 8.2 %all-to-all-start.2 = ((f32[32,8,128]{2,1,0:T(8,128)}), f32[32,8,128]{2,1,0:T(8,128)S(1)}, u32[]{:S(2)}, u32[]{:S(2)}) async-start(f32[32,8,128]{2,1,0:T(8,128)} %shard_map.72), calls=%async_computation.2 | async-start | bytes 262144 | tf_op jit(solution)/shard_map/all_to_all | solution.py:591
  174.3 0.1 fusion.5
  174.4 0.6 reduce_sum.65
  175.0 0.7 reshape.784.keep_ref
  176.3 0.6 pad_add_fusion.1.where_ref
  176.9 5.9 %all-to-all-done.2.in_ref = f32[32,8,128]{2,1,0:T(8,128)S(1)} async-done(((f32[32,8,128]{2,1,0:T(8,128)}), f32[32,8,128]{2,1,0:T(8,128)S(1)}, u32[]{:S(2)}, u32[]{:S(2)}) %all-to-all-start.2) | async-done | bytes 131104 | tf_op jit(solution)/shard_map/all_to_all | solution.py:591
  182.8 0.6 broadcast_in_dim.51.total_ref
  183.4 0.0 copy-done
  183.5 2.4 %shard_map.73 = (f32[3,1,512]{2,1,0:T(1,128)}, f32[1,512]{1,0:T(1,128)}) custom-call(s32[2]{0:T(128)} %pad_add_fusion.1.where_ref, f32[32,8,128]{2,1,0:T(8,128)} %copy-done, f32[512,512]{1,0:T(8,128)} %fusion.1.order_ref, f32[1,512]{1,0:T(1,128)} %reshape.784.keep_ref, f32[1,128]{1,0:T(1,128)} %broadcast_in_dim.51.total_ref), custom_call_target="tpu_custom_call" | custom-call | tf_op jit(solution)/shard_map/pallas_call | solution.py:608
  (22 shorter events, 0.2 us)
Async XLA Ops:
  0.6 5.5 %collective-permute-start.1 = (bf16[256,4096]{1,0:T(8,128)(2,1)}, bf16[256,4096]{1,0:T(8,128)(2,1)S(1)}, u32[]{:S(2)}, u32[]{:S(2)}) collective-permute-start(bf16[256,4096]{1,0:T(8,128)(2,1)} %param.5), channel_id=1, source_target_pairs={{0,1},{1,0},{2,3},{3,2},{4,5},{5,4},{6,7},{7,6},{8,9},{9,8},{10,11... | collective-permute-start | bytes 6291464 | tf_op jit(solution)/shard_map/ppermute | solution.py:99
  2.8 3.3 %collective-permute-start = (s32[256]{0:T(256)S(1)}, s32[256]{0:T(256)S(1)}, u32[]{:S(2)}, u32[]{:S(2)}) collective-permute-start(s32[256]{0:T(256)S(1)} %get-tuple-element.42), channel_id=1, source_target_pairs={{0,1},{1,0},{2,3},{3,2},{4,5},{5,4},{6,7},{7,6},{8,9},{9,8},{10,11... | collective-permute-start | bytes 3080 | tf_op jit(solution)/shard_map/ppermute | solution.py:99
  9.4 6.0 %copy-start.2 = (s32[3,1]{0,1:T(1,128)S(1)}, s32[3,1]{0,1:T(1,128)}, u32[]{:S(2)}) copy-start(s32[3,1]{0,1:T(1,128)} %param.9) | copy-start | bytes 40
  9.4 6.1 %copy-start.1 = (s32[1,8,128]{2,1,0:T(8,128)S(1)}, s32[1,8,128]{2,1,0:T(8,128)}, u32[]{:S(2)}) copy-start(s32[1,8,128]{2,1,0:T(8,128)} %param.8) | copy-start | bytes 12292
  9.4 32.4 %all-to-all-start = ((bf16[8,64,4096]{2,1,0:T(8,128)(2,1)}), bf16[8,64,4096]{2,1,0:T(8,128)(2,1)}, u32[]{:S(2)}, u32[]{:S(2)}) async-start(bf16[8,64,4096]{2,1,0:T(8,128)(2,1)} %bitcast.14), calls=%async_computation | async-start | bytes 8388608 | tf_op jit(solution)/shard_map/all_to_all | solution.py:502
  15.6 0.8 collective-permute-start.3
  46.1 20.1 %collective-permute-start.8 = (bf16[128,4096]{1,0:T(8,128)(2,1)S(1)}, bf16[128,4096]{1,0:T(8,128)(2,1)S(1)}, u32[]{:S(2)}, u32[]{:S(2)}) collective-permute-start(bf16[128,4096]{1,0:T(8,128)(2,1)S(1)} %get-tuple-element.24), channel_id=1, source_target_pairs={{0,32},{1,9},{2,34},{3,11},{4,36},{5,13},{6,38},{7,15},{8,40},{9,1... | collective-permute-start | bytes 3145736 | tf_op jit(solution)/shard_map/ppermute | solution.py:99
  55.6 90.3 %collective-permute-start.2 = (bf16[512,4096]{1,0:T(8,128)(2,1)}, bf16[512,4096]{1,0:T(8,128)(2,1)}, u32[]{:S(2)}, u32[]{:S(2)}) collective-permute-start(bf16[512,4096]{1,0:T(8,128)(2,1)} %bitcast.4.own_ref.refs_0_), channel_id=1, source_target_pairs={{0,96},{1,25},{2,98},{3,27},{4,100},{5,29},{6,102},{7,31},{8,104},... | collective-permute-start | bytes 12582920 | tf_op jit(solution)/shard_map/ppermute | solution.py:99
  55.7 49.8 %all-to-all-start.1 = ((bf16[8,8,4096]{2,1,0:T(8,128)(2,1)}), bf16[8,8,4096]{2,1,0:T(8,128)(2,1)}, u32[]{:S(2)}, u32[]{:S(2)}) async-start(bf16[8,8,4096]{2,1,0:T(8,128)(2,1)} %get-tuple-element.23), calls=%async_computation.1 | async-start | bytes 1048576 | tf_op jit(solution)/shard_map/all_to_all | solution.py:523
  62.7 48.0 %collective-permute-start.11 = (bf16[128,4096]{1,0:T(8,128)(2,1)}, bf16[128,4096]{1,0:T(8,128)(2,1)S(1)}, u32[]{:S(2)}, u32[]{:S(2)}) collective-permute-start(bf16[128,4096]{1,0:T(8,128)(2,1)} %get-tuple-element.27), channel_id=1, source_target_pairs={{0,32},{1,9},{2,34},{3,11},{4,36},{5,13},{6,38},{7,15},{8,40},{9,1... | collective-permute-start | bytes 3145736 | tf_op jit(solution)/shard_map/ppermute | solution.py:99
  64.2 56.0 %collective-permute-start.4 = (bf16[128,4096]{1,0:T(8,128)(2,1)}, bf16[128,4096]{1,0:T(8,128)(2,1)}, u32[]{:S(2)}, u32[]{:S(2)}) collective-permute-start(bf16[128,4096]{1,0:T(8,128)(2,1)} %get-tuple-element.20), channel_id=1, source_target_pairs={{0,32},{1,9},{2,34},{3,11},{4,36},{5,13},{6,38},{7,15},{8,40},{9,1... | collective-permute-start | bytes 3145736 | tf_op jit(solution)/shard_map/ppermute | solution.py:99
  65.3 47.3 %collective-permute-start.6 = (bf16[128,4096]{1,0:T(8,128)(2,1)}, bf16[128,4096]{1,0:T(8,128)(2,1)}, u32[]{:S(2)}, u32[]{:S(2)}) collective-permute-start(bf16[128,4096]{1,0:T(8,128)(2,1)} %get-tuple-element.21), channel_id=1, source_target_pairs={{0,32},{1,9},{2,34},{3,11},{4,36},{5,13},{6,38},{7,15},{8,40},{9,1... | collective-permute-start | bytes 3145736 | tf_op jit(solution)/shard_map/ppermute | solution.py:99
  67.4 70.6 %collective-permute-start.12 = (bf16[128,4096]{1,0:T(8,128)(2,1)}, bf16[128,4096]{1,0:T(8,128)(2,1)S(1)}, u32[]{:S(2)}, u32[]{:S(2)}) collective-permute-start(bf16[128,4096]{1,0:T(8,128)(2,1)} %broadcast_select_fusion.1), channel_id=1, source_target_pairs={{0,2},{1,7},{2,0},{3,5},{4,6},{5,3},{6,4},{7,1},{8,10},{9,15},{10,... | collective-permute-start | bytes 3145736 | tf_op jit(solution)/shard_map/ppermute | solution.py:99
  110.7 18.0 %collective-permute-start.14 = (f32[8,512]{1,0:T(8,128)S(1)}, f32[8,512]{1,0:T(8,128)S(1)}, u32[]{:S(2)}, u32[]{:S(2)}) collective-permute-start(f32[8,512]{1,0:T(8,128)S(1)} %stack.23.refs_1_.refs_2_.refs_5_.refs_8_.refs_4_), channel_id=1, source_target_pairs={{0,32},{1,9},{2,34},{3,11},{4,36},{5,13},{6,38},{7,15},{8,40},{9,1... | collective-permute-start | bytes 49160 | tf_op jit(solution)/shard_map/ppermute | solution.py:99
  112.7 18.7 %collective-permute-start.10 = (f32[8,512]{1,0:T(8,128)S(1)}, f32[8,512]{1,0:T(8,128)S(1)}, u32[]{:S(2)}, u32[]{:S(2)}) collective-permute-start(f32[8,512]{1,0:T(8,128)S(1)} %stack.23.refs_1_.refs_2_.refs_5_.refs_8_.refs_4_), channel_id=1, source_target_pairs={{0,34},{1,15},{2,0},{3,5},{4,38},{5,11},{6,4},{7,1},{8,42},{9,23},... | collective-permute-start | bytes 49160 | tf_op jit(solution)/shard_map/ppermute | solution.py:99
  120.2 15.2 %collective-permute-start.13 = (bf16[128,4096]{1,0:T(8,128)(2,1)}, bf16[128,4096]{1,0:T(8,128)(2,1)}, u32[]{:S(2)}, u32[]{:S(2)}) collective-permute-start(bf16[128,4096]{1,0:T(8,128)(2,1)} %broadcast_select_fusion), channel_id=1, source_target_pairs={{0,2},{1,7},{2,0},{3,5},{4,6},{5,3},{6,4},{7,1},{8,10},{9,15},{10,... | collective-permute-start | bytes 3145736 | tf_op jit(solution)/shard_map/ppermute | solution.py:99
  128.7 27.8 %collective-permute-start.7 = (bf16[128,4096]{1,0:T(8,128)(2,1)}, bf16[128,4096]{1,0:T(8,128)(2,1)S(1)}, u32[]{:S(2)}, u32[]{:S(2)}) collective-permute-start(bf16[128,4096]{1,0:T(8,128)(2,1)} %broadcast_select_fusion.2), channel_id=1, source_target_pairs={{0,2},{1,7},{2,0},{3,5},{4,6},{5,3},{6,4},{7,1},{8,10},{9,15},{10,... | collective-permute-start | bytes 3145736 | tf_op jit(solution)/shard_map/ppermute | solution.py:99
  131.4 26.3 %collective-permute-start.5 = (bf16[128,4096]{1,0:T(8,128)(2,1)}, bf16[128,4096]{1,0:T(8,128)(2,1)S(1)}, u32[]{:S(2)}, u32[]{:S(2)}) collective-permute-start(bf16[128,4096]{1,0:T(8,128)(2,1)} %broadcast_select_fusion.3), channel_id=1, source_target_pairs={{0,2},{1,7},{2,0},{3,5},{4,6},{5,3},{6,4},{7,1},{8,10},{9,15},{10,... | collective-permute-start | bytes 3145736 | tf_op jit(solution)/shard_map/ppermute | solution.py:99
  135.3 10.5 %collective-permute-start.9 = (f32[8,512]{1,0:T(8,128)S(1)}, f32[8,512]{1,0:T(8,128)S(1)}, u32[]{:S(2)}, u32[]{:S(2)}) collective-permute-start(f32[8,512]{1,0:T(8,128)S(1)} %stack.23.refs_1_.refs_2_.refs_5_.refs_8_.refs_4_), channel_id=1, source_target_pairs={{0,96},{1,25},{2,98},{3,27},{4,100},{5,29},{6,102},{7,31},{8,104},... | collective-permute-start | bytes 49160 | tf_op jit(solution)/shard_map/ppermute | solution.py:99
  166.1 16.7 %all-to-all-start.2 = ((f32[32,8,128]{2,1,0:T(8,128)}), f32[32,8,128]{2,1,0:T(8,128)S(1)}, u32[]{:S(2)}, u32[]{:S(2)}) async-start(f32[32,8,128]{2,1,0:T(8,128)} %shard_map.72), calls=%async_computation.2 | async-start | bytes 262144 | tf_op jit(solution)/shard_map/all_to_all | solution.py:591
  182.8 0.7 copy-start

commit v4 on v3

--- a/solution.py
+++ b/solution.py
@@ -109,10 +109,6 @@
 
 def exact(left, right):
     return jnp.dot(left, right, precision=lax.Precision.HIGHEST, preferred_element_type=F32)
-
-
-def exact_dot(left, right, dims=(((1,), (0,)), ((), ()))):
-    return lax.dot_general(left, right, dims, precision=lax.Precision.HIGHEST, preferred_element_type=F32)
 
 
 def split3(value):
@@ -410,7 +406,7 @@
         out_shape=[jax.ShapeDtypeStruct((8, 8, width), BF16), jax.ShapeDtypeStruct((1, 512), F32)]
         + [jax.ShapeDtypeStruct((hi - lo, width), BF16) for lo, hi in pieces],
         in_specs=[ANY_SPEC, VMEM_SPEC],
-        out_specs=[VMEM_SPEC, VMEM_SPEC] + [ANY_SPEC] * len(pieces),
+        out_specs=[VMEM_SPEC] * 3 + [ANY_SPEC] * (len(pieces) - 1),
         scratch_shapes=[
             pltpu.VMEM((512, width), BF16),
             pltpu.VMEM((512, 128), F32),
@@ -443,7 +439,9 @@
             both = both[:, 0:64] + both[:, 64:128]
             both = jnp.concatenate([both, jnp.zeros((4, 64), F32)], axis=0)
             at = (line * 2 + sd) * 64
-            final = final + exact_dot(both, order_ref[at : at + 64, :])
+            parts = jnp.concatenate([p.astype(F32) for p in split3(both)], axis=0).astype(BF16)
+            moved = jnp.dot(parts, order_ref[at : at + 64, :], preferred_element_type=F32)
+            final = final + (moved[0:8] + moved[8:16] + moved[16:24])
     far = 2.0 * far[:, 0:1]
     half_sum = half_sum[:, 0:1]
     keep = keep_ref[...]
@@ -516,14 +514,16 @@
     half = half[0]
 
     l = [send(v, UP) for v in cuts]
-    relays = [jnp.where(edge == 0, v, cut) for v, cut in zip(l, cuts)]
-    f = [send(v, ACROSS) for v in relays]
+    first_relay = jnp.where(edge == 0, l[0], cuts[0])
     r = send(own, DOWN)
 
     found = lax.all_to_all(found, AX, 0, 0, axis_index_groups=class_groups(), tiled=True)
-    found, _ = lax.optimization_barrier((found, relays[0]))
+    found, _ = lax.optimization_barrier((found, first_relay))
     found = jnp.sum(found.astype(F32), axis=0).astype(BF16)
     to_picks = inner(found, own)
+    second, to_picks = lax.optimization_barrier((l[1], to_picks))
+    relays = [first_relay] + [jnp.where(edge == 0, v, cut) for v, cut in zip([second, *l[2:]], cuts[1:])]
+    f = [send(v, ACROSS) for v in relays]
     pick_half = 0.5 * jnp.sum(jnp.square(found.astype(F32)), axis=1)
     near = pick_half[:3, None] - to_picks[:3]
     near1 = near[0]
@@ -597,7 +597,7 @@
     pair_y1 = jnp.where(pair_low, 2 - sd, 3 * sd)
     pair_y = jnp.where(first, pair_y0, pair_y1)
     src2, _, slot2 = source_of(line, line, pair_y, core, (rest // 4) * 32 + rest % 4)
-    in_order = (src2 * 4 + slot2 == iota((512, 512), 1)).astype(F32)
+    in_order = (src2 * 4 + slot2 == iota((512, 512), 1)).astype(BF16)
 
     class_counts = counts[0]
     own_counts = lax.dynamic_index_in_dim(class_counts, dp, 0, keepdims=False)

time: 187 us -> 186 us (level)
  no operation moved by 1% of the time
where the time goes in v4:
time: 186 us; the launch traced here: 185 us
  waiting for transfers between devices  70.4 us (38%)
  starting transfers between devices  49.5 us (27%)
  Pallas kernels  38.1 us (20%)
  other arithmetic  12.8 us (7%)
  matrix products  9.9 us (5%)
  local copies, waits for them, and re-layouts  2.37 us (1%)
  between operations  2.23 us (1%)
    all_to_all x1, waiting for transfers between devices, body(): lax.all_to_all(found, AX, 0, 0, axis_index_groups=class_groups(), tiled=T...  34 us
    ppermute x15, starting transfers between devices, send(): return lax.ppermute(value, AX, pairs)  28.3 us
    all_to_all x1, waiting for transfers between devices, body(): lax.all_to_all(outgoing.reshape(8, 64, width), AX, 0, 0, axis_index_group...  25.3 us
    pallas_call x3, Pallas kernels, early_pairs(): pl.pallas_call(functools.partial(early_kernel, tasks, q_parts, groups, le...  23.5 us
    pallas_call x1, Pallas kernels, last_pairs(): pl.pallas_call(functools.partial(last_kernel, tasks, q_parts, groups, len...  8.38 us
    all_to_all x1, starting transfers between devices, body(): lax.all_to_all(outbox, AX, 0, 0, axis_index_groups=final_groups(), tiled=...  8.2 us
    all_to_all x1, starting transfers between devices, body(): lax.all_to_all(found, AX, 0, 0, axis_index_groups=class_groups(), tiled=T...  7.03 us
    all_to_all x1, starting transfers between devices, body(): lax.all_to_all(outgoing.reshape(8, 64, width), AX, 0, 0, axis_index_group...  5.98 us
  transfers between devices with their start and end apart: 18, of which 6 were waited for; matrix products, arithmetic and copies ran while one was open for 11% of the time, Pallas kernels for 13%

profile of v4, /device:TPU:1, one launch (start us, length us, event | category | flops | bytes accessed | tf_op | source)
XLA Modules:
  0.0 185.4 jit_solution(13920200173042094215)
XLA Ops:
  0.6 1.5 collective-permute-start.1
  2.1 0.7 broadcast_select_fusion.7
  2.8 0.1 collective-permute-start
  2.9 2.8 %fusion.2 = f32[512,4096]{1,0:T(8,128)S(1)} fusion(bf16[256,4096]{1,0:T(8,128)(2,1)} %param.5, s32[256]{0:T(256)S(1)} %broadcast_select_fusion.6), kind=kOutput, calls=%fused_computation.11 | convolution fusion | flops 1073872896 | bytes 10486784 | tf_op jit(solution)/shard_map/dot_general | solution.py:497
  5.8 0.3 collective-permute-done
  6.1 3.4 %add_convert_fusion = bf16[512,4096]{1,0:T(8,128)(2,1)} fusion(f32[512,4096]{1,0:T(8,128)S(1)} %fusion.2, bf16[256,4096]{1,0:T(8,128)(2,1)S(1)} %collective-permute-done.1, s32[256]{0:T(256)S(1)} %collective-permute-done), kind=kOutput, calls=%fused_computation | convolution fusion | flops 1078067200 | bytes 14681088 | tf_op jit(solution)/shard_map/dot_general | solution.py:498
  9.4 6.0 %all-to-all-start = ((bf16[8,64,4096]{2,1,0:T(8,128)(2,1)}), bf16[8,64,4096]{2,1,0:T(8,128)(2,1)}, u32[]{:S(2)}, u32[]{:S(2)}) async-start(bf16[8,64,4096]{2,1,0:T(8,128)(2,1)} %bitcast.15), calls=%async_computation | async-start | bytes 8388608 | tf_op jit(solution)/shard_map/all_to_all | solution.py:500
  15.4 0.1 pad.2.clone
  15.5 0.1 pad_add_fusion
  15.6 0.7 collective-permute-start.3
  16.4 0.1 slice_reduce_fusion
  16.5 0.1 compare_convert_fusion.hit_ref
  16.5 25.3 %all-to-all-done = bf16[8,64,4096]{2,1,0:T(8,128)(2,1)} async-done(((bf16[8,64,4096]{2,1,0:T(8,128)(2,1)}), bf16[8,64,4096]{2,1,0:T(8,128)(2,1)}, u32[]{:S(2)}, u32[]{:S(2)}) %all-to-all-start) | async-done | bytes 4194336 | tf_op jit(solution)/shard_map/all_to_all | solution.py:500
  41.8 4.2 %shard_map.68 = (bf16[8,8,4096]{2,1,0:T(8,128)(2,1)}, f32[1,512]{1,0:T(1,128)S(1)}, bf16[128,4096]{1,0:T(8,128)(2,1)S(1)}, bf16[128,4096]{1,0:T(8,128)(2,1)}, bf...) custom-call(bf16[512,4096]{1,0:T(8,128)(2,1)} %bitcast.4.own_ref.refs_0_, bf16[8,512]{1,0:T(8,128)(2,1)S(1)} %compare_convert_fusion.hit_ref), custom_call_target="tpu_custom_call" | custom-call | flops 2147483648 | bytes 4194304 | tf_op jit(solution)/shard_map/pallas_call | solution.py:404
  46.1 6.6 %collective-permute-start.8 = (bf16[128,4096]{1,0:T(8,128)(2,1)S(1)}, bf16[128,4096]{1,0:T(8,128)(2,1)S(1)}, u32[]{:S(2)}, u32[]{:S(2)}) collective-permute-start(bf16[128,4096]{1,0:T(8,128)(2,1)S(1)} %get-tuple-element.26), channel_id=1, source_target_pairs={{0,32},{1,9},{2,34},{3,11},{4,36},{5,13},{6,38},{7,15},{8,40},{9,1... | collective-permute-start | bytes 3145736 | tf_op jit(solution)/shard_map/ppermute | solution.py:99
  52.7 1.0 fusion.1.order_ref
  53.7 0.6 fusion.11
  54.9 0.3 fusion
  55.3 0.1 collective-permute-start.2
  55.4 7.0 %all-to-all-start.1 = ((bf16[8,8,4096]{2,1,0:T(8,128)(2,1)}), bf16[8,8,4096]{2,1,0:T(8,128)(2,1)}, u32[]{:S(2)}, u32[]{:S(2)}) async-start(bf16[8,8,4096]{2,1,0:T(8,128)(2,1)} %get-tuple-element.25), calls=%async_computation.1 | async-start | bytes 1048576 | tf_op jit(solution)/shard_map/all_to_all | solution.py:520
  62.4 1.5 collective-permute-start.4
  63.9 1.2 collective-permute-start.6
  65.1 0.9 collective-permute-start.9
  65.9 0.0 collective-permute-done.8.refs_1_.refs_2_
  66.0 1.1 broadcast_select_fusion.1
  67.1 4.1 %collective-permute-start.12 = (bf16[128,4096]{1,0:T(8,128)(2,1)}, bf16[128,4096]{1,0:T(8,128)(2,1)S(1)}, u32[]{:S(2)}, u32[]{:S(2)}) collective-permute-start(bf16[128,4096]{1,0:T(8,128)(2,1)} %broadcast_select_fusion.1), channel_id=1, source_target_pairs={{0,2},{1,7},{2,0},{3,5},{4,6},{5,3},{6,4},{7,1},{8,10},{9,15},{10,... | collective-permute-start | bytes 3145736 | tf_op jit(solution)/shard_map/ppermute | solution.py:99
  71.2 34.0 %all-to-all-done.1 = bf16[8,8,4096]{2,1,0:T(8,128)(2,1)} async-done(((bf16[8,8,4096]{2,1,0:T(8,128)(2,1)}), bf16[8,8,4096]{2,1,0:T(8,128)(2,1)}, u32[]{:S(2)}, u32[]{:S(2)}) %all-to-all-start.1) | async-done | bytes 524320 | tf_op jit(solution)/shard_map/all_to_all | solution.py:520
  105.1 1.1 reduce_sum.61
  106.3 0.1 multiply_reduce_fusion
  106.4 3.4 %fusion.79 = f32[8,512]{1,0:T(8,128)S(1)} fusion(bf16[8,4096]{1,0:T(8,128)(2,1)S(1)} %reduce_sum.61, bf16[512,4096]{1,0:T(8,128)(2,1)} %bitcast.4.own_ref.refs_0_), kind=kOutput, calls=%fused_computation.202 | convolution fusion | flops 33554432 | bytes 4276224 | tf_op jit(solution)/shard_map/dot_general | solution.py:107
  109.8 0.0 collective-permute-done.9.refs_2_.refs_3_
  109.8 0.1 slice_subtract_fusion
  109.9 1.1 broadcast_select_fusion
  111.0 0.6 fusion.78
  111.6 0.8 collective-permute-start.14
  112.5 0.0 collective-permute-done.4.refs_4_
  112.5 5.2 %collective-permute-start.11 = (f32[8,512]{1,0:T(8,128)S(1)}, f32[8,512]{1,0:T(8,128)S(1)}, u32[]{:S(2)}, u32[]{:S(2)}) collective-permute-start(f32[8,512]{1,0:T(8,128)S(1)} %stack.23.refs_1_.refs_2_.refs_5_.refs_8_.refs_4_), channel_id=1, source_target_pairs={{0,34},{1,15},{2,0},{3,5},{4,38},{5,11},{6,4},{7,1},{8,42},{9,23},... | collective-permute-start | bytes 49160 | tf_op jit(solution)/shard_map/ppermute | solution.py:99
  117.7 2.4 %broadcast_select_fusion.3 = bf16[128,4096]{1,0:T(8,128)(2,1)} fusion(bf16[128,4096]{1,0:T(8,128)(2,1)} %collective-permute-done.4.refs_4_, bf16[128,4096]{1,0:T(8,128)(2,1)} %get-tuple-element.22, pred[]{:T(512)S(6)} %eq.162), kind=kLoop, calls=%fused_computation.8 | loop fusion | flops 524288 | bytes 3145729 | tf_op jit(solution)/shard_map/jit(_where)/select_n | solution.py:525
  120.1 0.2 collective-permute-start.13
  120.3 2.3 %broadcast_select_fusion.2 = bf16[128,4096]{1,0:T(8,128)(2,1)} fusion(bf16[128,4096]{1,0:T(8,128)(2,1)} %collective-permute-done.6.refs_5_, bf16[128,4096]{1,0:T(8,128)(2,1)} %get-tuple-element.23, pred[]{:T(512)S(6)} %eq.162), kind=kLoop, calls=%fused_computation.7 | loop fusion | flops 524288 | bytes 3145729 | tf_op jit(solution)/shard_map/jit(_where)/select_n | solution.py:525
  122.7 5.0 %shard_map.69 = (f32[8,512]{1,0:T(8,128)S(1)}, f32[8,128]{1,0:T(8,128)S(1)}) custom-call(s32[1]{0:T(128)} %bitcast.2.side_ref_in, bf16[512,4096]{1,0:T(8,128)(2,1)} %bitcast.4.own_ref.refs_0_, f32[8,512]{1,0:T(8,128)S(1)} %stack.23.refs_1_.refs_2_.refs_5_.refs_8_.refs_4_, f32[8,512]{1,0:T(8,128)S(1)} %stack.23.refs_1_.refs_2_.refs_5_.refs_8_.refs_4_), custom_call_target="tpu_custom_call" | custom-call | flops 2147483648 | bytes 4194304 | tf_op jit(solution)/shard_map/pallas_call | solution.py:286
  127.7 0.6 stack_broadcast_in_dim.7
  128.4 0.1 stack.24.refs_18_
  128.5 0.0 collective-permute-done.14
  128.5 2.7 %collective-permute-start.5 = (bf16[128,4096]{1,0:T(8,128)(2,1)}, bf16[128,4096]{1,0:T(8,128)(2,1)S(1)}, u32[]{:S(2)}, u32[]{:S(2)}) collective-permute-start(bf16[128,4096]{1,0:T(8,128)(2,1)} %broadcast_select_fusion.3), channel_id=1, source_target_pairs={{0,2},{1,7},{2,0},{3,5},{4,6},{5,3},{6,4},{7,1},{8,10},{9,15},{10,... | collective-permute-start | bytes 3145736 | tf_op jit(solution)/shard_map/ppermute | solution.py:99
  131.3 0.2 collective-permute-start.7
  131.5 0.0 collective-permute-done.12.refs_3_.refs_6_
  131.5 2.6 %collective-permute-start.10 = (f32[8,512]{1,0:T(8,128)S(1)}, f32[8,512]{1,0:T(8,128)S(1)}, u32[]{:S(2)}, u32[]{:S(2)}) collective-permute-start(f32[8,512]{1,0:T(8,128)S(1)} %stack.23.refs_1_.refs_2_.refs_5_.refs_8_.refs_4_), channel_id=1, source_target_pairs={{0,96},{1,25},{2,98},{3,27},{4,100},{5,29},{6,102},{7,31},{8,104},... | collective-permute-start | bytes 49160 | tf_op jit(solution)/shard_map/ppermute | solution.py:99
  134.0 1.2 collective-permute-done.13.refs_4_.refs_7_
  135.3 7.8 %shard_map.70 = (f32[8,256]{1,0:T(8,128)S(1)}, f32[8,256]{1,0:T(8,128)S(1)}, f32[3,512,128]{2,1,0:T(8,128)S(1)}, f32[8,128]{1,0:T(8,128)S(1)}) custom-call(s32[1]{0:T(128)} %bitcast.2.side_ref_in, bf16[512,4096]{1,0:T(8,128)(2,1)} %bitcast.4.own_ref.refs_0_, bf16[128,4096]{1,0:T(8,128)(2,1)S(1)} %collective-permute-done.8.refs_1_.refs_2_, ...), custom_call_target="tpu_custom_call" | custom-call | flops 2147483648 | bytes 8388608 | tf_op jit(solution)/shard_map/pallas_call | solution.py:286
  143.1 0.0 collective-permute-done.10.refs_9_.refs_5_
  143.1 10.7 %shard_map.71 = (f32[8,256]{1,0:T(8,128)S(1)}, f32[8,256]{1,0:T(8,128)S(1)}, f32[3,512,128]{2,1,0:T(8,128)S(1)}, f32[3,512,128]{2,1,0:T(8,128)S(1)}, f32[8,128]{1,0:T(8,128)S(1)}) custom-call(s32[1]{0:T(128)} %bitcast.2.side_ref_in, bf16[512,4096]{1,0:T(8,128)(2,1)} %bitcast.4.own_ref.refs_0_, bf16[512,4096]{1,0:T(8,128)(2,1)} %collective-permute-done.2.refs_1_, ...), custom_call_target="tpu_custom_call" | custom-call | flops 4294967296 | bytes 14680064 | tf_op jit(solution)/shard_map/pallas_call | solution.py:286
  153.8 0.0 collective-permute-done.5.refs_2_
  153.8 3.8 %collective-permute-done.7.refs_3_ = bf16[128,4096]{1,0:T(8,128)(2,1)S(1)} collective-permute-done((bf16[128,4096]{1,0:T(8,128)(2,1)}, bf16[128,4096]{1,0:T(8,128)(2,1)S(1)}, u32[]{:S(2)}, u32[]{:S(2)}) %collective-permute-start.7) | collective-permute-done | bytes 1048608 | tf_op jit(solution)/shard_map/ppermute | solution.py:99
  157.6 8.4 %shard_map.72 = f32[32,8,128]{2,1,0:T(8,128)} custom-call(s32[1]{0:T(128)} %bitcast.2.side_ref_in, bf16[512,4096]{1,0:T(8,128)(2,1)} %bitcast.4.own_ref.refs_0_, bf16[512,4096]{1,0:T(8,128)(2,1)} %collective-permute-done.2.refs_1_, bf16[128,4096]{1,0:T(8,128)(2,1)S(1)} %collective-permute-done.5.refs_2_, ...), custom_call_target="tpu_custom_call" | custom-call | flops 2147483648 | bytes 10485760 | tf_op jit(solution)/shard_map/pallas_call | solution.py:350
  166.0 8.2 %all-to-all-start.2 = ((f32[32,8,128]{2,1,0:T(8,128)}), f32[32,8,128]{2,1,0:T(8,128)S(1)}, u32[]{:S(2)}, u32[]{:S(2)}) async-start(f32[32,8,128]{2,1,0:T(8,128)} %shard_map.72), calls=%async_computation.2 | async-start | bytes 262144 | tf_op jit(solution)/shard_map/all_to_all | solution.py:591
  174.2 0.1 fusion.5
  174.3 0.7 reduce_sum.65
  175.7 0.7 reshape.784.keep_ref
  176.4 0.6 pad_add_fusion.1.where_ref
  177.0 5.8 %all-to-all-done.2.in_ref = f32[32,8,128]{2,1,0:T(8,128)S(1)} async-done(((f32[32,8,128]{2,1,0:T(8,128)}), f32[32,8,128]{2,1,0:T(8,128)S(1)}, u32[]{:S(2)}, u32[]{:S(2)}) %all-to-all-start.2) | async-done | bytes 131104 | tf_op jit(solution)/shard_map/all_to_all | solution.py:591
  182.8 0.6 broadcast_in_dim.51.total_ref
  183.4 0.0 copy-done
  183.4 2.0 %shard_map.73 = (f32[3,1,512]{2,1,0:T(1,128)}, f32[1,512]{1,0:T(1,128)}) custom-call(s32[2]{0:T(128)} %pad_add_fusion.1.where_ref, f32[32,8,128]{2,1,0:T(8,128)} %copy-done, bf16[512,512]{1,0:T(8,128)(2,1)} %fusion.1.order_ref, f32[1,512]{1,0:T(1,128)} %reshape.784.keep_ref, f32[1,128]{1,0:T(1,128)} %broadcast_in_dim.51.total_ref), custom_call_target="tpu_custom_call" | custom-call | tf_op jit(solution)/shard_map/pallas_call | solution.py:608
  (23 shorter events, 0.2 us)
Async XLA Ops:
  0.6 5.5 %collective-permute-start.1 = (bf16[256,4096]{1,0:T(8,128)(2,1)}, bf16[256,4096]{1,0:T(8,128)(2,1)S(1)}, u32[]{:S(2)}, u32[]{:S(2)}) collective-permute-start(bf16[256,4096]{1,0:T(8,128)(2,1)} %param.5), channel_id=1, source_target_pairs={{0,1},{1,0},{2,3},{3,2},{4,5},{5,4},{6,7},{7,6},{8,9},{9,8},{10,11... | collective-permute-start | bytes 6291464 | tf_op jit(solution)/shard_map/ppermute | solution.py:99
  2.8 3.3 %collective-permute-start = (s32[256]{0:T(256)S(1)}, s32[256]{0:T(256)S(1)}, u32[]{:S(2)}, u32[]{:S(2)}) collective-permute-start(s32[256]{0:T(256)S(1)} %get-tuple-element.46), channel_id=1, source_target_pairs={{0,1},{1,0},{2,3},{3,2},{4,5},{5,4},{6,7},{7,6},{8,9},{9,8},{10,11... | collective-permute-start | bytes 3080 | tf_op jit(solution)/shard_map/ppermute | solution.py:99
  9.4 6.0 %copy-start.2 = (s32[3,1]{0,1:T(1,128)S(1)}, s32[3,1]{0,1:T(1,128)}, u32[]{:S(2)}) copy-start(s32[3,1]{0,1:T(1,128)} %param.9) | copy-start | bytes 40
  9.4 6.1 %copy-start.1 = (s32[1,8,128]{2,1,0:T(8,128)S(1)}, s32[1,8,128]{2,1,0:T(8,128)}, u32[]{:S(2)}) copy-start(s32[1,8,128]{2,1,0:T(8,128)} %param.8) | copy-start | bytes 12292
  9.4 32.4 %all-to-all-start = ((bf16[8,64,4096]{2,1,0:T(8,128)(2,1)}), bf16[8,64,4096]{2,1,0:T(8,128)(2,1)}, u32[]{:S(2)}, u32[]{:S(2)}) async-start(bf16[8,64,4096]{2,1,0:T(8,128)(2,1)} %bitcast.15), calls=%async_computation | async-start | bytes 8388608 | tf_op jit(solution)/shard_map/all_to_all | solution.py:500
  15.6 0.8 collective-permute-start.3
  46.1 19.9 %collective-permute-start.8 = (bf16[128,4096]{1,0:T(8,128)(2,1)S(1)}, bf16[128,4096]{1,0:T(8,128)(2,1)S(1)}, u32[]{:S(2)}, u32[]{:S(2)}) collective-permute-start(bf16[128,4096]{1,0:T(8,128)(2,1)S(1)} %get-tuple-element.26), channel_id=1, source_target_pairs={{0,32},{1,9},{2,34},{3,11},{4,36},{5,13},{6,38},{7,15},{8,40},{9,1... | collective-permute-start | bytes 3145736 | tf_op jit(solution)/shard_map/ppermute | solution.py:99
  55.3 87.8 %collective-permute-start.2 = (bf16[512,4096]{1,0:T(8,128)(2,1)}, bf16[512,4096]{1,0:T(8,128)(2,1)}, u32[]{:S(2)}, u32[]{:S(2)}) collective-permute-start(bf16[512,4096]{1,0:T(8,128)(2,1)} %bitcast.4.own_ref.refs_0_), channel_id=1, source_target_pairs={{0,96},{1,25},{2,98},{3,27},{4,100},{5,29},{6,102},{7,31},{8,104},... | collective-permute-start | bytes 12582920 | tf_op jit(solution)/shard_map/ppermute | solution.py:99
  55.4 49.8 %all-to-all-start.1 = ((bf16[8,8,4096]{2,1,0:T(8,128)(2,1)}), bf16[8,8,4096]{2,1,0:T(8,128)(2,1)}, u32[]{:S(2)}, u32[]{:S(2)}) async-start(bf16[8,8,4096]{2,1,0:T(8,128)(2,1)} %get-tuple-element.25), calls=%async_computation.1 | async-start | bytes 1048576 | tf_op jit(solution)/shard_map/all_to_all | solution.py:520
  62.4 50.1 %collective-permute-start.4 = (bf16[128,4096]{1,0:T(8,128)(2,1)}, bf16[128,4096]{1,0:T(8,128)(2,1)}, u32[]{:S(2)}, u32[]{:S(2)}) collective-permute-start(bf16[128,4096]{1,0:T(8,128)(2,1)} %get-tuple-element.22), channel_id=1, source_target_pairs={{0,32},{1,9},{2,34},{3,11},{4,36},{5,13},{6,38},{7,15},{8,40},{9,1... | collective-permute-start | bytes 3145736 | tf_op jit(solution)/shard_map/ppermute | solution.py:99
  63.9 56.2 %collective-permute-start.6 = (bf16[128,4096]{1,0:T(8,128)(2,1)}, bf16[128,4096]{1,0:T(8,128)(2,1)}, u32[]{:S(2)}, u32[]{:S(2)}) collective-permute-start(bf16[128,4096]{1,0:T(8,128)(2,1)} %get-tuple-element.23), channel_id=1, source_target_pairs={{0,32},{1,9},{2,34},{3,11},{4,36},{5,13},{6,38},{7,15},{8,40},{9,1... | collective-permute-start | bytes 3145736 | tf_op jit(solution)/shard_map/ppermute | solution.py:99
  65.1 44.7 %collective-permute-start.9 = (bf16[128,4096]{1,0:T(8,128)(2,1)}, bf16[128,4096]{1,0:T(8,128)(2,1)S(1)}, u32[]{:S(2)}, u32[]{:S(2)}) collective-permute-start(bf16[128,4096]{1,0:T(8,128)(2,1)} %get-tuple-element.28), channel_id=1, source_target_pairs={{0,32},{1,9},{2,34},{3,11},{4,36},{5,13},{6,38},{7,15},{8,40},{9,1... | collective-permute-start | bytes 3145736 | tf_op jit(solution)/shard_map/ppermute | solution.py:99
  67.1 64.4 %collective-permute-start.12 = (bf16[128,4096]{1,0:T(8,128)(2,1)}, bf16[128,4096]{1,0:T(8,128)(2,1)S(1)}, u32[]{:S(2)}, u32[]{:S(2)}) collective-permute-start(bf16[128,4096]{1,0:T(8,128)(2,1)} %broadcast_select_fusion.1), channel_id=1, source_target_pairs={{0,2},{1,7},{2,0},{3,5},{4,6},{5,3},{6,4},{7,1},{8,10},{9,15},{10,... | collective-permute-start | bytes 3145736 | tf_op jit(solution)/shard_map/ppermute | solution.py:99
  111.6 16.9 %collective-permute-start.14 = (f32[8,512]{1,0:T(8,128)S(1)}, f32[8,512]{1,0:T(8,128)S(1)}, u32[]{:S(2)}, u32[]{:S(2)}) collective-permute-start(f32[8,512]{1,0:T(8,128)S(1)} %stack.23.refs_1_.refs_2_.refs_5_.refs_8_.refs_4_), channel_id=1, source_target_pairs={{0,32},{1,9},{2,34},{3,11},{4,36},{5,13},{6,38},{7,15},{8,40},{9,1... | collective-permute-start | bytes 49160 | tf_op jit(solution)/shard_map/ppermute | solution.py:99
  112.5 18.8 %collective-permute-start.11 = (f32[8,512]{1,0:T(8,128)S(1)}, f32[8,512]{1,0:T(8,128)S(1)}, u32[]{:S(2)}, u32[]{:S(2)}) collective-permute-start(f32[8,512]{1,0:T(8,128)S(1)} %stack.23.refs_1_.refs_2_.refs_5_.refs_8_.refs_4_), channel_id=1, source_target_pairs={{0,34},{1,15},{2,0},{3,5},{4,38},{5,11},{6,4},{7,1},{8,42},{9,23},... | collective-permute-start | bytes 49160 | tf_op jit(solution)/shard_map/ppermute | solution.py:99
  120.1 15.2 %collective-permute-start.13 = (bf16[128,4096]{1,0:T(8,128)(2,1)}, bf16[128,4096]{1,0:T(8,128)(2,1)}, u32[]{:S(2)}, u32[]{:S(2)}) collective-permute-start(bf16[128,4096]{1,0:T(8,128)(2,1)} %broadcast_select_fusion), channel_id=1, source_target_pairs={{0,2},{1,7},{2,0},{3,5},{4,6},{5,3},{6,4},{7,1},{8,10},{9,15},{10,... | collective-permute-start | bytes 3145736 | tf_op jit(solution)/shard_map/ppermute | solution.py:99
  128.5 25.3 %collective-permute-start.5 = (bf16[128,4096]{1,0:T(8,128)(2,1)}, bf16[128,4096]{1,0:T(8,128)(2,1)S(1)}, u32[]{:S(2)}, u32[]{:S(2)}) collective-permute-start(bf16[128,4096]{1,0:T(8,128)(2,1)} %broadcast_select_fusion.3), channel_id=1, source_target_pairs={{0,2},{1,7},{2,0},{3,5},{4,6},{5,3},{6,4},{7,1},{8,10},{9,15},{10,... | collective-permute-start | bytes 3145736 | tf_op jit(solution)/shard_map/ppermute | solution.py:99
  131.3 26.4 %collective-permute-start.7 = (bf16[128,4096]{1,0:T(8,128)(2,1)}, bf16[128,4096]{1,0:T(8,128)(2,1)S(1)}, u32[]{:S(2)}, u32[]{:S(2)}) collective-permute-start(bf16[128,4096]{1,0:T(8,128)(2,1)} %broadcast_select_fusion.2), channel_id=1, source_target_pairs={{0,2},{1,7},{2,0},{3,5},{4,6},{5,3},{6,4},{7,1},{8,10},{9,15},{10,... | collective-permute-start | bytes 3145736 | tf_op jit(solution)/shard_map/ppermute | solution.py:99
  131.5 11.6 %collective-permute-start.10 = (f32[8,512]{1,0:T(8,128)S(1)}, f32[8,512]{1,0:T(8,128)S(1)}, u32[]{:S(2)}, u32[]{:S(2)}) collective-permute-start(f32[8,512]{1,0:T(8,128)S(1)} %stack.23.refs_1_.refs_2_.refs_5_.refs_8_.refs_4_), channel_id=1, source_target_pairs={{0,96},{1,25},{2,98},{3,27},{4,100},{5,29},{6,102},{7,31},{8,104},... | collective-permute-start | bytes 49160 | tf_op jit(solution)/shard_map/ppermute | solution.py:99
  166.0 16.7 %all-to-all-start.2 = ((f32[32,8,128]{2,1,0:T(8,128)}), f32[32,8,128]{2,1,0:T(8,128)S(1)}, u32[]{:S(2)}, u32[]{:S(2)}) async-start(f32[32,8,128]{2,1,0:T(8,128)} %shard_map.72), calls=%async_computation.2 | async-start | bytes 262144 | tf_op jit(solution)/shard_map/all_to_all | solution.py:591
  182.8 0.7 copy-start

commit v5 on v4

--- a/solution.py
+++ b/solution.py
@@ -310,9 +310,9 @@
     cols = {0: col0_ref, 1: col1_ref}
     rows, far = pair_work(side_ref_in[0], tasks, q_parts, groups, hbm, notes, cols, q_buf, u_bufs, x_ref, side_ref, sems)
     g_ref[...] = extra_ref[...]
-    for ref, (row, at) in zip(lane_refs, lane_rows):
-        m = ref.shape[1]
-        g_ref[row : row + 3, at : at + m] += ref[0:3, :]
+    for ref, places in zip(lane_refs, lane_rows):
+        for row, at, lo, m in places:
+            g_ref[row : row + 3, at : at + m] += ref[0:3, lo : lo + m]
     for g, (row, at) in own_rows.items():
         for j in range(3):
             value = rows[g][j]
@@ -378,7 +378,7 @@
     for i, copy in enumerate(copies):
         copy.wait()
         for each, (lo, hi) in zip(out, pieces):
-            if hi == i * slab + slab:
+            if i * slab < hi <= i * slab + slab:
                 each.start()
 
         def step(k, _, i=i):
@@ -510,7 +510,7 @@
     valid = slot[0].astype(F32) < seen
     n_valid = jnp.sum(host_counts)
     hit = (place == jnp.concatenate([picks, -jnp.ones((5,), jnp.int32)])[:, None]).astype(BF16)
-    found, half, *cuts = prepare(own, hit, tuple((i, i + 128) for i in range(0, 512, 128)))
+    found, half, *cuts = prepare(own, hit, ((0, 128), (128, 256), (256, 384), (384, 512)))
     half = half[0]
 
     l = [send(v, UP) for v in cuts]
@@ -541,25 +541,17 @@
     l_low, l_high = info_l[:, :mid], info_l[:, mid:]
     f_low, f_high = info_f[:, :mid], info_f[:, mid:]
     lanes_1, _, far_1 = early_pairs(edge, [own], [[0]], [None], [info, info], [(0, [(0, True, False)])])
+    low = jnp.concatenate([l_low, f_low], axis=1)
     lanes_2, cols_2, far_2 = early_pairs(
-        edge,
-        [own, l[0], l[1], f[0], f[1]],
-        [[0]],
-        [[1, 2], [3, 4]],
-        [info, l_low, f_low],
-        [(0, [(0, True, True)]), (1, [(0, True, True)])],
+        edge, [own, l[0], l[1], f[0], f[1]], [[0]], [[1, 2, 3, 4]], [info, low], [(0, [(0, True, True)])]
     )
     lanes_3, cols_3, far_3 = early_pairs(
         edge,
         [own, r, *l, f[0], f[1]],
         [[0], [1]],
-        [[6, 7], [4, 5], [2, 3]],
-        [info, info_r, f_low, l_high, l_low],
-        [
-            (2, [(1, False, True)]),
-            (0, [(1, True, True)]),
-            (1, [(0, True, True), (1, False, True)]),
-        ],
+        [[2, 3, 6, 7], [4, 5]],
+        [info, info_r, low, l_high],
+        [(0, [(1, True, True)]), (1, [(0, True, True), (1, False, True)])],
     )
     none = jnp.zeros((512,), F32)
     extra = [none] * 16
@@ -568,11 +560,10 @@
     extra[11] = jnp.broadcast_to(jnp.sum(half), (512,))
     extra = jnp.stack(extra)
     lane_list = [
-        (lanes_1[0], (0, 0)),
-        (lanes_2[0], (4, 0)),
-        (lanes_2[1], (12, 0)),
-        (lanes_3[0], (12, 0)),
-        (lanes_3[1], (4, mid)),
+        (lanes_1[0], [(0, 0, 0, 512)]),
+        (lanes_2[0], [(4, 0, 0, mid), (12, 0, mid, mid)]),
+        (lanes_3[0], [(12, 0, mid, mid)]),
+        (lanes_3[1], [(4, mid, 0, mid)]),
     ]
     outbox = last_pairs(
         edge,

time: 186 us -> 186 us (level)
  Pallas kernels: 38.1 us -> 34.4 us
  waiting for transfers between devices: 70.4 us -> 74.1 us
    pallas_call x3, Pallas kernels: 23.5 us -> 19.8 us  [early_pairs(): pl.pallas_call(functools.partial(early_kernel, tasks, q_parts, groups, le...]
    ppermute x15, waiting for transfers between devices: 5.38 us -> 9.1 us  [send(): return lax.ppermute(value, AX, pairs)]
  transfers between devices with their start and end apart: 18 -> 18, of which waited for: 6 -> 6; matrix products, arithmetic and copies ran while one was open for 11% -> 11% of each run, Pallas kernels for 13% -> 11%
where the time goes in v5:
time: 186 us; the launch traced here: 185 us
  waiting for transfers between devices  74.1 us (40%)
  starting transfers between devices  49.5 us (27%)
  Pallas kernels  34.4 us (18%)
  other arithmetic  12.8 us (7%)
  matrix products  9.9 us (5%)
  local copies, waits for them, and re-layouts  2.37 us (1%)
  between operations  2.23 us (1%)
    all_to_all x1, waiting for transfers between devices, body(): lax.all_to_all(found, AX, 0, 0, axis_index_groups=class_groups(), tiled=T...  34 us
    ppermute x15, starting transfers between devices, send(): return lax.ppermute(value, AX, pairs)  28.3 us
    all_to_all x1, waiting for transfers between devices, body(): lax.all_to_all(outgoing.reshape(8, 64, width), AX, 0, 0, axis_index_group...  25.3 us
    pallas_call x3, Pallas kernels, early_pairs(): pl.pallas_call(functools.partial(early_kernel, tasks, q_parts, groups, le...  19.8 us
    ppermute x15, waiting for transfers between devices, send(): return lax.ppermute(value, AX, pairs)  9.1 us
    pallas_call x1, Pallas kernels, last_pairs(): pl.pallas_call(functools.partial(last_kernel, tasks, q_parts, groups, len...  8.38 us
    all_to_all x1, starting transfers between devices, body(): lax.all_to_all(outbox, AX, 0, 0, axis_index_groups=final_groups(), tiled=...  8.2 us
    all_to_all x1, starting transfers between devices, body(): lax.all_to_all(found, AX, 0, 0, axis_index_groups=class_groups(), tiled=T...  7.03 us
  transfers between devices with their start and end apart: 18, of which 6 were waited for; matrix products, arithmetic and copies ran while one was open for 11% of the time, Pallas kernels for 11%

profile of v5, /device:TPU:1, one launch (start us, length us, event | category | flops | bytes accessed | tf_op | source)
XLA Modules:
  0.0 185.4 jit_solution(4341561761893339064)
XLA Ops:
  0.6 1.5 collective-permute-start.1
  2.1 0.7 broadcast_select_fusion.7
  2.8 0.1 collective-permute-start
  2.9 2.8 %fusion.2 = f32[512,4096]{1,0:T(8,128)S(1)} fusion(bf16[256,4096]{1,0:T(8,128)(2,1)} %param.5, s32[256]{0:T(256)S(1)} %broadcast_select_fusion.6), kind=kOutput, calls=%fused_computation.11 | convolution fusion | flops 1073872896 | bytes 10486784 | tf_op jit(solution)/shard_map/dot_general | solution.py:497
  5.8 0.3 collective-permute-done
  6.1 0.0 collective-permute-done.1
  6.1 3.4 %add_convert_fusion = bf16[512,4096]{1,0:T(8,128)(2,1)} fusion(f32[512,4096]{1,0:T(8,128)S(1)} %fusion.2, bf16[256,4096]{1,0:T(8,128)(2,1)S(1)} %collective-permute-done.1, s32[256]{0:T(256)S(1)} %collective-permute-done), kind=kOutput, calls=%fused_computation | convolution fusion | flops 1078067200 | bytes 14681088 | tf_op jit(solution)/shard_map/dot_general | solution.py:498
  9.4 6.0 %all-to-all-start = ((bf16[8,64,4096]{2,1,0:T(8,128)(2,1)}), bf16[8,64,4096]{2,1,0:T(8,128)(2,1)}, u32[]{:S(2)}, u32[]{:S(2)}) async-start(bf16[8,64,4096]{2,1,0:T(8,128)(2,1)} %bitcast.15), calls=%async_computation | async-start | bytes 8388608 | tf_op jit(solution)/shard_map/all_to_all | solution.py:500
  15.4 0.1 pad.4.clone
  15.5 0.1 pad_add_fusion
  15.6 0.7 collective-permute-start.3
  16.3 0.0 collective-permute-done.3
  16.4 0.1 slice_reduce_fusion
  16.5 0.1 compare_convert_fusion.hit_ref
  16.5 25.3 %all-to-all-done = bf16[8,64,4096]{2,1,0:T(8,128)(2,1)} async-done(((bf16[8,64,4096]{2,1,0:T(8,128)(2,1)}), bf16[8,64,4096]{2,1,0:T(8,128)(2,1)}, u32[]{:S(2)}, u32[]{:S(2)}) %all-to-all-start) | async-done | bytes 4194336 | tf_op jit(solution)/shard_map/all_to_all | solution.py:500
  41.8 4.2 %shard_map.68 = (bf16[8,8,4096]{2,1,0:T(8,128)(2,1)}, f32[1,512]{1,0:T(1,128)S(1)}, bf16[128,4096]{1,0:T(8,128)(2,1)S(1)}, bf16[128,4096]{1,0:T(8,128)(2,1)}, bf...) custom-call(bf16[512,4096]{1,0:T(8,128)(2,1)} %bitcast.4.own_ref.refs_0_, bf16[8,512]{1,0:T(8,128)(2,1)S(1)} %compare_convert_fusion.hit_ref), custom_call_target="tpu_custom_call" | custom-call | flops 2147483648 | bytes 4194304 | tf_op jit(solution)/shard_map/pallas_call | solution.py:404
  46.1 6.6 %collective-permute-start.8 = (bf16[128,4096]{1,0:T(8,128)(2,1)S(1)}, bf16[128,4096]{1,0:T(8,128)(2,1)S(1)}, u32[]{:S(2)}, u32[]{:S(2)}) collective-permute-start(bf16[128,4096]{1,0:T(8,128)(2,1)S(1)} %get-tuple-element.25), channel_id=1, source_target_pairs={{0,32},{1,9},{2,34},{3,11},{4,36},{5,13},{6,38},{7,15},{8,40},{9,1... | collective-permute-start | bytes 3145736 | tf_op jit(solution)/shard_map/ppermute | solution.py:99
  52.7 1.0 fusion.1.order_ref
  53.7 0.6 fusion.11
  54.9 0.3 fusion
  55.3 0.1 collective-permute-start.2
  55.4 7.0 %all-to-all-start.1 = ((bf16[8,8,4096]{2,1,0:T(8,128)(2,1)}), bf16[8,8,4096]{2,1,0:T(8,128)(2,1)}, u32[]{:S(2)}, u32[]{:S(2)}) async-start(bf16[8,8,4096]{2,1,0:T(8,128)(2,1)} %get-tuple-element.24), calls=%async_computation.1 | async-start | bytes 1048576 | tf_op jit(solution)/shard_map/all_to_all | solution.py:520
  62.4 1.5 collective-permute-start.4
  63.9 1.2 collective-permute-start.6
  65.1 0.9 collective-permute-start.9
  65.9 0.0 collective-permute-done.8.refs_1_.refs_2_
  66.0 1.1 broadcast_select_fusion.1
  67.1 4.1 %collective-permute-start.12 = (bf16[128,4096]{1,0:T(8,128)(2,1)}, bf16[128,4096]{1,0:T(8,128)(2,1)S(1)}, u32[]{:S(2)}, u32[]{:S(2)}) collective-permute-start(bf16[128,4096]{1,0:T(8,128)(2,1)} %broadcast_select_fusion.1), channel_id=1, source_target_pairs={{0,2},{1,7},{2,0},{3,5},{4,6},{5,3},{6,4},{7,1},{8,10},{9,15},{10,... | collective-permute-start | bytes 3145736 | tf_op jit(solution)/shard_map/ppermute | solution.py:99
  71.2 34.0 %all-to-all-done.1 = bf16[8,8,4096]{2,1,0:T(8,128)(2,1)} async-done(((bf16[8,8,4096]{2,1,0:T(8,128)(2,1)}), bf16[8,8,4096]{2,1,0:T(8,128)(2,1)}, u32[]{:S(2)}, u32[]{:S(2)}) %all-to-all-start.1) | async-done | bytes 524320 | tf_op jit(solution)/shard_map/all_to_all | solution.py:520
  105.1 1.1 reduce_sum.61
  106.3 0.1 multiply_reduce_fusion
  106.4 3.4 %fusion.79 = f32[8,512]{1,0:T(8,128)S(1)} fusion(bf16[8,4096]{1,0:T(8,128)(2,1)S(1)} %reduce_sum.61, bf16[512,4096]{1,0:T(8,128)(2,1)} %bitcast.4.own_ref.refs_0_), kind=kOutput, calls=%fused_computation.203 | convolution fusion | flops 33554432 | bytes 4276224 | tf_op jit(solution)/shard_map/dot_general | solution.py:107
  109.8 0.0 collective-permute-done.9.refs_2_.refs_3_
  109.8 0.1 slice_subtract_fusion
  109.9 1.1 broadcast_select_fusion
  111.0 0.6 fusion.78
  111.6 0.8 collective-permute-start.14
  112.5 0.0 collective-permute-done.4.refs_4_
  112.5 5.2 %collective-permute-start.11 = (f32[8,512]{1,0:T(8,128)S(1)}, f32[8,512]{1,0:T(8,128)S(1)}, u32[]{:S(2)}, u32[]{:S(2)}) collective-permute-start(f32[8,512]{1,0:T(8,128)S(1)} %stack.23.refs_1_.refs_2_.refs_5_.refs_8_.refs_4_), channel_id=1, source_target_pairs={{0,34},{1,15},{2,0},{3,5},{4,38},{5,11},{6,4},{7,1},{8,42},{9,23},... | collective-permute-start | bytes 49160 | tf_op jit(solution)/shard_map/ppermute | solution.py:99
  117.7 2.4 %broadcast_select_fusion.3 = bf16[128,4096]{1,0:T(8,128)(2,1)} fusion(bf16[128,4096]{1,0:T(8,128)(2,1)} %collective-permute-done.4.refs_4_, bf16[128,4096]{1,0:T(8,128)(2,1)} %get-tuple-element.21, pred[]{:T(512)S(6)} %eq.162), kind=kLoop, calls=%fused_computation.8 | loop fusion | flops 524288 | bytes 3145729 | tf_op jit(solution)/shard_map/jit(_where)/select_n | solution.py:525
  120.1 0.0 collective-permute-done.6.refs_5_
  120.1 0.2 collective-permute-start.13
  120.3 2.3 %broadcast_select_fusion.2 = bf16[128,4096]{1,0:T(8,128)(2,1)} fusion(bf16[128,4096]{1,0:T(8,128)(2,1)} %collective-permute-done.6.refs_5_, bf16[128,4096]{1,0:T(8,128)(2,1)} %get-tuple-element.22, pred[]{:T(512)S(6)} %eq.162), kind=kLoop, calls=%fused_computation.7 | loop fusion | flops 524288 | bytes 3145729 | tf_op jit(solution)/shard_map/jit(_where)/select_n | solution.py:525
  122.7 5.0 %shard_map.69 = (f32[8,512]{1,0:T(8,128)S(1)}, f32[8,128]{1,0:T(8,128)S(1)}) custom-call(s32[1]{0:T(128)} %bitcast.2.side_ref_in, bf16[512,4096]{1,0:T(8,128)(2,1)} %bitcast.4.own_ref.refs_0_, f32[8,512]{1,0:T(8,128)S(1)} %stack.23.refs_1_.refs_2_.refs_5_.refs_8_.refs_4_, f32[8,512]{1,0:T(8,128)S(1)} %stack.23.refs_1_.refs_2_.refs_5_.refs_8_.refs_4_), custom_call_target="tpu_custom_call" | custom-call | flops 2147483648 | bytes 4194304 | tf_op jit(solution)/shard_map/pallas_call | solution.py:286
  127.7 0.6 stack_broadcast_in_dim.7
  128.4 0.1 stack.24.refs_17_
  128.5 0.0 collective-permute-done.14
  128.5 2.7 %collective-permute-start.5 = (bf16[128,4096]{1,0:T(8,128)(2,1)}, bf16[128,4096]{1,0:T(8,128)(2,1)S(1)}, u32[]{:S(2)}, u32[]{:S(2)}) collective-permute-start(bf16[128,4096]{1,0:T(8,128)(2,1)} %broadcast_select_fusion.3), channel_id=1, source_target_pairs={{0,2},{1,7},{2,0},{3,5},{4,6},{5,3},{6,4},{7,1},{8,10},{9,15},{10,... | collective-permute-start | bytes 3145736 | tf_op jit(solution)/shard_map/ppermute | solution.py:99
  131.3 0.2 collective-permute-start.7
  131.5 2.6 %collective-permute-start.10 = (f32[8,512]{1,0:T(8,128)S(1)}, f32[8,512]{1,0:T(8,128)S(1)}, u32[]{:S(2)}, u32[]{:S(2)}) collective-permute-start(f32[8,512]{1,0:T(8,128)S(1)} %stack.23.refs_1_.refs_2_.refs_5_.refs_8_.refs_4_), channel_id=1, source_target_pairs={{0,96},{1,25},{2,98},{3,27},{4,100},{5,29},{6,102},{7,31},{8,104},... | collective-permute-start | bytes 49160 | tf_op jit(solution)/shard_map/ppermute | solution.py:99
  134.0 1.2 collective-permute-done.13.refs_4_.refs_7_
  135.3 5.9 %shard_map.70 = (f32[8,512]{1,0:T(8,128)S(1)}, f32[3,512,128]{2,1,0:T(8,128)S(1)}, f32[8,128]{1,0:T(8,128)S(1)}) custom-call(s32[1]{0:T(128)} %bitcast.2.side_ref_in, bf16[512,4096]{1,0:T(8,128)(2,1)} %bitcast.4.own_ref.refs_0_, bf16[128,4096]{1,0:T(8,128)(2,1)S(1)} %collective-permute-done.8.refs_1_.refs_2_, ...), custom_call_target="tpu_custom_call" | custom-call | flops 2147483648 | bytes 8388608 | tf_op jit(solution)/shard_map/pallas_call | solution.py:286
  141.2 8.9 %shard_map.71 = (f32[8,512]{1,0:T(8,128)S(1)}, f32[8,256]{1,0:T(8,128)S(1)}, f32[3,512,128]{2,1,0:T(8,128)S(1)}, f32[3,512,128]{2,1,0:T(8,128)S(1)}, f32[8,128]{1,0:T(8,128)S(1)}) custom-call(s32[1]{0:T(128)} %bitcast.2.side_ref_in, bf16[512,4096]{1,0:T(8,128)(2,1)} %bitcast.4.own_ref.refs_0_, bf16[512,4096]{1,0:T(8,128)(2,1)} %collective-permute-done.2.refs_1_, ...), custom_call_target="tpu_custom_call" | custom-call | flops 4294967296 | bytes 14680064 | tf_op jit(solution)/shard_map/pallas_call | solution.py:286
  150.1 7.5 %collective-permute-done.7.refs_3_ = bf16[128,4096]{1,0:T(8,128)(2,1)S(1)} collective-permute-done((bf16[128,4096]{1,0:T(8,128)(2,1)}, bf16[128,4096]{1,0:T(8,128)(2,1)S(1)}, u32[]{:S(2)}, u32[]{:S(2)}) %collective-permute-start.7) | collective-permute-done | bytes 1048608 | tf_op jit(solution)/shard_map/ppermute | solution.py:99
  157.6 8.4 %shard_map.72 = f32[32,8,128]{2,1,0:T(8,128)} custom-call(s32[1]{0:T(128)} %bitcast.2.side_ref_in, bf16[512,4096]{1,0:T(8,128)(2,1)} %bitcast.4.own_ref.refs_0_, bf16[512,4096]{1,0:T(8,128)(2,1)} %collective-permute-done.2.refs_1_, bf16[128,4096]{1,0:T(8,128)(2,1)S(1)} %collective-permute-done.5.refs_2_, ...), custom_call_target="tpu_custom_call" | custom-call | flops 2147483648 | bytes 10485760 | tf_op jit(solution)/shard_map/pallas_call | solution.py:350
  166.0 8.2 %all-to-all-start.2 = ((f32[32,8,128]{2,1,0:T(8,128)}), f32[32,8,128]{2,1,0:T(8,128)S(1)}, u32[]{:S(2)}, u32[]{:S(2)}) async-start(f32[32,8,128]{2,1,0:T(8,128)} %shard_map.72), calls=%async_computation.2 | async-start | bytes 262144 | tf_op jit(solution)/shard_map/all_to_all | solution.py:582
  174.2 0.1 fusion.5
  174.3 0.7 reduce_sum.65
  175.7 0.7 reshape.784.keep_ref
  176.4 0.6 pad_add_fusion.1.where_ref
  177.0 5.8 %all-to-all-done.2.in_ref = f32[32,8,128]{2,1,0:T(8,128)S(1)} async-done(((f32[32,8,128]{2,1,0:T(8,128)}), f32[32,8,128]{2,1,0:T(8,128)S(1)}, u32[]{:S(2)}, u32[]{:S(2)}) %all-to-all-start.2) | async-done | bytes 131104 | tf_op jit(solution)/shard_map/all_to_all | solution.py:582
  182.8 0.6 broadcast_in_dim.51.total_ref
  183.4 0.0 copy-done
  183.4 2.0 %shard_map.73 = (f32[3,1,512]{2,1,0:T(1,128)}, f32[1,512]{1,0:T(1,128)}) custom-call(s32[2]{0:T(128)} %pad_add_fusion.1.where_ref, f32[32,8,128]{2,1,0:T(8,128)} %copy-done, bf16[512,512]{1,0:T(8,128)(2,1)} %fusion.1.order_ref, f32[1,512]{1,0:T(1,128)} %reshape.784.keep_ref, f32[1,128]{1,0:T(1,128)} %broadcast_in_dim.51.total_ref), custom_call_target="tpu_custom_call" | custom-call | tf_op jit(solution)/shard_map/pallas_call | solution.py:599
  (24 shorter events, 0.2 us)
Async XLA Ops:
  0.6 5.5 %collective-permute-start.1 = (bf16[256,4096]{1,0:T(8,128)(2,1)}, bf16[256,4096]{1,0:T(8,128)(2,1)S(1)}, u32[]{:S(2)}, u32[]{:S(2)}) collective-permute-start(bf16[256,4096]{1,0:T(8,128)(2,1)} %param.5), channel_id=1, source_target_pairs={{0,1},{1,0},{2,3},{3,2},{4,5},{5,4},{6,7},{7,6},{8,9},{9,8},{10,11... | collective-permute-start | bytes 6291464 | tf_op jit(solution)/shard_map/ppermute | solution.py:99
  2.8 3.3 %collective-permute-start = (s32[256]{0:T(256)S(1)}, s32[256]{0:T(256)S(1)}, u32[]{:S(2)}, u32[]{:S(2)}) collective-permute-start(s32[256]{0:T(256)S(1)} %get-tuple-element.44), channel_id=1, source_target_pairs={{0,1},{1,0},{2,3},{3,2},{4,5},{5,4},{6,7},{7,6},{8,9},{9,8},{10,11... | collective-permute-start | bytes 3080 | tf_op jit(solution)/shard_map/ppermute | solution.py:99
  9.4 6.0 %copy-start.2 = (s32[3,1]{0,1:T(1,128)S(1)}, s32[3,1]{0,1:T(1,128)}, u32[]{:S(2)}) copy-start(s32[3,1]{0,1:T(1,128)} %param.9) | copy-start | bytes 40
  9.4 6.1 %copy-start.1 = (s32[1,8,128]{2,1,0:T(8,128)S(1)}, s32[1,8,128]{2,1,0:T(8,128)}, u32[]{:S(2)}) copy-start(s32[1,8,128]{2,1,0:T(8,128)} %param.8) | copy-start | bytes 12292
  9.4 32.4 %all-to-all-start = ((bf16[8,64,4096]{2,1,0:T(8,128)(2,1)}), bf16[8,64,4096]{2,1,0:T(8,128)(2,1)}, u32[]{:S(2)}, u32[]{:S(2)}) async-start(bf16[8,64,4096]{2,1,0:T(8,128)(2,1)} %bitcast.15), calls=%async_computation | async-start | bytes 8388608 | tf_op jit(solution)/shard_map/all_to_all | solution.py:500
  15.6 0.8 collective-permute-start.3
  46.1 19.9 %collective-permute-start.8 = (bf16[128,4096]{1,0:T(8,128)(2,1)S(1)}, bf16[128,4096]{1,0:T(8,128)(2,1)S(1)}, u32[]{:S(2)}, u32[]{:S(2)}) collective-permute-start(bf16[128,4096]{1,0:T(8,128)(2,1)S(1)} %get-tuple-element.25), channel_id=1, source_target_pairs={{0,32},{1,9},{2,34},{3,11},{4,36},{5,13},{6,38},{7,15},{8,40},{9,1... | collective-permute-start | bytes 3145736 | tf_op jit(solution)/shard_map/ppermute | solution.py:99
  55.3 85.9 %collective-permute-start.2 = (bf16[512,4096]{1,0:T(8,128)(2,1)}, bf16[512,4096]{1,0:T(8,128)(2,1)}, u32[]{:S(2)}, u32[]{:S(2)}) collective-permute-start(bf16[512,4096]{1,0:T(8,128)(2,1)} %bitcast.4.own_ref.refs_0_), channel_id=1, source_target_pairs={{0,96},{1,25},{2,98},{3,27},{4,100},{5,29},{6,102},{7,31},{8,104},... | collective-permute-start | bytes 12582920 | tf_op jit(solution)/shard_map/ppermute | solution.py:99
  55.4 49.8 %all-to-all-start.1 = ((bf16[8,8,4096]{2,1,0:T(8,128)(2,1)}), bf16[8,8,4096]{2,1,0:T(8,128)(2,1)}, u32[]{:S(2)}, u32[]{:S(2)}) async-start(bf16[8,8,4096]{2,1,0:T(8,128)(2,1)} %get-tuple-element.24), calls=%async_computation.1 | async-start | bytes 1048576 | tf_op jit(solution)/shard_map/all_to_all | solution.py:520
  62.4 50.1 %collective-permute-start.4 = (bf16[128,4096]{1,0:T(8,128)(2,1)}, bf16[128,4096]{1,0:T(8,128)(2,1)}, u32[]{:S(2)}, u32[]{:S(2)}) collective-permute-start(bf16[128,4096]{1,0:T(8,128)(2,1)} %get-tuple-element.21), channel_id=1, source_target_pairs={{0,32},{1,9},{2,34},{3,11},{4,36},{5,13},{6,38},{7,15},{8,40},{9,1... | collective-permute-start | bytes 3145736 | tf_op jit(solution)/shard_map/ppermute | solution.py:99
  63.9 56.2 %collective-permute-start.6 = (bf16[128,4096]{1,0:T(8,128)(2,1)}, bf16[128,4096]{1,0:T(8,128)(2,1)}, u32[]{:S(2)}, u32[]{:S(2)}) collective-permute-start(bf16[128,4096]{1,0:T(8,128)(2,1)} %get-tuple-element.22), channel_id=1, source_target_pairs={{0,32},{1,9},{2,34},{3,11},{4,36},{5,13},{6,38},{7,15},{8,40},{9,1... | collective-permute-start | bytes 3145736 | tf_op jit(solution)/shard_map/ppermute | solution.py:99
  65.1 44.7 %collective-permute-start.9 = (bf16[128,4096]{1,0:T(8,128)(2,1)}, bf16[128,4096]{1,0:T(8,128)(2,1)S(1)}, u32[]{:S(2)}, u32[]{:S(2)}) collective-permute-start(bf16[128,4096]{1,0:T(8,128)(2,1)} %get-tuple-element.27), channel_id=1, source_target_pairs={{0,32},{1,9},{2,34},{3,11},{4,36},{5,13},{6,38},{7,15},{8,40},{9,1... | collective-permute-start | bytes 3145736 | tf_op jit(solution)/shard_map/ppermute | solution.py:99
  67.1 64.4 %collective-permute-start.12 = (bf16[128,4096]{1,0:T(8,128)(2,1)}, bf16[128,4096]{1,0:T(8,128)(2,1)S(1)}, u32[]{:S(2)}, u32[]{:S(2)}) collective-permute-start(bf16[128,4096]{1,0:T(8,128)(2,1)} %broadcast_select_fusion.1), channel_id=1, source_target_pairs={{0,2},{1,7},{2,0},{3,5},{4,6},{5,3},{6,4},{7,1},{8,10},{9,15},{10,... | collective-permute-start | bytes 3145736 | tf_op jit(solution)/shard_map/ppermute | solution.py:99
  111.6 16.9 %collective-permute-start.14 = (f32[8,512]{1,0:T(8,128)S(1)}, f32[8,512]{1,0:T(8,128)S(1)}, u32[]{:S(2)}, u32[]{:S(2)}) collective-permute-start(f32[8,512]{1,0:T(8,128)S(1)} %stack.23.refs_1_.refs_2_.refs_5_.refs_8_.refs_4_), channel_id=1, source_target_pairs={{0,32},{1,9},{2,34},{3,11},{4,36},{5,13},{6,38},{7,15},{8,40},{9,1... | collective-permute-start | bytes 49160 | tf_op jit(solution)/shard_map/ppermute | solution.py:99
  112.5 18.8 %collective-permute-start.11 = (f32[8,512]{1,0:T(8,128)S(1)}, f32[8,512]{1,0:T(8,128)S(1)}, u32[]{:S(2)}, u32[]{:S(2)}) collective-permute-start(f32[8,512]{1,0:T(8,128)S(1)} %stack.23.refs_1_.refs_2_.refs_5_.refs_8_.refs_4_), channel_id=1, source_target_pairs={{0,34},{1,15},{2,0},{3,5},{4,38},{5,11},{6,4},{7,1},{8,42},{9,23},... | collective-permute-start | bytes 49160 | tf_op jit(solution)/shard_map/ppermute | solution.py:99
  120.1 15.2 %collective-permute-start.13 = (bf16[128,4096]{1,0:T(8,128)(2,1)}, bf16[128,4096]{1,0:T(8,128)(2,1)}, u32[]{:S(2)}, u32[]{:S(2)}) collective-permute-start(bf16[128,4096]{1,0:T(8,128)(2,1)} %broadcast_select_fusion), channel_id=1, source_target_pairs={{0,2},{1,7},{2,0},{3,5},{4,6},{5,3},{6,4},{7,1},{8,10},{9,15},{10,... | collective-permute-start | bytes 3145736 | tf_op jit(solution)/shard_map/ppermute | solution.py:99
  128.5 21.6 %collective-permute-start.5 = (bf16[128,4096]{1,0:T(8,128)(2,1)}, bf16[128,4096]{1,0:T(8,128)(2,1)S(1)}, u32[]{:S(2)}, u32[]{:S(2)}) collective-permute-start(bf16[128,4096]{1,0:T(8,128)(2,1)} %broadcast_select_fusion.3), channel_id=1, source_target_pairs={{0,2},{1,7},{2,0},{3,5},{4,6},{5,3},{6,4},{7,1},{8,10},{9,15},{10,... | collective-permute-start | bytes 3145736 | tf_op jit(solution)/shard_map/ppermute | solution.py:99
  131.3 26.4 %collective-permute-start.7 = (bf16[128,4096]{1,0:T(8,128)(2,1)}, bf16[128,4096]{1,0:T(8,128)(2,1)S(1)}, u32[]{:S(2)}, u32[]{:S(2)}) collective-permute-start(bf16[128,4096]{1,0:T(8,128)(2,1)} %broadcast_select_fusion.2), channel_id=1, source_target_pairs={{0,2},{1,7},{2,0},{3,5},{4,6},{5,3},{6,4},{7,1},{8,10},{9,15},{10,... | collective-permute-start | bytes 3145736 | tf_op jit(solution)/shard_map/ppermute | solution.py:99
  131.5 9.6 %collective-permute-start.10 = (f32[8,512]{1,0:T(8,128)S(1)}, f32[8,512]{1,0:T(8,128)S(1)}, u32[]{:S(2)}, u32[]{:S(2)}) collective-permute-start(f32[8,512]{1,0:T(8,128)S(1)} %stack.23.refs_1_.refs_2_.refs_5_.refs_8_.refs_4_), channel_id=1, source_target_pairs={{0,96},{1,25},{2,98},{3,27},{4,100},{5,29},{6,102},{7,31},{8,104},... | collective-permute-start | bytes 49160 | tf_op jit(solution)/shard_map/ppermute | solution.py:99
  166.0 16.7 %all-to-all-start.2 = ((f32[32,8,128]{2,1,0:T(8,128)}), f32[32,8,128]{2,1,0:T(8,128)S(1)}, u32[]{:S(2)}, u32[]{:S(2)}) async-start(f32[32,8,128]{2,1,0:T(8,128)} %shard_map.72), calls=%async_computation.2 | async-start | bytes 262144 | tf_op jit(solution)/shard_map/all_to_all | solution.py:582
  182.8 0.7 copy-start
